TPU v7x, 768 devices: a whole 4x8x12 slice. The times are simulated.
768 devices in a mesh: dp: 12 (over z_lo, x), spatial: 64 (over y, z_hi, core).
Axes of the slice: x: 4, y: 8, z: 12 (z_hi: 4, z_lo: 3; z = z_hi * 3 + z_lo), core: 2. Of those that a mesh axis runs over, the one named last changes fastest.
Arguments:
- volume: bfloat16 [12, 128, 16, 8, 128], P('dp', 'spatial'), may hold values from -16 to 16
- cotangent: bfloat16 [12, 128, 16, 8, 128], P('dp', 'spatial'), may hold values from -6 to 6
- master: float32 [3456, 128], P('dp'), may hold values from -0.109375 to 0.109375
- moment: float32 [3456, 128], P('dp'), may hold values from -6 to 6
- second: float32 [3456, 128], P('dp'), may hold values from 0.25 to 4
Outputs:
- activation: bfloat16 [12, 128, 16, 8, 128], P('dp', 'spatial')
- input_grad: bfloat16 [12, 128, 16, 8, 128], P('dp', 'spatial')
- master_next: float32 [3456, 128], P('dp')
- moment_next: float32 [3456, 128], P('dp')
- second_next: float32 [3456, 128], P('dp')
All inputs are finite; a program needn't handle non-finite values.
Results may differ from a plain program's by a relative error of at most 0.002.
The roundings to bfloat16 on the way count: a program that leaves them out, or rounds other values in their place, can miss the bound.
Values may be sent and summed in bfloat16 or wider, within the bound.
No kernel may reach another device: no remote copies, remote signals or barrier semaphores. Data moves between devices by JAX's collectives and lax.ppermute only.
A program may use at most 64 MiB of HBM per device.

v0:
```python
import math

import jax
import jax.numpy as jnp
from jax import lax
from jax.sharding import PartitionSpec as P


def copy_for_each(value, axis):
    count = lax.axis_size(axis)
    return lax.all_to_all(
        jnp.broadcast_to(value[None], (count, *value.shape)), axis, 0, 0, tiled=True
    )


def joined_along(tiles, dim):
    tiles = jnp.moveaxis(tiles, 0, dim)
    dims = tiles.shape
    return tiles.reshape(*dims[:dim], dims[dim] * dims[dim + 1], *dims[dim + 2 :])


def gather_directly(value, axis, dim):
    tiles = copy_for_each(value, axis)
    return joined_along(tiles, dim)


def with_halo(block, sides, width):
    for axis, dim in sides:
        count = lax.axis_size(axis)
        forward = [(i, i + 1) for i in range(count - 1)]
        backward = [(target, source) for source, target in forward]
        low = lax.ppermute(
            lax.slice_in_dim(block, block.shape[dim] - width, None, axis=dim), axis, forward
        )
        high = lax.ppermute(lax.slice_in_dim(block, 0, width, axis=dim), axis, backward)
        block = jnp.concatenate([low, block, high], axis=dim)
    return block


def in_blocks(value, dim, count):
    before, after = (value.shape[:dim], value.shape[dim + 1 :])
    return jnp.moveaxis(value.reshape(*before, count, -1, *after), dim, 0)


def sum_at_owner(value, axis, dim):
    tiles = in_blocks(value, dim, lax.axis_size(axis))
    arrived = lax.all_to_all(tiles, axis, split_axis=0, concat_axis=0, tiled=True)
    return arrived.astype(jnp.float32).sum(axis=0)


def total_of_pieces(value, axis):
    return lax.all_gather(value, axis).sum(0)


def silu_slope(preact):
    sigma = jax.nn.sigmoid(preact)
    return sigma * (1.0 + preact * (1.0 - sigma))


def pad_sides(field):
    return jnp.pad(field, ((0, 0), (1, 1), (1, 1), (0, 0)))


def forward_taps(padded, kernel, planes, rows, cols):
    width = kernel.shape[1]
    total = jnp.zeros((planes * rows * cols, width), jnp.float32)
    for offset_z in range(3):
        for offset_y in range(3):
            for offset_x in range(3):
                tap_index = offset_z * 9 + offset_y * 3 + offset_x
                piece = padded[
                    offset_z : offset_z + planes,
                    offset_y : offset_y + rows,
                    offset_x : offset_x + cols,
                ].reshape(-1, width)
                total = total + jnp.dot(
                    piece, kernel[tap_index], preferred_element_type=jnp.float32
                )
    return total


def backward_taps(grad_pad, kernel, planes, rows, cols):
    width = kernel.shape[1]
    total = jnp.zeros((planes * rows * cols, width), jnp.float32)
    for offset_z in range(3):
        for offset_y in range(3):
            for offset_x in range(3):
                tap_index = offset_z * 9 + offset_y * 3 + offset_x
                piece = grad_pad[
                    2 - offset_z : 2 - offset_z + planes,
                    2 - offset_y : 2 - offset_y + rows,
                    2 - offset_x : 2 - offset_x + cols,
                ].reshape(-1, width)
                total = total + lax.dot_general(
                    piece,
                    kernel[tap_index],
                    (((1,), (1,)), ((), ())),
                    preferred_element_type=jnp.float32,
                )
    return total


def weight_taps(padded, hidden_grad, planes, rows, cols):
    width = hidden_grad.shape[1]
    blocks = []
    for offset_z in range(3):
        for offset_y in range(3):
            for offset_x in range(3):
                piece = padded[
                    offset_z : offset_z + planes,
                    offset_y : offset_y + rows,
                    offset_x : offset_x + cols,
                ].reshape(-1, width)
                blocks.append(
                    lax.dot_general(
                        piece,
                        hidden_grad,
                        (((0,), (0,)), ((), ())),
                        preferred_element_type=jnp.float32,
                    )
                )
    return jnp.concatenate(blocks, axis=0)


def per_device(volume, cotangent, master, moment, second):
    planes = volume.shape[1]
    rows = volume.shape[2]
    cols = volume.shape[3]
    width = volume.shape[4]
    kernel = gather_directly(master.astype(jnp.bfloat16), "dp", 0).reshape(27, width, width)
    wide = with_halo(volume, (("spatial", 1),), 1)[0]
    padded = pad_sides(wide)
    preact = forward_taps(padded, kernel, planes, rows, cols)
    activated = jax.nn.silu(preact).astype(jnp.bfloat16)
    hidden_grad = (cotangent[0].reshape(-1, width).astype(jnp.float32) * silu_slope(preact)).astype(
        jnp.bfloat16
    )
    grad_block = hidden_grad.reshape(1, planes, rows, cols, width)
    wide_grad = with_halo(grad_block, (("spatial", 1),), 1)[0]
    grad_pad = pad_sides(wide_grad)
    input_grad = backward_taps(grad_pad, kernel, planes, rows, cols).astype(jnp.bfloat16)
    local_grad = weight_taps(padded, hidden_grad, planes, rows, cols)
    partial_grad = sum_at_owner(local_grad.astype(jnp.bfloat16), "dp", 0)
    shard = total_of_pieces(partial_grad, "spatial")
    cells_all = lax.axis_size("dp") * lax.axis_size("spatial") * planes * rows * cols
    weight_grad = shard / math.sqrt(cells_all)
    moment_next = 0.9 * moment + 0.1 * weight_grad
    second_next = 0.999 * second + 0.001 * weight_grad * weight_grad
    master_next = master - 0.001 * (moment_next / (jnp.sqrt(second_next) + 1e-08) + 0.01 * master)
    activation = activated.reshape(1, planes, rows, cols, width)
    input_block = input_grad.reshape(1, planes, rows, cols, width)
    return (activation, input_block, master_next, moment_next, second_next)


def solution(mesh):
    return jax.shard_map(
        per_device,
        mesh=mesh,
        in_specs=(
            P("dp", "spatial", None, None, None),
            P("dp", "spatial", None, None, None),
            P("dp", None),
            P("dp", None),
            P("dp", None),
        ),
        out_specs=(
            P("dp", "spatial", None, None, None),
            P("dp", "spatial", None, None, None),
            P("dp", None),
            P("dp", None),
            P("dp", None),
        ),
        check_vma=False,
    )
```

profile of v0, /device:TPU:67, one launch (start us, length us, event | category | flops | bytes accessed | tf_op | source)
XLA Modules:
  0.0 223.3 jit_solution(6352765980049104075)
XLA Ops:
  7.2 1.0 convert_element_type.29
  8.1 1.0 broadcast_in_dim.2
  9.2 7.0 %all-to-all-start = ((bf16[12,288,128]{2,1,0:T(8,128)(2,1)}), bf16[12,288,128]{2,1,0:T(8,128)(2,1)S(1)}, u32[]{:S(2)}, u32[]{:S(2)}) async-start(bf16[12,288,128]{2,1,0:T(8,128)(2,1)} %broadcast_in_dim.2), calls=%async_computation | async-start | bytes 1769472 | tf_op jit(solution)/shard_map/all_to_all | solution.py:11
  16.2 0.8 fusion.41
  16.9 7.8 %collective-permute-start.1 = (bf16[1,1,16,8,128]{4,3,2,1,0:T(8,128)(2,1)S(1)}, bf16[1,1,16,8,128]{4,3,2,1,0:T(8,128)(2,1)S(1)}, u32[]{:S(2)}, u32[]{:S(2)}) collective-permute-start(bf16[1,1,16,8,128]{4,3,2,1,0:T(8,128)(2,1)S(1)} %get-tuple-element.65), channel_id=1, source_target_pairs={{1,0},{2,1},{3,2},{4,3},{5,4},{6,5},{7,6},{8,7},{9,8},{10,9},{11,1... | collective-permute-start | bytes 98312 | tf_op jit(solution)/shard_map/ppermute | solution.py:35
  24.7 5.3 %collective-permute-start = (bf16[1,1,16,8,128]{4,3,2,1,0:T(8,128)(2,1)S(1)}, bf16[1,1,16,8,128]{4,3,2,1,0:T(8,128)(2,1)S(1)}, u32[]{:S(2)}, u32[]{:S(2)}) collective-permute-start(bf16[1,1,16,8,128]{4,3,2,1,0:T(8,128)(2,1)S(1)} %get-tuple-element.64), channel_id=1, source_target_pairs={{0,1},{1,2},{2,3},{3,4},{4,5},{5,6},{6,7},{7,8},{8,9},{9,10},{10,1... | collective-permute-start | bytes 98312 | tf_op jit(solution)/shard_map/ppermute | solution.py:32
  30.0 3.3 %collective-permute-done.1 = bf16[1,1,16,8,128]{4,3,2,1,0:T(8,128)(2,1)S(1)} collective-permute-done((bf16[1,1,16,8,128]{4,3,2,1,0:T(8,128)(2,1)S(1)}, bf16[1,1,16,8,128]{4,3,2,1,0:T(8,128)(2,1)S(1)}, u32[]{:S(2)}, u32[]{:S(2)}) %collective-permute-start.1) | collective-permute-done | bytes 32800 | tf_op jit(solution)/shard_map/ppermute | solution.py:35
  33.3 0.9 maximum_bitcast_fusion
  34.2 0.8 pad_maximum_fusion.2
  39.2 0.8 fusion.33
  40.3 0.2 fusion.29
  41.7 0.2 fusion.22
  41.9 0.2 fusion.21
  42.8 0.2 fusion.32
  45.6 0.2 fusion.5
  45.8 21.9 %all_to_all.10 = bf16[12,288,128]{2,1,0:T(8,128)(2,1)S(1)} all-to-all(bf16[12,288,128]{2,1,0:T(8,128)(2,1)S(1)} %bitcast.348), channel_id=1, replica_groups=mesh['dp'=12,'spatial'=64] {'dp'}, dimensions={0} | all-to-all | bytes 1769472 | tf_op jit(solution)/shard_map/all_to_all | solution.py:47
  67.7 0.8 convert_reduce_fusion
  68.5 1.9 collective-permute-start.3
  70.4 7.3 %collective-permute-start.2 = (bf16[1,1,16,8,128]{4,3,2,1,0:T(8,128)(2,1)S(1)}, bf16[1,1,16,8,128]{4,3,2,1,0:T(8,128)(2,1)S(1)}, u32[]{:S(2)}, u32[]{:S(2)}) collective-permute-start(bf16[1,1,16,8,128]{4,3,2,1,0:T(8,128)(2,1)S(1)} %get-tuple-element.60), channel_id=1, source_target_pairs={{0,1},{1,2},{2,3},{3,4},{4,5},{5,6},{6,7},{7,8},{8,9},{9,10},{10,1... | collective-permute-start | bytes 98312 | tf_op jit(solution)/shard_map/ppermute | solution.py:32
  77.8 1.1 collective-permute-done.2
  83.6 0.8 fusion.4
  84.4 127.1 %all-gather.3.cloned.1.call-done = f32[18432,128]{1,0:T(8,128)} async-done(((f32[288,128]{1,0:T(8,128)}), f32[18432,128]{1,0:T(8,128)}) %all-gather.3.cloned.1.call-update) | async-done | bytes 9437200 | tf_op jit(solution)/shard_map/all_gather | solution.py:52
  211.5 4.1 %reduce_sum.19 = f32[288,128]{1,0:T(8,128)S(1)} reduce(f32[64,288,128]{2,1,0:T(8,128)} %bitcast.291, f32[]{:T(128)} %constant.8.clone.1), dimensions={0}, to_apply=%region_1.2 | reduce | flops 2322432 | bytes 9584644 | tf_op jit(solution)/shard_map/reduce_sum | solution.py:52
  215.7 0.8 multiply_subtract_fusion
  (96 shorter events, 13.2 us)
Async XLA Ops:
  7.2 30.2 %copy-start = (bf16[1,2,16,8,128]{4,3,2,1,0:T(8,128)(2,1)S(1)}, bf16[1,2,16,8,128]{4,3,2,1,0:T(8,128)(2,1)}, u32[]{:S(2)}) copy-start(bf16[1,2,16,8,128]{4,3,2,1,0:T(8,128)(2,1)} %param.5) | copy-start | bytes 196612
  7.2 32.0 %copy-start.4 = (bf16[1,2,16,8,128]{4,3,2,1,0:T(8,128)(2,1)S(1)}, bf16[1,2,16,8,128]{4,3,2,1,0:T(8,128)(2,1)}, u32[]{:S(2)}) copy-start(bf16[1,2,16,8,128]{4,3,2,1,0:T(8,128)(2,1)} %param.6) | copy-start | bytes 196612
  9.2 26.1 %all-to-all-start = ((bf16[12,288,128]{2,1,0:T(8,128)(2,1)}), bf16[12,288,128]{2,1,0:T(8,128)(2,1)S(1)}, u32[]{:S(2)}, u32[]{:S(2)}) async-start(bf16[12,288,128]{2,1,0:T(8,128)(2,1)} %broadcast_in_dim.2), calls=%async_computation | async-start | bytes 1769472 | tf_op jit(solution)/shard_map/all_to_all | solution.py:11
  16.2 195.3 %all-gather.3.cloned.1.call-start = ((), (), s32[]{:S(2)}) async-start(), calls=%async_computation.2 | async-start | bytes 9584640 | tf_op jit(solution)/shard_map/all_gather | solution.py:52
  16.9 16.4 %collective-permute-start.1 = (bf16[1,1,16,8,128]{4,3,2,1,0:T(8,128)(2,1)S(1)}, bf16[1,1,16,8,128]{4,3,2,1,0:T(8,128)(2,1)S(1)}, u32[]{:S(2)}, u32[]{:S(2)}) collective-permute-start(bf16[1,1,16,8,128]{4,3,2,1,0:T(8,128)(2,1)S(1)} %get-tuple-element.65), channel_id=1, source_target_pairs={{1,0},{2,1},{3,2},{4,3},{5,4},{6,5},{7,6},{8,7},{9,8},{10,9},{11,1... | collective-permute-start | bytes 98312 | tf_op jit(solution)/shard_map/ppermute | solution.py:35
  24.7 8.6 %collective-permute-start = (bf16[1,1,16,8,128]{4,3,2,1,0:T(8,128)(2,1)S(1)}, bf16[1,1,16,8,128]{4,3,2,1,0:T(8,128)(2,1)S(1)}, u32[]{:S(2)}, u32[]{:S(2)}) collective-permute-start(bf16[1,1,16,8,128]{4,3,2,1,0:T(8,128)(2,1)S(1)} %get-tuple-element.64), channel_id=1, source_target_pairs={{0,1},{1,2},{2,3},{3,4},{4,5},{5,6},{6,7},{7,8},{8,9},{9,10},{10,1... | collective-permute-start | bytes 98312 | tf_op jit(solution)/shard_map/ppermute | solution.py:32
  68.5 9.3 %collective-permute-start.3 = (bf16[1,1,16,8,128]{4,3,2,1,0:T(8,128)(2,1)S(1)}, bf16[1,1,16,8,128]{4,3,2,1,0:T(8,128)(2,1)S(1)}, u32[]{:S(2)}, u32[]{:S(2)}) collective-permute-start(bf16[1,1,16,8,128]{4,3,2,1,0:T(8,128)(2,1)S(1)} %get-tuple-element.61), channel_id=1, source_target_pairs={{1,0},{2,1},{3,2},{4,3},{5,4},{6,5},{7,6},{8,7},{9,8},{10,9},{11,1... | collective-permute-start | bytes 98312 | tf_op jit(solution)/shard_map/ppermute | solution.py:35
  70.4 8.5 %collective-permute-start.2 = (bf16[1,1,16,8,128]{4,3,2,1,0:T(8,128)(2,1)S(1)}, bf16[1,1,16,8,128]{4,3,2,1,0:T(8,128)(2,1)S(1)}, u32[]{:S(2)}, u32[]{:S(2)}) collective-permute-start(bf16[1,1,16,8,128]{4,3,2,1,0:T(8,128)(2,1)S(1)} %get-tuple-element.60), channel_id=1, source_target_pairs={{0,1},{1,2},{2,3},{3,4},{4,5},{5,6},{6,7},{7,8},{8,9},{9,10},{10,1... | collective-permute-start | bytes 98312 | tf_op jit(solution)/shard_map/ppermute | solution.py:32
  79.4 136.3 %copy-start.1 = (f32[288,128]{1,0:T(8,128)S(1)}, f32[288,128]{1,0:T(8,128)}, u32[]{:S(2)}) copy-start(f32[288,128]{1,0:T(8,128)} %param.7) | copy-start | bytes 442372
  79.4 136.3 %copy-start.2 = (f32[288,128]{1,0:T(8,128)S(1)}, f32[288,128]{1,0:T(8,128)}, u32[]{:S(2)}) copy-start(f32[288,128]{1,0:T(8,128)} %param.9) | copy-start | bytes 442372
  79.4 136.3 %copy-start.3 = (f32[288,128]{1,0:T(8,128)S(1)}, f32[288,128]{1,0:T(8,128)}, u32[]{:S(2)}) copy-start(f32[288,128]{1,0:T(8,128)} %param.8) | copy-start | bytes 442372
Sparse Core Ops, SparseCore 0:
  68.6 142.8 all-gather.2
where the time goes:
time: 224 us; the launch traced here: 223 us
  waiting for transfers between devices  132 us (59%)
  starting transfers between devices  29.3 us (13%)
  blocking collectives  21.9 us (10%)
  matrix products  15.2 us (7%)
  between operations  14.6 us (7%)
  other arithmetic  8.36 us (4%)
  local copies, waits for them, and re-layouts  2.37 us (1%)
    all_gather x1, waiting for transfers between devices, total_of_pieces(): return lax.all_gather(value, axis).sum(0)  127 us
    all_to_all x1, blocking collectives, sum_at_owner(): lax.all_to_all(tiles, axis, split_axis=0, concat_axis=0, tiled=True)  21.9 us
    ppermute x2, starting transfers between devices, with_halo(): lax.ppermute(lax.slice_in_dim(block, block.shape[dim] - width, None, axis...  12.6 us
    ppermute x2, starting transfers between devices, with_halo(): lax.ppermute(lax.slice_in_dim(block, 0, width, axis=dim), axis, backward)  9.68 us
    all_to_all x1, starting transfers between devices, copy_for_each(): lax.all_to_all(jnp.broadcast_to(value[None], (count, *value.shape)), axis...  6.99 us
    dot_general x27, matrix products, weight_taps(): lax.dot_general(piece, hidden_grad, (((0,), (0,)), ((), ())), preferred_e...  5.55 us
    dot_general x27, matrix products, backward_taps(): lax.dot_general(piece, kernel[tap_index], (((1,), (1,)), ((), ())), prefe...  5.04 us
    dot_general x27, matrix products, forward_taps(): jnp.dot(piece, kernel[tap_index], preferred_element_type=jnp.float32)  4.65 us
  transfers between devices with their start and end apart: 6, of which 3 were waited for; matrix products, arithmetic and copies ran while one was open for 4% of the time, Pallas kernels for 0%

commit v1 on v0

--- a/solution.py
+++ b/solution.py
@@ -48,8 +48,21 @@
     return arrived.astype(jnp.float32).sum(axis=0)
 
 
+def exchanged(tiles, axis, groups):
+    return lax.all_to_all(tiles, axis, 0, 0, tiled=True, axis_index_groups=groups)
+
+
 def total_of_pieces(value, axis):
-    return lax.all_gather(value, axis).sum(0)
+    count = lax.axis_size(axis)
+    inner = 8
+    outer = count // inner
+    same_inner = [[o * inner + i for o in range(outer)] for i in range(inner)]
+    same_outer = [[o * inner + i for i in range(inner)] for o in range(outer)]
+    pieces = value.reshape(outer, -1, value.shape[-1])
+    piece = exchanged(pieces, axis, same_inner).sum(0)
+    piece = exchanged(jnp.broadcast_to(piece[None], (inner, *piece.shape)), axis, same_outer).sum(0)
+    whole = exchanged(jnp.broadcast_to(piece[None], (outer, *piece.shape)), axis, same_inner)
+    return whole.reshape(value.shape)
 
 
 def silu_slope(preact):

time: 224 us -> 144 us (0.64)
  the two profiles are of different devices: /device:TPU:67 before, /device:TPU:64 now
where the time goes in v1:
time: 144 us; the launch traced here: 143 us
  waiting for transfers between devices  54.3 us (38%)
  starting transfers between devices  50.5 us (35%)
  matrix products  31.4 us (22%)
  local copies, waits for them, and re-layouts  3.85 us (3%)
  other arithmetic  1.97 us (1%)
    all_to_all x3, waiting for transfers between devices, exchanged(): lax.all_to_all(tiles, axis, 0, 0, tiled=True, axis_index_groups=groups)  30.8 us
    dot_general x27, matrix products, weight_taps(): lax.dot_general(piece, hidden_grad, (((0,), (0,)), ((), ())), preferred_e...  21.7 us
    all_to_all x3, starting transfers between devices, exchanged(): lax.all_to_all(tiles, axis, 0, 0, tiled=True, axis_index_groups=groups)  20.2 us
    all_to_all x1, waiting for transfers between devices, sum_at_owner(): lax.all_to_all(tiles, axis, split_axis=0, concat_axis=0, tiled=True)  14.2 us
    all_to_all x1, starting transfers between devices, copy_for_each(): lax.all_to_all(jnp.broadcast_to(value[None], (count, *value.shape)), axis...  12.3 us
    all_to_all x1, starting transfers between devices, sum_at_owner(): lax.all_to_all(tiles, axis, split_axis=0, concat_axis=0, tiled=True)  8.21 us
    ppermute x2, starting transfers between devices, with_halo(): lax.ppermute(lax.slice_in_dim(block, block.shape[dim] - width, None, axis...  7.13 us
    ppermute x2, waiting for transfers between devices, with_halo(): lax.ppermute(lax.slice_in_dim(block, 0, width, axis=dim), axis, backward)  5.81 us
  transfers between devices with their start and end apart: 9, of which 6 were waited for; matrix products, arithmetic and copies ran while one was open for 5% of the time, Pallas kernels for 0%

profile of v1, /device:TPU:64, one launch (start us, length us, event | category | flops | bytes accessed | tf_op | source)
XLA Modules:
  0.0 143.1 jit_solution(6856673817046531478)
XLA Ops:
  0.6 0.9 convert_element_type.29
  1.6 1.0 broadcast_in_dim.6
  2.6 12.3 %all-to-all-start = ((bf16[12,288,128]{2,1,0:T(8,128)(2,1)}), bf16[12,288,128]{2,1,0:T(8,128)(2,1)S(1)}, u32[]{:S(2)}, u32[]{:S(2)}) async-start(bf16[12,288,128]{2,1,0:T(8,128)(2,1)} %broadcast_in_dim.6), calls=%async_computation | async-start | bytes 1769472 | tf_op jit(solution)/shard_map/all_to_all | solution.py:11
  14.9 1.3 collective-permute-start
  16.2 1.3 collective-permute-start.1
  17.5 5.8 %collective-permute-done.1 = bf16[1,1,16,8,128]{4,3,2,1,0:T(8,128)(2,1)S(1)} collective-permute-done((bf16[1,1,16,8,128]{4,3,2,1,0:T(8,128)(2,1)S(1)}, bf16[1,1,16,8,128]{4,3,2,1,0:T(8,128)(2,1)S(1)}, u32[]{:S(2)}, u32[]{:S(2)}) %collective-permute-start.1) | collective-permute-done | bytes 32800 | tf_op jit(solution)/shard_map/ppermute | solution.py:35
  23.7 3.5 %all-to-all-done = bf16[12,288,128]{2,1,0:T(8,128)(2,1)S(1)} async-done(((bf16[12,288,128]{2,1,0:T(8,128)(2,1)}), bf16[12,288,128]{2,1,0:T(8,128)(2,1)S(1)}, u32[]{:S(2)}, u32[]{:S(2)}) %all-to-all-start) | async-done | bytes 884768 | tf_op jit(solution)/shard_map/all_to_all | solution.py:11
  31.3 0.8 fusion.33
  40.2 0.8 fusion.20
  42.6 0.8 fusion.32
  47.4 0.8 fusion.12
  49.8 0.8 fusion.9
  50.6 0.8 fusion.8
  53.0 5.8 %collective-permute-start.2 = (bf16[1,1,16,8,128]{4,3,2,1,0:T(8,128)(2,1)S(1)}, bf16[1,1,16,8,128]{4,3,2,1,0:T(8,128)(2,1)S(1)}, u32[]{:S(2)}, u32[]{:S(2)}) collective-permute-start(bf16[1,1,16,8,128]{4,3,2,1,0:T(8,128)(2,1)S(1)} %get-tuple-element.62), channel_id=1, source_target_pairs={{0,1},{1,2},{2,3},{3,4},{4,5},{5,6},{6,7},{7,8},{8,9},{9,10},{10,1... | collective-permute-start | bytes 98312 | tf_op jit(solution)/shard_map/ppermute | solution.py:32
  58.9 1.3 collective-permute-start.3
  60.2 0.8 fusion.5
  61.0 8.2 %all-to-all-start.1 = ((bf16[12,288,128]{2,1,0:T(8,128)(2,1)}), bf16[12,288,128]{2,1,0:T(8,128)(2,1)S(1)}, u32[]{:S(2)}, u32[]{:S(2)}) async-start(bf16[12,288,128]{2,1,0:T(8,128)(2,1)} %bitcast.88), calls=%async_computation.1 | async-start | bytes 1769472 | tf_op jit(solution)/shard_map/all_to_all | solution.py:47
  73.1 14.2 %all-to-all-done.1 = bf16[12,288,128]{2,1,0:T(8,128)(2,1)S(1)} async-done(((bf16[12,288,128]{2,1,0:T(8,128)(2,1)}), bf16[12,288,128]{2,1,0:T(8,128)(2,1)S(1)}, u32[]{:S(2)}, u32[]{:S(2)}) %all-to-all-start.1) | async-done | bytes 884768 | tf_op jit(solution)/shard_map/all_to_all | solution.py:47
  88.1 10.5 %all-to-all-start.2 = ((f32[8,36,128]{2,1,0:T(8,128)}), f32[8,36,128]{2,1,0:T(8,128)S(1)}, u32[]{:S(2)}, u32[]{:S(2)}) async-start(f32[8,36,128]{2,1,0:T(8,128)} %reshape.294), calls=%async_computation.2 | async-start | bytes 327680 | tf_op jit(solution)/shard_map/all_to_all | solution.py:52
  98.9 9.1 %all-to-all-done.2 = f32[8,36,128]{2,1,0:T(8,128)S(1)} async-done(((f32[8,36,128]{2,1,0:T(8,128)}), f32[8,36,128]{2,1,0:T(8,128)S(1)}, u32[]{:S(2)}, u32[]{:S(2)}) %all-to-all-start.2) | async-done | bytes 147488 | tf_op jit(solution)/shard_map/all_to_all | solution.py:52
  108.7 6.3 %all-to-all-start.3 = ((f32[8,36,128]{2,1,0:T(8,128)}), f32[8,36,128]{2,1,0:T(8,128)S(1)}, u32[]{:S(2)}, u32[]{:S(2)}) async-start(f32[8,36,128]{2,1,0:T(8,128)} %broadcast_in_dim.7), calls=%async_computation.3 | async-start | bytes 327680 | tf_op jit(solution)/shard_map/all_to_all | solution.py:52
  115.3 13.0 %all-to-all-done.3 = f32[8,36,128]{2,1,0:T(8,128)S(1)} async-done(((f32[8,36,128]{2,1,0:T(8,128)}), f32[8,36,128]{2,1,0:T(8,128)S(1)}, u32[]{:S(2)}, u32[]{:S(2)}) %all-to-all-start.3) | async-done | bytes 147488 | tf_op jit(solution)/shard_map/all_to_all | solution.py:52
  129.1 3.4 %all-to-all-start.4 = ((f32[8,36,128]{2,1,0:T(8,128)}), f32[8,36,128]{2,1,0:T(8,128)S(1)}, u32[]{:S(2)}, u32[]{:S(2)}) async-start(f32[8,36,128]{2,1,0:T(8,128)} %broadcast_in_dim.8), calls=%async_computation.4 | async-start | bytes 327680 | tf_op jit(solution)/shard_map/all_to_all | solution.py:52
  133.5 8.7 %all-to-all-done.4 = f32[8,36,128]{2,1,0:T(8,128)S(1)} async-done(((f32[8,36,128]{2,1,0:T(8,128)}), f32[8,36,128]{2,1,0:T(8,128)S(1)}, u32[]{:S(2)}, u32[]{:S(2)}) %all-to-all-start.4) | async-done | bytes 147488 | tf_op jit(solution)/shard_map/all_to_all | solution.py:52
  (107 shorter events, 29.6 us)
Async XLA Ops:
  2.6 12.3 %copy-start = (bf16[1,2,16,8,128]{4,3,2,1,0:T(8,128)(2,1)S(1)}, bf16[1,2,16,8,128]{4,3,2,1,0:T(8,128)(2,1)}, u32[]{:S(2)}) copy-start(bf16[1,2,16,8,128]{4,3,2,1,0:T(8,128)(2,1)} %param.5) | copy-start | bytes 196612
  2.6 24.5 %all-to-all-start = ((bf16[12,288,128]{2,1,0:T(8,128)(2,1)}), bf16[12,288,128]{2,1,0:T(8,128)(2,1)S(1)}, u32[]{:S(2)}, u32[]{:S(2)}) async-start(bf16[12,288,128]{2,1,0:T(8,128)(2,1)} %broadcast_in_dim.6), calls=%async_computation | async-start | bytes 1769472 | tf_op jit(solution)/shard_map/all_to_all | solution.py:11
  14.9 2.6 %collective-permute-start = (bf16[1,1,16,8,128]{4,3,2,1,0:T(8,128)(2,1)S(1)}, bf16[1,1,16,8,128]{4,3,2,1,0:T(8,128)(2,1)S(1)}, u32[]{:S(2)}, u32[]{:S(2)}) collective-permute-start(bf16[1,1,16,8,128]{4,3,2,1,0:T(8,128)(2,1)S(1)} %get-tuple-element.66), channel_id=1, source_target_pairs={{0,1},{1,2},{2,3},{3,4},{4,5},{5,6},{6,7},{7,8},{8,9},{9,10},{10,1... | collective-permute-start | bytes 98312 | tf_op jit(solution)/shard_map/ppermute | solution.py:32
  16.2 7.1 %collective-permute-start.1 = (bf16[1,1,16,8,128]{4,3,2,1,0:T(8,128)(2,1)S(1)}, bf16[1,1,16,8,128]{4,3,2,1,0:T(8,128)(2,1)S(1)}, u32[]{:S(2)}, u32[]{:S(2)}) collective-permute-start(bf16[1,1,16,8,128]{4,3,2,1,0:T(8,128)(2,1)S(1)} %get-tuple-element.67), channel_id=1, source_target_pairs={{1,0},{2,1},{3,2},{4,3},{5,4},{6,5},{7,6},{8,7},{9,8},{10,9},{11,1... | collective-permute-start | bytes 98312 | tf_op jit(solution)/shard_map/ppermute | solution.py:35
  30.5 0.8 copy-start.4
  53.0 16.2 %collective-permute-start.2 = (bf16[1,1,16,8,128]{4,3,2,1,0:T(8,128)(2,1)S(1)}, bf16[1,1,16,8,128]{4,3,2,1,0:T(8,128)(2,1)S(1)}, u32[]{:S(2)}, u32[]{:S(2)}) collective-permute-start(bf16[1,1,16,8,128]{4,3,2,1,0:T(8,128)(2,1)S(1)} %get-tuple-element.62), channel_id=1, source_target_pairs={{0,1},{1,2},{2,3},{3,4},{4,5},{5,6},{6,7},{7,8},{8,9},{9,10},{10,1... | collective-permute-start | bytes 98312 | tf_op jit(solution)/shard_map/ppermute | solution.py:32
  58.9 10.3 %collective-permute-start.3 = (bf16[1,1,16,8,128]{4,3,2,1,0:T(8,128)(2,1)S(1)}, bf16[1,1,16,8,128]{4,3,2,1,0:T(8,128)(2,1)S(1)}, u32[]{:S(2)}, u32[]{:S(2)}) collective-permute-start(bf16[1,1,16,8,128]{4,3,2,1,0:T(8,128)(2,1)S(1)} %get-tuple-element.63), channel_id=1, source_target_pairs={{1,0},{2,1},{3,2},{4,3},{5,4},{6,5},{7,6},{8,7},{9,8},{10,9},{11,1... | collective-permute-start | bytes 98312 | tf_op jit(solution)/shard_map/ppermute | solution.py:35
  61.0 26.3 %all-to-all-start.1 = ((bf16[12,288,128]{2,1,0:T(8,128)(2,1)}), bf16[12,288,128]{2,1,0:T(8,128)(2,1)S(1)}, u32[]{:S(2)}, u32[]{:S(2)}) async-start(bf16[12,288,128]{2,1,0:T(8,128)(2,1)} %bitcast.88), calls=%async_computation.1 | async-start | bytes 1769472 | tf_op jit(solution)/shard_map/all_to_all | solution.py:47
  88.1 20.0 %all-to-all-start.2 = ((f32[8,36,128]{2,1,0:T(8,128)}), f32[8,36,128]{2,1,0:T(8,128)S(1)}, u32[]{:S(2)}, u32[]{:S(2)}) async-start(f32[8,36,128]{2,1,0:T(8,128)} %reshape.294), calls=%async_computation.2 | async-start | bytes 327680 | tf_op jit(solution)/shard_map/all_to_all | solution.py:52
  108.7 19.6 %all-to-all-start.3 = ((f32[8,36,128]{2,1,0:T(8,128)}), f32[8,36,128]{2,1,0:T(8,128)S(1)}, u32[]{:S(2)}, u32[]{:S(2)}) async-start(f32[8,36,128]{2,1,0:T(8,128)} %broadcast_in_dim.7), calls=%async_computation.3 | async-start | bytes 327680 | tf_op jit(solution)/shard_map/all_to_all | solution.py:52
  129.1 13.1 %all-to-all-start.4 = ((f32[8,36,128]{2,1,0:T(8,128)}), f32[8,36,128]{2,1,0:T(8,128)S(1)}, u32[]{:S(2)}, u32[]{:S(2)}) async-start(f32[8,36,128]{2,1,0:T(8,128)} %broadcast_in_dim.8), calls=%async_computation.4 | async-start | bytes 327680 | tf_op jit(solution)/shard_map/all_to_all | solution.py:52
  132.4 9.8 %copy-start.1 = (f32[288,128]{1,0:T(8,128)S(1)}, f32[288,128]{1,0:T(8,128)}, u32[]{:S(2)}) copy-start(f32[288,128]{1,0:T(8,128)} %param.7) | copy-start | bytes 442372
  132.5 9.8 %copy-start.2 = (f32[288,128]{1,0:T(8,128)S(1)}, f32[288,128]{1,0:T(8,128)}, u32[]{:S(2)}) copy-start(f32[288,128]{1,0:T(8,128)} %param.9) | copy-start | bytes 442372
  132.5 9.8 %copy-start.3 = (f32[288,128]{1,0:T(8,128)S(1)}, f32[288,128]{1,0:T(8,128)}, u32[]{:S(2)}) copy-start(f32[288,128]{1,0:T(8,128)} %param.8) | copy-start | bytes 442372

commit v2 on v0

v2 whole, which is shorter than its diff:
```python
import functools
import math

import jax
import jax.numpy as jnp
from jax import lax
from jax.experimental import pallas as pl
from jax.experimental.pallas import tpu as pltpu
from jax.sharding import PartitionSpec as P

F32 = jnp.float32
BF16 = jnp.bfloat16
OUTER = 8
MIDDLE = 4
PAIR = 2
HALF = 64
PIECE = 24


def core_is_low():
    return lax.rem(lax.axis_index("spatial"), PAIR) == 0


def lane_of(shape):
    return lax.broadcasted_iota(jnp.int32, shape, len(shape) - 1)


def pick(low, when_low, when_high):
    return jnp.where(low, when_low, when_high)


def pack_body(master_ref, volume_ref, send_ref, edge_ref):
    low = core_is_low()
    rows = master_ref.shape[0] // 2
    top = master_ref[:rows]
    bottom = master_ref[rows:]
    first = pick(low, top, pltpu.roll(top, HALF, 1))
    second = pick(low, pltpu.roll(bottom, HALF, 1), bottom)
    packed = jnp.where(lane_of(top.shape) < HALF, first, second).astype(BF16)
    for owner in range(send_ref.shape[0]):
        send_ref[owner] = packed
    edge_ref[...] = pick(low, volume_ref[0, 0].astype(F32), volume_ref[0, 1].astype(F32)).astype(BF16)


def shifted(plane, dy, dx):
    rows, cols, width = plane.shape
    if dx:
        at = lax.broadcasted_iota(jnp.int32, plane.shape, 1)
        keep = at < cols - 1 if dx > 0 else at > 0
        plane = jnp.where(keep, pltpu.roll(plane, (-dx) % cols, 1), 0.0)
    if dy:
        gap = jnp.zeros((1, cols, width), plane.dtype)
        plane = jnp.concatenate([plane[1:], gap] if dy > 0 else [gap, plane[:-1]], axis=0)
    return plane


def write_windows(window_ref, planes, sign):
    cells = planes[0].shape[0] * planes[0].shape[1]
    width = planes[0].shape[2]
    for index, plane in enumerate(planes):
        for dx in (-1, 0, 1):
            column = shifted(plane, 0, dx)
            for dy in (-1, 0, 1):
                tap = (sign * dy + 1) * 3 + sign * dx + 1
                window_ref[index * cells : (index + 1) * cells, tap * width : (tap + 1) * width] = (
                    shifted(column, dy, 0).reshape(cells, width).astype(BF16)
                )


def forward_body(
    kernel_ref,
    volume_ref,
    beside_ref,
    far_ref,
    near_ref,
    cot_ref,
    cot_beside_ref,
    half_kernel_ref,
    own_act_ref,
    swap_ref,
    near_grad_ref,
    far_grad_ref,
    weight_ref,
    window_ref,
    turned_ref,
    total_ref,
):
    low = core_is_low()
    owners, rows, width = kernel_ref.shape
    mask = (lane_of((rows, width)) < HALF) == low
    for owner in range(owners):
        packed = kernel_ref[owner].astype(F32)
        rolled = pltpu.roll(packed, HALF, 1)
        base = owner * 2 * rows
        half_kernel_ref[base : base + rows] = jnp.where(mask, pick(low, packed, rolled), 0.0).astype(BF16)
        half_kernel_ref[base + rows : base + 2 * rows] = jnp.where(
            mask, pick(low, rolled, packed), 0.0
        ).astype(BF16)
    own = [volume_ref[0, i].astype(F32) for i in range(2)]
    beside = [beside_ref[0, i].astype(F32) for i in range(2)]
    far = far_ref[...].astype(F32)
    near = near_ref[...].astype(F32)
    planes = [pick(low, near, far)]
    planes += [pick(low, own[i], beside[i]) for i in range(2)]
    planes += [pick(low, beside[i], own[i]) for i in range(2)]
    planes += [pick(low, far, near)]
    write_windows(window_ref, planes, 1)
    cells = planes[0].shape[0] * planes[0].shape[1]
    count = 4 * cells
    span = 9 * width
    preact = jnp.zeros((count, width), F32)
    for a in range(3):
        preact = preact + jnp.dot(
            window_ref[a * cells : a * cells + count],
            half_kernel_ref[a * span : (a + 1) * span],
            preferred_element_type=F32,
        )
    sigma = jax.nn.sigmoid(preact)
    slope = sigma * (1.0 + preact * (1.0 - sigma))
    activation = (preact * sigma).astype(BF16)
    cot_own = cot_ref[0].astype(F32).reshape(2 * cells, width)
    cot_beside = cot_beside_ref[0].astype(F32).reshape(2 * cells, width)
    cotangent = jnp.concatenate(
        [pick(low, cot_own, cot_beside), pick(low, cot_beside, cot_own)], axis=0
    )
    wide_mask = (lane_of((count, width)) < HALF) == low
    grad = jnp.where(wide_mask, cotangent * slope, 0.0)
    rounded = grad.astype(BF16)
    swap_ref[:count] = rounded
    act_low = activation[: 2 * cells]
    act_high = activation[2 * cells :]
    own_act_ref[...] = pick(low, act_low.astype(F32), act_high.astype(F32)).astype(BF16)
    swap_ref[count:] = pick(low, act_high.astype(F32), act_low.astype(F32)).astype(BF16)
    first = grad[:cells]
    last = grad[3 * cells :]
    near_grad_ref[...] = pick(low, first, last).astype(BF16)
    far_grad_ref[...] = pick(low, last, first).astype(BF16)
    turned_ref[...] = grad.T.astype(BF16)
    mine = pick(low, turned_ref[:HALF].astype(F32), turned_ref[HALF:].astype(F32)).astype(BF16)
    for a in range(3):
        total_ref[:, a * span : (a + 1) * span] = jnp.dot(
            mine, window_ref[a * cells : a * cells + count], preferred_element_type=F32
        )
    lane = lane_of((HALF, width))

    def columns(start):
        tile, offset = divmod(start, width)
        here = total_ref[:, tile * width : (tile + 1) * width]
        if not offset:
            return here
        here = pltpu.roll(here, width - offset, 1)
        if (tile + 1) * width >= total_ref.shape[1]:
            return here
        after = pltpu.roll(total_ref[:, (tile + 1) * width : (tile + 2) * width], width - offset, 1)
        return jnp.where(lane < width - offset, here, after)

    shard = 2 * rows
    rest = shard - 2 * width
    folds = width // rest
    group = HALF // folds
    for owner in range(owners):
        start = owner * shard
        weight_ref[owner, :HALF] = columns(start).astype(BF16)
        weight_ref[owner, HALF : 2 * HALF] = columns(start + width).astype(BF16)
        tail = columns(start + 2 * width)
        folded = tail[:group]
        for fold in range(1, folds):
            part = pltpu.roll(tail[fold * group : (fold + 1) * group], fold * rest, 1)
            folded = jnp.where(lane[:group] >= fold * rest, part, folded)
        weight_ref[owner, 2 * HALF :] = folded.astype(BF16)


def backward_body(
    mine_ref, other_ref, own_ref, got_ref, near_ref, far_ref, act_ref, out_act_ref, out_ref, window_ref
):
    low = core_is_low()
    cells, width = near_ref.shape
    shape = out_ref.shape[2:]
    count = 4 * cells
    full = own_ref[:count].astype(F32) + got_ref[:count].astype(F32)
    edge = (near_ref[...].astype(F32) + far_ref[...].astype(F32)).reshape(shape)
    grads = [full[i * cells : (i + 1) * cells].reshape(shape) for i in range(4)]
    planes = [pick(low, edge, grads[1]), pick(low, grads[0], grads[2])]
    planes += [pick(low, grads[1], grads[3]), pick(low, grads[2], edge)]
    write_windows(window_ref, planes, -1)
    total = jnp.zeros((2 * cells, width), F32)
    for a in range(3):
        for e in range(9):
            tap = a * 9 + e
            weight = mine_ref[tap * width : (tap + 1) * width] + other_ref[tap * width : (tap + 1) * width]
            total = total + lax.dot_general(
                window_ref[(2 - a) * cells : (4 - a) * cells, e * width : (e + 1) * width],
                weight,
                (((1,), (1,)), ((), ())),
                preferred_element_type=F32,
            )
    out_ref[0] = total.reshape(2, *shape).astype(BF16)
    activation = act_ref[...].astype(F32) + got_ref[count:].astype(F32)
    lane_low = (lane_of(activation.shape) < HALF) == low
    activation = jnp.where(lane_low, act_ref[...].astype(F32), got_ref[count:].astype(F32))
    out_act_ref[0] = activation.reshape(2, *shape).astype(BF16)


def update_body(cells_all, grads_ref, master_ref, moment_ref, second_ref, out_ref, out_m_ref, out_s_ref, grad_ref):
    rows, width = master_ref.shape
    pieces = rows // 2 // PIECE
    halves = []
    for half in range(PAIR):
        halves.append(
            jnp.concatenate([grads_ref[PAIR * i + half] for i in range(pieces)], axis=0)
        )
    rest = rows - 2 * width
    folds = width // rest
    group = HALF // folds
    for part in range(2):
        both = jnp.concatenate([h[part * HALF : (part + 1) * HALF] for h in halves], axis=0)
        grad_ref[part * width : (part + 1) * width] = both.T
    tails = []
    for h in halves:
        tail = h[2 * HALF :]
        for fold in range(folds):
            tails.append(pltpu.roll(tail, width - fold * rest, 1) if fold else tail)
    assert len(tails) * group == width
    grad_ref[2 * width :] = jnp.concatenate(tails, axis=0).T[:rest]
    weight_grad = grad_ref[...] / math.sqrt(cells_all)
    moment_next = 0.9 * moment_ref[...] + 0.1 * weight_grad
    second_next = 0.999 * second_ref[...] + 0.001 * weight_grad * weight_grad
    master = master_ref[...]
    out_ref[...] = master - 0.001 * (moment_next / (jnp.sqrt(second_next) + 1e-08) + 0.01 * master)
    out_m_ref[...] = moment_next
    out_s_ref[...] = second_next


def exchanged(tiles, groups):
    return lax.all_to_all(tiles, "spatial", 0, 0, tiled=True, axis_index_groups=groups)


def moved(value, perm):
    return lax.ppermute(value, "spatial", perm)


def per_device(volume, cotangent, master, moment, second):
    _, planes, rows, cols, width = volume.shape
    cells = rows * cols
    owners = lax.axis_size("dp")
    count = lax.axis_size("spatial")
    shard = master.shape[0]
    taps_all = owners * shard
    like = jax.ShapeDtypeStruct

    def inside(pairs):
        return [(i, j) for i, j in pairs if 0 <= j < count]

    swap = [(i, i ^ 1) for i in range(count)]
    near = inside((i, i - 1 if i % 2 == 0 else i + 1) for i in range(count))
    far_out = inside((i, i - 2 if i % 2 == 0 else i + 2) for i in range(count))
    far_in = inside((i, i + 2 if i % 2 == 0 else i - 2) for i in range(count))

    send, edge = pl.pallas_call(
        pack_body,
        out_shape=(like((owners, shard // 2, width), BF16), like((rows, cols, width), BF16)),
        name="pack",
    )(master, volume)
    halves = lax.all_to_all(send, "dp", 0, 0, tiled=True)
    far_plane = moved(edge, far_out)
    near_plane = moved(edge, near)
    beside = moved(volume, swap)
    cot_beside = moved(cotangent, swap)
    half_kernel, own_act, swapped, near_grad, far_grad, weight = pl.pallas_call(
        forward_body,
        out_shape=(
            like((taps_all, width), BF16),
            like((2 * cells, width), BF16),
            like((6 * cells, width), BF16),
            like((cells, width), BF16),
            like((cells, width), BF16),
            like((owners, shard // 2, width), BF16),
        ),
        scratch_shapes=[
            pltpu.VMEM((6 * cells, 9 * width), BF16),
            pltpu.VMEM((width, 4 * cells), BF16),
            pltpu.VMEM((HALF, taps_all), F32),
        ],
        name="forward",
    )(halves, volume, beside, far_plane, near_plane, cotangent, cot_beside)
    arrived = lax.all_to_all(weight, "dp", 0, 0, tiled=True)

    got = moved(swapped, swap)
    near_got = moved(near_grad, near)
    far_got = moved(far_grad, far_in)
    other_kernel = moved(half_kernel, swap)
    activation, input_grad = pl.pallas_call(
        backward_body,
        out_shape=(like(volume.shape, BF16), like(volume.shape, BF16)),
        scratch_shapes=[pltpu.VMEM((4 * cells, 9 * width), BF16)],
        cost_estimate=pl.CostEstimate(
            flops=2 * 2 * cells * taps_all * width, bytes_accessed=4 * taps_all * width, transcendentals=0
        ),
        name="backward",
    )(half_kernel, other_kernel, swapped, got, near_got, far_got, own_act)

    same_y = [
        [(y * MIDDLE + h) * PAIR + c for h in range(MIDDLE)] for y in range(OUTER) for c in range(PAIR)
    ]
    same_rest = [[y * MIDDLE * PAIR + r for y in range(OUTER)] for r in range(MIDDLE * PAIR)]
    same_z = [
        [(y * MIDDLE + h) * PAIR + c for y in range(OUTER) for c in range(PAIR)] for h in range(MIDDLE)
    ]
    pieces = shard // 2 // PIECE
    summed = arrived.astype(F32).sum(axis=0).reshape(pieces, PIECE, width)
    summed = jnp.pad(summed, ((0, OUTER - pieces), (0, 0), (0, 0)))
    piece = exchanged(summed, same_rest).sum(0)
    piece = exchanged(jnp.broadcast_to(piece[None], (MIDDLE, PIECE, width)), same_y).sum(0)
    joined = exchanged(jnp.broadcast_to(piece[None], (OUTER * PAIR, PIECE, width)), same_z)
    cells_all = owners * count * planes * cells
    state = like(master.shape, F32)
    master_next, moment_next, second_next = pl.pallas_call(
        functools.partial(update_body, cells_all),
        out_shape=(state, state, state),
        scratch_shapes=[pltpu.VMEM(master.shape, F32)],
        name="update",
    )(joined, master, moment, second)
    return (activation, input_grad, master_next, moment_next, second_next)


def solution(mesh):
    return jax.shard_map(
        per_device,
        mesh=mesh,
        in_specs=(
            P("dp", "spatial", None, None, None),
            P("dp", "spatial", None, None, None),
            P("dp", None),
            P("dp", None),
            P("dp", None),
        ),
        out_specs=(
            P("dp", "spatial", None, None, None),
            P("dp", "spatial", None, None, None),
            P("dp", None),
            P("dp", None),
            P("dp", None),
        ),
        check_vma=False,
    )
```

time: 224 us -> 117 us (0.52)
  the two profiles are of different devices: /device:TPU:67 before, /device:TPU:38 now
where the time goes in v2:
time: 117 us; the launch traced here: 116 us
  starting transfers between devices  57.2 us (49%)
  blocking collectives  26.1 us (22%)
  waiting for transfers between devices  17.2 us (15%)
  Pallas kernels  11.2 us (10%)
  local copies, waits for them, and re-layouts  3.84 us (3%)
    ppermute x8, starting transfers between devices, moved(): return lax.ppermute(value, 'spatial', perm)  31.8 us
    all_to_all x2, blocking collectives, exchanged(): lax.all_to_all(tiles, 'spatial', 0, 0, tiled=True, axis_index_groups=groups)  26.1 us
    ppermute x8, waiting for transfers between devices, moved(): return lax.ppermute(value, 'spatial', perm)  9.55 us
    all_to_all x1, starting transfers between devices, exchanged(): lax.all_to_all(tiles, 'spatial', 0, 0, tiled=True, axis_index_groups=groups)  8.86 us
    all_to_all x1, starting transfers between devices, per_device(): halves = lax.all_to_all(send, 'dp', 0, 0, tiled=True)  8.54 us
    all_to_all x1, starting transfers between devices, per_device(): arrived = lax.all_to_all(weight, 'dp', 0, 0, tiled=True)  7.95 us
    all_to_all x1, waiting for transfers between devices, per_device(): arrived = lax.all_to_all(weight, 'dp', 0, 0, tiled=True)  7.62 us
    pallas_call x1, Pallas kernels, per_device(): pl.pallas_call(forward_body, out_shape=(like((taps_all, width), BF16), li...  4.5 us
  transfers between devices with their start and end apart: 11, of which 4 were waited for; matrix products, arithmetic and copies ran while one was open for 1% of the time, Pallas kernels for 2%

profile of v2, /device:TPU:38, one launch (start us, length us, event | category | flops | bytes accessed | tf_op | source)
XLA Modules:
  0.0 116.4 jit_solution(10650799361732578124)
XLA Ops:
  0.6 1.8 %pack.1 = (bf16[12,144,128]{2,1,0:T(8,128)(2,1)}, bf16[16,8,128]{2,1,0:T(8,128)(2,1)}) custom-call(f32[288,128]{1,0:T(8,128)} %master_ref.3, bf16[1,2,16,8,128]{4,3,2,1,0:T(8,128)(2,1)} %volume_ref.3), custom_call_target="tpu_custom_call" | custom-call | tf_op jit(solution)/shard_map/pack/pallas_call | solution.py:259
  2.4 8.5 %all-to-all-start = ((bf16[12,144,128]{2,1,0:T(8,128)(2,1)}), bf16[12,144,128]{2,1,0:T(8,128)(2,1)S(1)}, u32[]{:S(2)}, u32[]{:S(2)}) async-start(bf16[12,144,128]{2,1,0:T(8,128)(2,1)} %get-tuple-element.18), calls=%async_computation | async-start | bytes 884736 | tf_op jit(solution)/shard_map/all_to_all | solution.py:264
  11.0 1.9 %collective-permute-start.3 = (bf16[1,2,16,8,128]{4,3,2,1,0:T(8,128)(2,1)S(1)}, bf16[1,2,16,8,128]{4,3,2,1,0:T(8,128)(2,1)S(1)}, u32[]{:S(2)}, u32[]{:S(2)}) collective-permute-start(bf16[1,2,16,8,128]{4,3,2,1,0:T(8,128)(2,1)S(1)} %copy-done.7), channel_id=1, source_target_pairs={{0,1},{1,0},{2,3},{3,2},{4,5},{5,4},{6,7},{7,6},{8,9},{9,8},{10,11... | collective-permute-start | bytes 196616 | tf_op jit(solution)/shard_map/ppermute | solution.py:239
  12.9 2.4 %collective-permute-start = (bf16[1,2,16,8,128]{4,3,2,1,0:T(8,128)(2,1)S(1)}, bf16[1,2,16,8,128]{4,3,2,1,0:T(8,128)(2,1)S(1)}, u32[]{:S(2)}, u32[]{:S(2)}) collective-permute-start(bf16[1,2,16,8,128]{4,3,2,1,0:T(8,128)(2,1)S(1)} %copy-done.4), channel_id=1, source_target_pairs={{0,1},{1,0},{2,3},{3,2},{4,5},{5,4},{6,7},{7,6},{8,9},{9,8},{10,11... | collective-permute-start | bytes 196616 | tf_op jit(solution)/shard_map/ppermute | solution.py:239
  15.3 12.3 %collective-permute-start.2 = (bf16[16,8,128]{2,1,0:T(8,128)(2,1)S(1)}, bf16[16,8,128]{2,1,0:T(8,128)(2,1)S(1)}, u32[]{:S(2)}, u32[]{:S(2)}) collective-permute-start(bf16[16,8,128]{2,1,0:T(8,128)(2,1)S(1)} %copy-done.16), channel_id=1, source_target_pairs={{1,2},{2,1},{3,4},{4,3},{5,6},{6,5},{7,8},{8,7},{9,10},{10,9},{11,... | collective-permute-start | bytes 98312 | tf_op jit(solution)/shard_map/ppermute | solution.py:239
  27.6 3.7 %collective-permute-start.1 = (bf16[16,8,128]{2,1,0:T(8,128)(2,1)S(1)}, bf16[16,8,128]{2,1,0:T(8,128)(2,1)S(1)}, u32[]{:S(2)}, u32[]{:S(2)}) collective-permute-start(bf16[16,8,128]{2,1,0:T(8,128)(2,1)S(1)} %copy-done.16), channel_id=1, source_target_pairs={{1,3},{2,0},{3,5},{4,2},{5,7},{6,4},{7,9},{8,6},{9,11},{10,8},{11,... | collective-permute-start | bytes 98312 | tf_op jit(solution)/shard_map/ppermute | solution.py:239
  31.3 3.9 %collective-permute-done.1.far_ref = bf16[16,8,128]{2,1,0:T(8,128)(2,1)S(1)} collective-permute-done((bf16[16,8,128]{2,1,0:T(8,128)(2,1)S(1)}, bf16[16,8,128]{2,1,0:T(8,128)(2,1)S(1)}, u32[]{:S(2)}, u32[]{:S(2)}) %collective-permute-start.1) | collective-permute-done | bytes 32800 | tf_op jit(solution)/shard_map/ppermute | solution.py:239
  35.9 0.8 copy-done
  36.7 4.5 %forward.1 = (bf16[3456,128]{1,0:T(8,128)(2,1)}, bf16[256,128]{1,0:T(8,128)(2,1)}, bf16[768,128]{1,0:T(8,128)(2,1)}, bf16[128,128]{1,0:T(8,128)(2,1)}, bf16[128,...) custom-call(bf16[12,144,128]{2,1,0:T(8,128)(2,1)} %copy-done, bf16[1,2,16,8,128]{4,3,2,1,0:T(8,128)(2,1)} %volume_ref.3, ...), custom_call_target="tpu_custom_call" | custom-call | tf_op jit(solution)/shard_map/forward/pallas_call | solution.py:269
  41.2 7.9 %all-to-all-start.1 = ((bf16[12,144,128]{2,1,0:T(8,128)(2,1)}), bf16[12,144,128]{2,1,0:T(8,128)(2,1)S(1)}, u32[]{:S(2)}, u32[]{:S(2)}) async-start(bf16[12,144,128]{2,1,0:T(8,128)(2,1)} %get-tuple-element.27), calls=%async_computation.1 | async-start | bytes 884736 | tf_op jit(solution)/shard_map/all_to_all | solution.py:286
  49.1 1.9 %collective-permute-start.4 = (bf16[3456,128]{1,0:T(8,128)(2,1)S(1)}, bf16[3456,128]{1,0:T(8,128)(2,1)S(1)}, u32[]{:S(2)}, u32[]{:S(2)}) collective-permute-start(bf16[3456,128]{1,0:T(8,128)(2,1)S(1)} %copy-done.1), channel_id=1, source_target_pairs={{0,1},{1,0},{2,3},{3,2},{4,5},{5,4},{6,7},{7,6},{8,9},{9,8},{10,11... | collective-permute-start | bytes 2654216 | tf_op jit(solution)/shard_map/ppermute | solution.py:239
  51.1 7.6 %all-to-all-done.1 = bf16[12,144,128]{2,1,0:T(8,128)(2,1)S(1)} async-done(((bf16[12,144,128]{2,1,0:T(8,128)(2,1)}), bf16[12,144,128]{2,1,0:T(8,128)(2,1)S(1)}, u32[]{:S(2)}, u32[]{:S(2)}) %all-to-all-start.1) | async-done | bytes 442400 | tf_op jit(solution)/shard_map/all_to_all | solution.py:286
  58.8 10.3 %all_to_all.25 = f32[8,24,128]{2,1,0:T(8,128)S(1)} all-to-all(f32[8,24,128]{2,1,0:T(8,128)S(1)} %pad.4), channel_id=1, replica_groups={{0,8,16,24,32,40,48,56},{1,9,17,25,33,41,49,57},{2,10,18,26,34,42,50,58..., dimensions={0} | all-to-all | bytes 196608 | tf_op jit(solution)/shard_map/all_to_all | solution.py:235
  69.1 15.8 %all_to_all.26 = f32[4,24,128]{2,1,0:T(8,128)S(1)} all-to-all(f32[4,24,128]{2,1,0:T(8,128)S(1)} %broadcast_in_dim.4), channel_id=1, replica_groups={{0,2,4,6},{1,3,5,7},{8,10,12,14},{9,11,13,15},{16,18,20,22},{17,19,21,2..., dimensions={0} | all-to-all | bytes 98304 | tf_op jit(solution)/shard_map/all_to_all | solution.py:235
  84.9 0.7 broadcast_in_dim.5
  85.6 8.9 %all-to-all-start.4 = ((f32[16,24,128]{2,1,0:T(8,128)}), f32[16,24,128]{2,1,0:T(8,128)S(1)}, u32[]{:S(2)}, u32[]{:S(2)}) async-start(f32[16,24,128]{2,1,0:T(8,128)} %broadcast_in_dim.5), calls=%async_computation.4 | async-start | bytes 393216 | tf_op jit(solution)/shard_map/all_to_all | solution.py:235
  94.4 2.0 %collective-permute-start.5 = (bf16[768,128]{1,0:T(8,128)(2,1)S(1)}, bf16[768,128]{1,0:T(8,128)(2,1)S(1)}, u32[]{:S(2)}, u32[]{:S(2)}) collective-permute-start(bf16[768,128]{1,0:T(8,128)(2,1)S(1)} %copy-done.5), channel_id=1, source_target_pairs={{0,1},{1,0},{2,3},{3,2},{4,5},{5,4},{6,7},{7,6},{8,9},{9,8},{10,11... | collective-permute-start | bytes 589832 | tf_op jit(solution)/shard_map/ppermute | solution.py:239
  96.5 2.3 %collective-permute-start.6 = (bf16[128,128]{1,0:T(8,128)(2,1)S(1)}, bf16[128,128]{1,0:T(8,128)(2,1)S(1)}, u32[]{:S(2)}, u32[]{:S(2)}) collective-permute-start(bf16[128,128]{1,0:T(8,128)(2,1)S(1)} %copy-done.15), channel_id=1, source_target_pairs={{1,2},{2,1},{3,4},{4,3},{5,6},{6,5},{7,8},{8,7},{9,10},{10,9},{11,... | collective-permute-start | bytes 98312 | tf_op jit(solution)/shard_map/ppermute | solution.py:239
  98.8 5.3 %collective-permute-start.7 = (bf16[128,128]{1,0:T(8,128)(2,1)S(1)}, bf16[128,128]{1,0:T(8,128)(2,1)S(1)}, u32[]{:S(2)}, u32[]{:S(2)}) collective-permute-start(bf16[128,128]{1,0:T(8,128)(2,1)S(1)} %copy-done.14), channel_id=1, source_target_pairs={{0,2},{2,4},{3,1},{4,6},{5,3},{6,8},{7,5},{8,10},{9,7},{10,12},{11... | collective-permute-start | bytes 98312 | tf_op jit(solution)/shard_map/ppermute | solution.py:239
  104.1 2.7 %collective-permute-done.6.near_ref = bf16[128,128]{1,0:T(8,128)(2,1)S(1)} collective-permute-done((bf16[128,128]{1,0:T(8,128)(2,1)S(1)}, bf16[128,128]{1,0:T(8,128)(2,1)S(1)}, u32[]{:S(2)}, u32[]{:S(2)}) %collective-permute-start.6) | collective-permute-done | bytes 32800 | tf_op jit(solution)/shard_map/ppermute | solution.py:239
  106.8 2.9 %collective-permute-done.7.far_ref = bf16[128,128]{1,0:T(8,128)(2,1)S(1)} collective-permute-done((bf16[128,128]{1,0:T(8,128)(2,1)S(1)}, bf16[128,128]{1,0:T(8,128)(2,1)S(1)}, u32[]{:S(2)}, u32[]{:S(2)}) %collective-permute-start.7) | collective-permute-done | bytes 32800 | tf_op jit(solution)/shard_map/ppermute | solution.py:239
  110.8 2.8 %backward.1 = (bf16[1,2,16,8,128]{4,3,2,1,0:T(8,128)(2,1)}, bf16[1,2,16,8,128]{4,3,2,1,0:T(8,128)(2,1)}) custom-call(bf16[3456,128]{1,0:T(8,128)(2,1)} %get-tuple-element.20.mine_ref, bf16[3456,128]{1,0:T(8,128)(2,1)} %copy-done.2, bf16[768,128]{1,0:T(8,128)(2,1)} %get-tuple-element.21.own_ref, bf16[768,128]{1,0:T(8,128)(2,1)} %copy-done.6, ...), custom_call_target="tpu_custom_call" | custom-call | flops 226492416 | bytes 1769472 | tf_op jit(solution)/shard_map/backward/pallas_call | solution.py:292
  113.6 0.7 copy-done.3
  114.3 2.1 %update.1 = (f32[288,128]{1,0:T(8,128)}, f32[288,128]{1,0:T(8,128)}, f32[288,128]{1,0:T(8,128)}) custom-call(f32[16,24,128]{2,1,0:T(8,128)} %copy-done.3, f32[288,128]{1,0:T(8,128)} %master_ref.3, f32[288,128]{1,0:T(8,128)} %moment_ref.1, f32[288,128]{1,0:T(8,128)} %second_ref.1), custom_call_target="tpu_custom_call" | custom-call | tf_op jit(solution)/shard_map/update/pallas_call | solution.py:317
  (44 shorter events, 1.8 us)
Async XLA Ops:
  2.4 8.6 %copy-start.7 = (bf16[1,2,16,8,128]{4,3,2,1,0:T(8,128)(2,1)S(1)}, bf16[1,2,16,8,128]{4,3,2,1,0:T(8,128)(2,1)}, u32[]{:S(2)}) copy-start(bf16[1,2,16,8,128]{4,3,2,1,0:T(8,128)(2,1)} %cot_ref.1) | copy-start | bytes 196612
  2.4 10.5 %copy-start.4 = (bf16[1,2,16,8,128]{4,3,2,1,0:T(8,128)(2,1)S(1)}, bf16[1,2,16,8,128]{4,3,2,1,0:T(8,128)(2,1)}, u32[]{:S(2)}) copy-start(bf16[1,2,16,8,128]{4,3,2,1,0:T(8,128)(2,1)} %volume_ref.3) | copy-start | bytes 196612
  2.4 12.9 %copy-start.16 = (bf16[16,8,128]{2,1,0:T(8,128)(2,1)S(1)}, bf16[16,8,128]{2,1,0:T(8,128)(2,1)}, u32[]{:S(2)}) copy-start(bf16[16,8,128]{2,1,0:T(8,128)(2,1)} %get-tuple-element.19) | copy-start | bytes 98308
  2.4 32.8 %all-to-all-start = ((bf16[12,144,128]{2,1,0:T(8,128)(2,1)}), bf16[12,144,128]{2,1,0:T(8,128)(2,1)S(1)}, u32[]{:S(2)}, u32[]{:S(2)}) async-start(bf16[12,144,128]{2,1,0:T(8,128)(2,1)} %get-tuple-element.18), calls=%async_computation | async-start | bytes 884736 | tf_op jit(solution)/shard_map/all_to_all | solution.py:264
  11.0 24.3 %collective-permute-start.3 = (bf16[1,2,16,8,128]{4,3,2,1,0:T(8,128)(2,1)S(1)}, bf16[1,2,16,8,128]{4,3,2,1,0:T(8,128)(2,1)S(1)}, u32[]{:S(2)}, u32[]{:S(2)}) collective-permute-start(bf16[1,2,16,8,128]{4,3,2,1,0:T(8,128)(2,1)S(1)} %copy-done.7), channel_id=1, source_target_pairs={{0,1},{1,0},{2,3},{3,2},{4,5},{5,4},{6,7},{7,6},{8,9},{9,8},{10,11... | collective-permute-start | bytes 196616 | tf_op jit(solution)/shard_map/ppermute | solution.py:239
  12.9 22.3 %collective-permute-start = (bf16[1,2,16,8,128]{4,3,2,1,0:T(8,128)(2,1)S(1)}, bf16[1,2,16,8,128]{4,3,2,1,0:T(8,128)(2,1)S(1)}, u32[]{:S(2)}, u32[]{:S(2)}) collective-permute-start(bf16[1,2,16,8,128]{4,3,2,1,0:T(8,128)(2,1)S(1)} %copy-done.4), channel_id=1, source_target_pairs={{0,1},{1,0},{2,3},{3,2},{4,5},{5,4},{6,7},{7,6},{8,9},{9,8},{10,11... | collective-permute-start | bytes 196616 | tf_op jit(solution)/shard_map/ppermute | solution.py:239
  15.3 15.9 %collective-permute-start.2 = (bf16[16,8,128]{2,1,0:T(8,128)(2,1)S(1)}, bf16[16,8,128]{2,1,0:T(8,128)(2,1)S(1)}, u32[]{:S(2)}, u32[]{:S(2)}) collective-permute-start(bf16[16,8,128]{2,1,0:T(8,128)(2,1)S(1)} %copy-done.16), channel_id=1, source_target_pairs={{1,2},{2,1},{3,4},{4,3},{5,6},{6,5},{7,8},{8,7},{9,10},{10,9},{11,... | collective-permute-start | bytes 98312 | tf_op jit(solution)/shard_map/ppermute | solution.py:239
  27.6 7.6 %collective-permute-start.1 = (bf16[16,8,128]{2,1,0:T(8,128)(2,1)S(1)}, bf16[16,8,128]{2,1,0:T(8,128)(2,1)S(1)}, u32[]{:S(2)}, u32[]{:S(2)}) collective-permute-start(bf16[16,8,128]{2,1,0:T(8,128)(2,1)S(1)} %copy-done.16), channel_id=1, source_target_pairs={{1,3},{2,0},{3,5},{4,2},{5,7},{6,4},{7,9},{8,6},{9,11},{10,8},{11,... | collective-permute-start | bytes 98312 | tf_op jit(solution)/shard_map/ppermute | solution.py:239
  31.3 4.0 %copy-start.12 = (bf16[16,8,128]{2,1,0:T(8,128)(2,1)}, bf16[16,8,128]{2,1,0:T(8,128)(2,1)S(1)}, u32[]{:S(2)}) copy-start(bf16[16,8,128]{2,1,0:T(8,128)(2,1)S(1)} %collective-permute-done.2.near_ref) | copy-start | bytes 98308
  35.9 0.8 copy-start
  41.2 8.0 %copy-start.1 = (bf16[3456,128]{1,0:T(8,128)(2,1)S(1)}, bf16[3456,128]{1,0:T(8,128)(2,1)}, u32[]{:S(2)}) copy-start(bf16[3456,128]{1,0:T(8,128)(2,1)} %get-tuple-element.20.mine_ref) | copy-start | bytes 2654212
  41.2 17.5 %all-to-all-start.1 = ((bf16[12,144,128]{2,1,0:T(8,128)(2,1)}), bf16[12,144,128]{2,1,0:T(8,128)(2,1)S(1)}, u32[]{:S(2)}, u32[]{:S(2)}) async-start(bf16[12,144,128]{2,1,0:T(8,128)(2,1)} %get-tuple-element.27), calls=%async_computation.1 | async-start | bytes 884736 | tf_op jit(solution)/shard_map/all_to_all | solution.py:286
  49.1 60.6 %collective-permute-start.4 = (bf16[3456,128]{1,0:T(8,128)(2,1)S(1)}, bf16[3456,128]{1,0:T(8,128)(2,1)S(1)}, u32[]{:S(2)}, u32[]{:S(2)}) collective-permute-start(bf16[3456,128]{1,0:T(8,128)(2,1)S(1)} %copy-done.1), channel_id=1, source_target_pairs={{0,1},{1,0},{2,3},{3,2},{4,5},{5,4},{6,7},{7,6},{8,9},{9,8},{10,11... | collective-permute-start | bytes 2654216 | tf_op jit(solution)/shard_map/ppermute | solution.py:239
  85.6 8.9 %copy-start.5 = (bf16[768,128]{1,0:T(8,128)(2,1)S(1)}, bf16[768,128]{1,0:T(8,128)(2,1)}, u32[]{:S(2)}) copy-start(bf16[768,128]{1,0:T(8,128)(2,1)} %get-tuple-element.21.own_ref) | copy-start | bytes 589828
  85.6 10.9 %copy-start.15 = (bf16[128,128]{1,0:T(8,128)(2,1)S(1)}, bf16[128,128]{1,0:T(8,128)(2,1)}, u32[]{:S(2)}) copy-start(bf16[128,128]{1,0:T(8,128)(2,1)} %get-tuple-element.22) | copy-start | bytes 98308
  85.6 13.2 %copy-start.14 = (bf16[128,128]{1,0:T(8,128)(2,1)S(1)}, bf16[128,128]{1,0:T(8,128)(2,1)}, u32[]{:S(2)}) copy-start(bf16[128,128]{1,0:T(8,128)(2,1)} %get-tuple-element.23) | copy-start | bytes 98308
  85.6 28.1 %all-to-all-start.4 = ((f32[16,24,128]{2,1,0:T(8,128)}), f32[16,24,128]{2,1,0:T(8,128)S(1)}, u32[]{:S(2)}, u32[]{:S(2)}) async-start(f32[16,24,128]{2,1,0:T(8,128)} %broadcast_in_dim.5), calls=%async_computation.4 | async-start | bytes 393216 | tf_op jit(solution)/shard_map/all_to_all | solution.py:235
  94.4 15.3 %collective-permute-start.5 = (bf16[768,128]{1,0:T(8,128)(2,1)S(1)}, bf16[768,128]{1,0:T(8,128)(2,1)S(1)}, u32[]{:S(2)}, u32[]{:S(2)}) collective-permute-start(bf16[768,128]{1,0:T(8,128)(2,1)S(1)} %copy-done.5), channel_id=1, source_target_pairs={{0,1},{1,0},{2,3},{3,2},{4,5},{5,4},{6,7},{7,6},{8,9},{9,8},{10,11... | collective-permute-start | bytes 589832 | tf_op jit(solution)/shard_map/ppermute | solution.py:239
  96.5 10.4 %collective-permute-start.6 = (bf16[128,128]{1,0:T(8,128)(2,1)S(1)}, bf16[128,128]{1,0:T(8,128)(2,1)S(1)}, u32[]{:S(2)}, u32[]{:S(2)}) collective-permute-start(bf16[128,128]{1,0:T(8,128)(2,1)S(1)} %copy-done.15), channel_id=1, source_target_pairs={{1,2},{2,1},{3,4},{4,3},{5,6},{6,5},{7,8},{8,7},{9,10},{10,9},{11,... | collective-permute-start | bytes 98312 | tf_op jit(solution)/shard_map/ppermute | solution.py:239
  98.8 10.9 %collective-permute-start.7 = (bf16[128,128]{1,0:T(8,128)(2,1)S(1)}, bf16[128,128]{1,0:T(8,128)(2,1)S(1)}, u32[]{:S(2)}, u32[]{:S(2)}) collective-permute-start(bf16[128,128]{1,0:T(8,128)(2,1)S(1)} %copy-done.14), channel_id=1, source_target_pairs={{0,2},{2,4},{3,1},{4,6},{5,3},{6,8},{7,5},{8,10},{9,7},{10,12},{11... | collective-permute-start | bytes 98312 | tf_op jit(solution)/shard_map/ppermute | solution.py:239
  106.8 2.9 %copy-start.10 = (bf16[128,128]{1,0:T(8,128)(2,1)}, bf16[128,128]{1,0:T(8,128)(2,1)S(1)}, u32[]{:S(2)}) copy-start(bf16[128,128]{1,0:T(8,128)(2,1)S(1)} %collective-permute-done.6.near_ref) | copy-start | bytes 98308
  109.8 0.7 copy-start.6
  109.8 1.0 copy-start.2
  113.6 0.7 copy-start.3
  (4 other events, 2.5 us)

commit v3 on v2

v3 whole, which is shorter than its diff:
```python
import functools
import math

import jax
import jax.numpy as jnp
from jax import lax
from jax.experimental import pallas as pl
from jax.experimental.pallas import tpu as pltpu
from jax.sharding import PartitionSpec as P

F32 = jnp.float32
BF16 = jnp.bfloat16
OUTER = 8
MIDDLE = 4
PAIR = 2
HALF = 64
PIECE = 24


def core_is_low():
    return lax.rem(lax.axis_index("spatial"), PAIR) == 0


def lane_of(shape):
    return lax.broadcasted_iota(jnp.int32, shape, len(shape) - 1)


def pick(low, when_low, when_high):
    return jnp.where(low, when_low, when_high)


def pack_body(master_ref, volume_ref, cot_ref, send_ref, edge_ref, slab_ref):
    low = core_is_low()
    rows = master_ref.shape[0] // 2
    top = master_ref[:rows]
    bottom = master_ref[rows:]
    first = pick(low, top, pltpu.roll(top, HALF, 1))
    second = pick(low, pltpu.roll(bottom, HALF, 1), bottom)
    packed = jnp.where(lane_of(top.shape) < HALF, first, second).astype(BF16)
    for owner in range(send_ref.shape[0]):
        send_ref[owner] = packed
    edge_ref[...] = pick(low, volume_ref[0, 0].astype(F32), volume_ref[0, 1].astype(F32)).astype(BF16)
    slab_ref[:2] = volume_ref[0]
    slab_ref[2:] = cot_ref[0]


def shifted(plane, dy, dx):
    _, cols, width = plane.shape
    if dx:
        at = lax.broadcasted_iota(jnp.int32, plane.shape, 1)
        keep = at < cols - 1 if dx > 0 else at > 0
        plane = jnp.where(keep, pltpu.roll(plane, (-dx) % cols, 1), 0.0)
    if dy:
        gap = jnp.zeros((1, cols, width), plane.dtype)
        plane = jnp.concatenate([plane[1:], gap] if dy > 0 else [gap, plane[:-1]], axis=0)
    return plane


def tap_pieces(plane, sign):
    columns = [shifted(plane, 0, sign * (f - 1)) for f in range(3)]
    return [shifted(columns[f], sign * (e - 1), 0) for e in range(3) for f in range(3)]


def forward_body(
    kernel_ref,
    volume_ref,
    cot_ref,
    beside_ref,
    far_ref,
    near_ref,
    act_ref,
    grad_ref,
    first_ref,
    last_ref,
    weight_ref,
    window_ref,
    wide_ref,
    turned_ref,
    stack_ref,
    total_ref,
):
    low = core_is_low()
    owners, rows, width = kernel_ref.shape
    own = [volume_ref[0, i].astype(F32) for i in range(2)]
    beside = [beside_ref[i].astype(F32) for i in range(2)]
    far = far_ref[...].astype(F32)
    near = near_ref[...].astype(F32)
    planes = [pick(low, near, far)]
    planes += [pick(low, own[i], beside[i]) for i in range(2)]
    planes += [pick(low, beside[i], own[i]) for i in range(2)]
    planes += [pick(low, far, near)]
    cells = planes[0].shape[0] * planes[0].shape[1]
    for index, plane in enumerate(planes):
        for tap, piece in enumerate(tap_pieces(plane, 1)):
            window_ref[index * cells : (index + 1) * cells, tap * width : (tap + 1) * width] = (
                piece.reshape(cells, width).astype(BF16)
            )
    mask = (lane_of((rows, width)) < HALF) == low
    group = owners // 3
    for j in range(group):
        base = j * 2 * rows
        ends = []
        for offset in range(3):
            packed = kernel_ref[offset * group + j].astype(F32)
            rolled = pltpu.roll(packed, HALF, 1)
            ends.append((pick(low, packed, rolled), pick(low, rolled, packed)))
        for k in range(2):
            at = slice(base + k * rows, base + (k + 1) * rows)
            wide_ref[at, :width] = jnp.where(mask, ends[0][k], ends[1][1 - k]).astype(BF16)
            wide_ref[at, width:] = jnp.where(mask, ends[2][k], 0.0).astype(BF16)
    count = 4 * cells
    span = 9 * width
    product = jnp.dot(window_ref[...], wide_ref[...], preferred_element_type=F32)
    wide_mask = (lane_of((count, width)) < HALF) == low
    preact = product[:count, :width] + product[2 * cells :, width:]
    preact = preact + pltpu.roll(product[cells : cells + count, :width], HALF, 1)
    preact = jnp.where(wide_mask, preact, 0.0)
    sigma = jax.nn.sigmoid(preact)
    slope = sigma * (1.0 + preact * (1.0 - sigma))
    act_ref[...] = (preact * sigma).astype(BF16)
    cot_own = cot_ref[0].astype(F32).reshape(2 * cells, width)
    cot_beside = beside_ref[2:].astype(F32).reshape(2 * cells, width)
    cotangent = jnp.concatenate(
        [pick(low, cot_own, cot_beside), pick(low, cot_beside, cot_own)], axis=0
    )
    grad = jnp.where(wide_mask, cotangent * slope, 0.0)
    rounded = grad.astype(BF16)
    grad_ref[...] = rounded
    first_ref[...] = rounded[:cells]
    last_ref[...] = rounded[3 * cells :]
    turned_ref[...] = grad.T
    mine = pick(low, turned_ref[:HALF], turned_ref[HALF:]).astype(BF16)
    stack_ref[...] = jnp.zeros_like(stack_ref)
    for offset in range(3):
        stack_ref[offset * HALF : (offset + 1) * HALF, offset * cells : offset * cells + count] = mine
    stacked = jnp.dot(stack_ref[...], window_ref[...], preferred_element_type=F32)
    for offset in range(3):
        total_ref[:, offset * span : (offset + 1) * span] = stacked[offset * HALF : (offset + 1) * HALF]
    lane = lane_of((HALF, width))

    def columns(start):
        tile, offset = divmod(start, width)
        here = total_ref[:, tile * width : (tile + 1) * width]
        if not offset:
            return here
        here = pltpu.roll(here, width - offset, 1)
        if (tile + 1) * width >= total_ref.shape[1]:
            return here
        after = pltpu.roll(total_ref[:, (tile + 1) * width : (tile + 2) * width], width - offset, 1)
        return jnp.where(lane < width - offset, here, after)

    shard = 2 * rows
    rest = shard - 2 * width
    folds = width // rest
    lines = HALF // folds
    for owner in range(owners):
        start = owner * shard
        weight_ref[owner, :HALF] = columns(start).astype(BF16)
        weight_ref[owner, HALF : 2 * HALF] = columns(start + width).astype(BF16)
        tail = columns(start + 2 * width)
        folded = tail[:lines]
        for fold in range(1, folds):
            part = pltpu.roll(tail[fold * lines : (fold + 1) * lines], fold * rest, 1)
            folded = jnp.where(lane[:lines] >= fold * rest, part, folded)
        weight_ref[owner, 2 * HALF :] = folded.astype(BF16)


def backward_body(
    kernel_ref, grad_ref, before_ref, after_ref, act_ref, own_ref, swap_ref, here_ref, there_ref, turn_ref, window_ref
):
    low = core_is_low()
    owners, rows, width = kernel_ref.shape
    cells = before_ref.shape[0]
    count = 4 * cells
    shape = (cells // 8, 8, width)
    mask = (lane_of((rows, width)) < HALF) == low
    for owner in range(owners):
        packed = kernel_ref[owner].astype(F32)
        rolled = pltpu.roll(packed, HALF, 1)
        one, two = pick(low, packed, rolled), pick(low, rolled, packed)
        base = owner * 2 * rows
        for ref, top, bottom, keep in ((here_ref, one, two, mask), (there_ref, two, one, ~mask)):
            ref[base : base + rows] = jnp.where(keep, top, 0.0).astype(BF16)
            ref[base + rows : base + 2 * rows] = jnp.where(keep, bottom, 0.0).astype(BF16)
    for offset in range(3):
        for pair in range(5):
            tap = offset * 9 + 2 * pair
            weight = here_ref[tap * width : (tap + 1) * width]
            if pair < 4:
                weight = weight + there_ref[(tap + 1) * width : (tap + 2) * width]
            turn_ref[offset, :, pair * width : (pair + 1) * width] = weight
    planes = [before_ref[...]] + [grad_ref[i * cells : (i + 1) * cells] for i in range(4)] + [after_ref[...]]
    for index, plane in enumerate(planes):
        pieces = tap_pieces(plane.astype(F32).reshape(shape), -1)
        for pair in range(5):
            piece = pieces[2 * pair].reshape(cells, width)
            if pair < 4:
                piece = piece + pltpu.roll(pieces[2 * pair + 1].reshape(cells, width), HALF, 1)
            window_ref[index * cells : (index + 1) * cells, pair * width : (pair + 1) * width] = piece.astype(
                BF16
            )
    total = jnp.zeros((count, width), F32)
    for offset in range(3):
        total = total + lax.dot_general(
            window_ref[(2 - offset) * cells : (2 - offset) * cells + count],
            turn_ref[offset],
            (((1,), (1,)), ((), ())),
            preferred_element_type=F32,
        )
    half = count // 2
    own_ref[...] = pick(low, total[:half], total[half:])
    swap_ref[:half] = pick(low, total[half:], total[:half])
    act = act_ref[...].astype(F32)
    swap_ref[half:] = pick(low, act[half:], act[:half])


def finish_body(own_ref, act_ref, got_ref, out_act_ref, out_ref):
    low = core_is_low()
    half, _ = own_ref.shape
    shape = out_ref.shape[1:]
    out_ref[0] = (own_ref[...] + got_ref[:half]).reshape(shape).astype(BF16)
    act = act_ref[...].astype(F32)
    mine = pick(low, act[:half], act[half:])
    mask = (lane_of(mine.shape) < HALF) == low
    out_act_ref[0] = jnp.where(mask, mine, got_ref[half:]).reshape(shape).astype(BF16)


def update_body(cells_all, grads_ref, master_ref, moment_ref, second_ref, out_ref, out_m_ref, out_s_ref, grad_ref):
    rows, width = master_ref.shape
    pieces = rows // 2 // PIECE
    halves = []
    for half in range(PAIR):
        halves.append(
            jnp.concatenate([grads_ref[PAIR * i + half] for i in range(pieces)], axis=0)
        )
    rest = rows - 2 * width
    folds = width // rest
    group = HALF // folds
    for part in range(2):
        both = jnp.concatenate([h[part * HALF : (part + 1) * HALF] for h in halves], axis=0)
        grad_ref[part * width : (part + 1) * width] = both.T
    tails = []
    for h in halves:
        tail = h[2 * HALF :]
        for fold in range(folds):
            tails.append(pltpu.roll(tail, width - fold * rest, 1) if fold else tail)
    assert len(tails) * group == width
    grad_ref[2 * width :] = jnp.concatenate(tails, axis=0).T[:rest]
    weight_grad = grad_ref[...] / math.sqrt(cells_all)
    moment_next = 0.9 * moment_ref[...] + 0.1 * weight_grad
    second_next = 0.999 * second_ref[...] + 0.001 * weight_grad * weight_grad
    master = master_ref[...]
    out_ref[...] = master - 0.001 * (moment_next / (jnp.sqrt(second_next) + 1e-08) + 0.01 * master)
    out_m_ref[...] = moment_next
    out_s_ref[...] = second_next


def exchanged(tiles, groups):
    return lax.all_to_all(tiles, "spatial", 0, 0, tiled=True, axis_index_groups=groups)


def moved(value, perm):
    return lax.ppermute(value, "spatial", perm)


def layer(volume, cotangent, master, moment, second):
    _, planes, rows, cols, width = volume.shape
    cells = rows * cols
    owners = lax.axis_size("dp")
    count = lax.axis_size("spatial")
    shard = master.shape[0]
    taps_all = owners * shard
    like = jax.ShapeDtypeStruct

    def inside(pairs):
        return [(i, j) for i, j in pairs if 0 <= j < count]

    swap = [(i, i ^ 1) for i in range(count)]
    near = inside((i, i - 1 if i % 2 == 0 else i + 1) for i in range(count))
    far = inside((i, i - 2 if i % 2 == 0 else i + 2) for i in range(count))
    onward = inside((i, i + 2) for i in range(count))
    backward = inside((i, i - 2) for i in range(count))

    send, edge, slab = pl.pallas_call(
        pack_body,
        out_shape=(
            like((owners, shard // 2, width), BF16),
            like((rows, cols, width), BF16),
            like((4, rows, cols, width), BF16),
        ),
        name="pack",
    )(master, volume, cotangent)
    halves = lax.all_to_all(send, "dp", 0, 0, tiled=True)
    far_plane = moved(edge, far)
    near_plane = moved(edge, near)
    beside = moved(slab, swap)
    cell_half = like((cells, width), BF16)
    cell_all = like((4 * cells, width), BF16)
    act, grad, first, last, weight = pl.pallas_call(
        forward_body,
        out_shape=(cell_all, cell_all, cell_half, cell_half, like((owners, shard // 2, width), BF16)),
        scratch_shapes=[
            pltpu.VMEM((6 * cells, 9 * width), BF16),
            pltpu.VMEM((9 * width, 2 * width), BF16),
            pltpu.VMEM((width, 4 * cells), F32),
            pltpu.VMEM((3 * HALF, 6 * cells), BF16),
            pltpu.VMEM((HALF, taps_all), F32),
        ],
        name="forward",
    )(halves, volume, cotangent, beside, far_plane, near_plane)
    arrived = lax.all_to_all(weight, "dp", 0, 0, tiled=True)
    before = moved(last, onward)
    after = moved(first, backward)
    own, swapped = pl.pallas_call(
        backward_body,
        out_shape=(like((2 * cells, width), F32), like((4 * cells, width), F32)),
        scratch_shapes=[
            pltpu.VMEM((taps_all, width), BF16),
            pltpu.VMEM((taps_all, width), BF16),
            pltpu.VMEM((3, width, 5 * width), BF16),
            pltpu.VMEM((6 * cells, 5 * width), BF16),
        ],
        cost_estimate=pl.CostEstimate(
            flops=2 * 2 * cells * taps_all * width, bytes_accessed=taps_all * width, transcendentals=0
        ),
        name="backward",
    )(halves, grad, before, after, act)
    got = moved(swapped, swap)
    activation, input_grad = pl.pallas_call(
        finish_body, out_shape=(like(volume.shape, BF16), like(volume.shape, BF16)), name="finish"
    )(own, act, got)

    same_y = [
        [(y * MIDDLE + h) * PAIR + c for h in range(MIDDLE)] for y in range(OUTER) for c in range(PAIR)
    ]
    same_rest = [[y * MIDDLE * PAIR + r for y in range(OUTER)] for r in range(MIDDLE * PAIR)]
    same_z = [
        [(y * MIDDLE + h) * PAIR + c for y in range(OUTER) for c in range(PAIR)] for h in range(MIDDLE)
    ]
    pieces = shard // 2 // PIECE
    summed = arrived.astype(F32).sum(axis=0).reshape(pieces, PIECE, width)
    summed = jnp.pad(summed, ((0, OUTER - pieces), (0, 0), (0, 0)))
    piece = exchanged(summed, same_rest)
    piece = piece.sum(0)
    piece = exchanged(jnp.broadcast_to(piece[None], (MIDDLE, PIECE, width)), same_y)
    piece = piece.sum(0)
    joined = exchanged(jnp.broadcast_to(piece[None], (OUTER * PAIR, PIECE, width)), same_z)
    cells_all = owners * count * planes * cells
    state = like(master.shape, F32)
    master_next, moment_next, second_next = pl.pallas_call(
        functools.partial(update_body, cells_all),
        out_shape=(state, state, state),
        scratch_shapes=[pltpu.VMEM(master.shape, F32)],
        name="update",
    )(joined, master, moment, second)
    return (activation, input_grad, master_next, moment_next, second_next)


def solution(mesh):
    return jax.shard_map(
        layer,
        mesh=mesh,
        in_specs=(
            P("dp", "spatial", None, None, None),
            P("dp", "spatial", None, None, None),
            P("dp", None),
            P("dp", None),
            P("dp", None),
        ),
        out_specs=(
            P("dp", "spatial", None, None, None),
            P("dp", "spatial", None, None, None),
            P("dp", None),
            P("dp", None),
            P("dp", None),
        ),
        check_vma=False,
    )
```

time: 117 us -> 120 us (1.026)
  the two profiles are of different devices: /device:TPU:38 before, /device:TPU:33 now
where the time goes in v3:
time: 120 us
  blocking collectives  47.2 us (39%)
  starting transfers between devices  46.9 us (39%)
  Pallas kernels  12.9 us (11%)
  waiting for transfers between devices  7.54 us (6%)
  local copies, waits for them, and re-layouts  4.15 us (3%)
    all_to_all x2, blocking collectives, exchanged(): lax.all_to_all(tiles, 'spatial', 0, 0, tiled=True, axis_index_groups=groups)  29.7 us
    ppermute x6, starting transfers between devices, moved(): return lax.ppermute(value, 'spatial', perm)  27.6 us
    all_to_all x1, blocking collectives, layer(): arrived = lax.all_to_all(weight, 'dp', 0, 0, tiled=True)  17.5 us
    all_to_all x1, starting transfers between devices, exchanged(): lax.all_to_all(tiles, 'spatial', 0, 0, tiled=True, axis_index_groups=groups)  11.5 us
    all_to_all x1, starting transfers between devices, layer(): halves = lax.all_to_all(send, 'dp', 0, 0, tiled=True)  7.8 us
    ppermute x6, waiting for transfers between devices, moved(): return lax.ppermute(value, 'spatial', perm)  7.54 us
    pallas_call x1, Pallas kernels, layer(): pl.pallas_call(forward_body, out_shape=(cell_all, cell_all, cell_half, ce...  4.25 us
    unnamed x24, local copies, waits for them, and re-layouts  3.44 us
  transfers between devices with their start and end apart: 8, of which 4 were waited for; matrix products, arithmetic and copies ran while one was open for 0% of the time, Pallas kernels for 4%

profile of v3, /device:TPU:33, one launch (start us, length us, event | category | flops | bytes accessed | tf_op | source)
XLA Modules:
  0.0 119.6 jit_solution(6961276175329355127)
XLA Ops:
  0.6 1.8 %pack.1 = (bf16[12,144,128]{2,1,0:T(8,128)(2,1)}, bf16[16,8,128]{2,1,0:T(8,128)(2,1)}, bf16[4,16,8,128]{3,2,1,0:T(8,128)(2,1)}) custom-call(f32[288,128]{1,0:T(8,128)} %master_ref.3, bf16[1,2,16,8,128]{4,3,2,1,0:T(8,128)(2,1)} %volume_ref.3, bf16[1,2,16,8,128]{4,3,2,1,0:T(8,128)(2,1)} %cot_ref.3), custom_call_target="tpu_custom_call" | custom-call | tf_op jit(solution)/shard_map/pack/pallas_call | solution.py:284
  2.5 7.8 %all-to-all-start = ((bf16[12,144,128]{2,1,0:T(8,128)(2,1)}), bf16[12,144,128]{2,1,0:T(8,128)(2,1)S(1)}, u32[]{:S(2)}, u32[]{:S(2)}) async-start(bf16[12,144,128]{2,1,0:T(8,128)(2,1)} %get-tuple-element.20), calls=%async_computation | async-start | bytes 884736 | tf_op jit(solution)/shard_map/all_to_all | solution.py:293
  10.3 2.9 %collective-permute-start = (bf16[4,16,8,128]{3,2,1,0:T(8,128)(2,1)S(1)}, bf16[4,16,8,128]{3,2,1,0:T(8,128)(2,1)S(1)}, u32[]{:S(2)}, u32[]{:S(2)}) collective-permute-start(bf16[4,16,8,128]{3,2,1,0:T(8,128)(2,1)S(1)} %copy-done.6), channel_id=1, source_target_pairs={{0,1},{1,0},{2,3},{3,2},{4,5},{5,4},{6,7},{7,6},{8,9},{9,8},{10,11... | collective-permute-start | bytes 393224 | tf_op jit(solution)/shard_map/ppermute | solution.py:263
  13.2 8.8 %collective-permute-start.1 = (bf16[16,8,128]{2,1,0:T(8,128)(2,1)S(1)}, bf16[16,8,128]{2,1,0:T(8,128)(2,1)S(1)}, u32[]{:S(2)}, u32[]{:S(2)}) collective-permute-start(bf16[16,8,128]{2,1,0:T(8,128)(2,1)S(1)} %copy-done.9), channel_id=1, source_target_pairs={{1,3},{2,0},{3,5},{4,2},{5,7},{6,4},{7,9},{8,6},{9,11},{10,8},{11,... | collective-permute-start | bytes 98312 | tf_op jit(solution)/shard_map/ppermute | solution.py:263
  22.0 1.9 %collective-permute-start.2 = (bf16[16,8,128]{2,1,0:T(8,128)(2,1)S(1)}, bf16[16,8,128]{2,1,0:T(8,128)(2,1)S(1)}, u32[]{:S(2)}, u32[]{:S(2)}) collective-permute-start(bf16[16,8,128]{2,1,0:T(8,128)(2,1)S(1)} %copy-done.9), channel_id=1, source_target_pairs={{1,2},{2,1},{3,4},{4,3},{5,6},{6,5},{7,8},{8,7},{9,10},{10,9},{11,... | collective-permute-start | bytes 98312 | tf_op jit(solution)/shard_map/ppermute | solution.py:263
  23.9 3.8 %collective-permute-done.1.far_ref = bf16[16,8,128]{2,1,0:T(8,128)(2,1)S(1)} collective-permute-done((bf16[16,8,128]{2,1,0:T(8,128)(2,1)S(1)}, bf16[16,8,128]{2,1,0:T(8,128)(2,1)S(1)}, u32[]{:S(2)}, u32[]{:S(2)}) %collective-permute-start.1) | collective-permute-done | bytes 32800 | tf_op jit(solution)/shard_map/ppermute | solution.py:263
  27.8 1.4 %collective-permute-done.2.near_ref = bf16[16,8,128]{2,1,0:T(8,128)(2,1)S(1)} collective-permute-done((bf16[16,8,128]{2,1,0:T(8,128)(2,1)S(1)}, bf16[16,8,128]{2,1,0:T(8,128)(2,1)S(1)}, u32[]{:S(2)}, u32[]{:S(2)}) %collective-permute-start.2) | collective-permute-done | bytes 32800 | tf_op jit(solution)/shard_map/ppermute | solution.py:263
  29.8 0.8 copy-done
  30.6 4.3 %forward.1 = (bf16[512,128]{1,0:T(8,128)(2,1)}, bf16[512,128]{1,0:T(8,128)(2,1)}, bf16[128,128]{1,0:T(8,128)(2,1)}, bf16[128,128]{1,0:T(8,128)(2,1)}, bf16[12,144,128]{2,1,0:T(8,128)(2,1)}) custom-call(bf16[12,144,128]{2,1,0:T(8,128)(2,1)} %copy-done, bf16[1,2,16,8,128]{4,3,2,1,0:T(8,128)(2,1)} %volume_ref.3, bf16[1,2,16,8,128]{4,3,2,1,0:T(8,128)(2,1)} %cot_ref.3, ...), custom_call_target="tpu_custom_call" | custom-call | tf_op jit(solution)/shard_map/forward/pallas_call | solution.py:299
  34.8 17.5 %all_to_all.25 = bf16[12,144,128]{2,1,0:T(8,128)(2,1)S(1)} all-to-all(bf16[12,144,128]{2,1,0:T(8,128)(2,1)} %get-tuple-element.31), channel_id=1, replica_groups=mesh['dp'=12,'spatial'=64] {'dp'}, dimensions={0} | all-to-all | bytes 884736 | tf_op jit(solution)/shard_map/all_to_all | solution.py:311
  52.4 8.9 %all_to_all.26 = f32[8,24,128]{2,1,0:T(8,128)S(1)} all-to-all(f32[8,24,128]{2,1,0:T(8,128)S(1)} %pad.4), channel_id=1, replica_groups={{0,8,16,24,32,40,48,56},{1,9,17,25,33,41,49,57},{2,10,18,26,34,42,50,58..., dimensions={0} | all-to-all | bytes 196608 | tf_op jit(solution)/shard_map/all_to_all | solution.py:259
  61.4 20.8 %all_to_all.27 = f32[4,24,128]{2,1,0:T(8,128)S(1)} all-to-all(f32[4,24,128]{2,1,0:T(8,128)S(1)} %broadcast_in_dim.4), channel_id=1, replica_groups={{0,2,4,6},{1,3,5,7},{8,10,12,14},{9,11,13,15},{16,18,20,22},{17,19,21,2..., dimensions={0} | all-to-all | bytes 98304 | tf_op jit(solution)/shard_map/all_to_all | solution.py:259
  82.2 0.7 broadcast_in_dim.5
  82.9 11.5 %all-to-all-start.4 = ((f32[16,24,128]{2,1,0:T(8,128)}), f32[16,24,128]{2,1,0:T(8,128)S(1)}, u32[]{:S(2)}, u32[]{:S(2)}) async-start(f32[16,24,128]{2,1,0:T(8,128)} %broadcast_in_dim.5), calls=%async_computation.4 | async-start | bytes 393216 | tf_op jit(solution)/shard_map/all_to_all | solution.py:259
  94.4 2.2 %collective-permute-start.3 = (bf16[128,128]{1,0:T(8,128)(2,1)S(1)}, bf16[128,128]{1,0:T(8,128)(2,1)S(1)}, u32[]{:S(2)}, u32[]{:S(2)}) collective-permute-start(bf16[128,128]{1,0:T(8,128)(2,1)S(1)} %copy-done.8), channel_id=1, source_target_pairs={{0,2},{1,3},{2,4},{3,5},{4,6},{5,7},{6,8},{7,9},{8,10},{9,11},{10,... | collective-permute-start | bytes 98312 | tf_op jit(solution)/shard_map/ppermute | solution.py:263
  96.6 8.2 %collective-permute-start.4 = (bf16[128,128]{1,0:T(8,128)(2,1)S(1)}, bf16[128,128]{1,0:T(8,128)(2,1)S(1)}, u32[]{:S(2)}, u32[]{:S(2)}) collective-permute-start(bf16[128,128]{1,0:T(8,128)(2,1)S(1)} %copy-done.7), channel_id=1, source_target_pairs={{2,0},{3,1},{4,2},{5,3},{6,4},{7,5},{8,6},{9,7},{10,8},{11,9},{12,... | collective-permute-start | bytes 98312 | tf_op jit(solution)/shard_map/ppermute | solution.py:263
  104.8 1.0 collective-permute-done.4.after_ref
  106.4 2.9 %backward.1 = (f32[256,128]{1,0:T(8,128)}, f32[512,128]{1,0:T(8,128)}) custom-call(bf16[12,144,128]{2,1,0:T(8,128)(2,1)} %copy-done, bf16[512,128]{1,0:T(8,128)(2,1)} %get-tuple-element.23.grad_ref, bf16[128,128]{1,0:T(8,128)(2,1)} %copy-done.10, bf16[128,128]{1,0:T(8,128)(2,1)} %copy-done.11, bf16[512,128]{1,0:T(8,128)(2,1)} %get-tuple-element.26.act_ref), custom_call_target="tpu_custom_call" | custom-call | flops 226492416 | bytes 442368 | tf_op jit(solution)/shard_map/backward/pallas_call | solution.py:314
  109.4 3.6 %collective-permute-start.5 = (f32[512,128]{1,0:T(8,128)}, f32[512,128]{1,0:T(8,128)S(1)}, u32[]{:S(2)}, u32[]{:S(2)}) collective-permute-start(f32[512,128]{1,0:T(8,128)} %get-tuple-element.28), channel_id=1, source_target_pairs={{0,1},{1,0},{2,3},{3,2},{4,5},{5,4},{6,7},{7,6},{8,9},{9,8},{10,11... | collective-permute-start | bytes 786440 | tf_op jit(solution)/shard_map/ppermute | solution.py:263
  113.0 1.4 %collective-permute-done.5.got_ref = f32[512,128]{1,0:T(8,128)S(1)} collective-permute-done((f32[512,128]{1,0:T(8,128)}, f32[512,128]{1,0:T(8,128)S(1)}, u32[]{:S(2)}, u32[]{:S(2)}) %collective-permute-start.5) | collective-permute-done | bytes 262176 | tf_op jit(solution)/shard_map/ppermute | solution.py:263
  114.4 0.7 copy-done.2
  115.1 1.7 %finish.1 = (bf16[1,2,16,8,128]{4,3,2,1,0:T(8,128)(2,1)}, bf16[1,2,16,8,128]{4,3,2,1,0:T(8,128)(2,1)}) custom-call(f32[256,128]{1,0:T(8,128)} %get-tuple-element.27.own_ref, bf16[512,128]{1,0:T(8,128)(2,1)} %get-tuple-element.26.act_ref, f32[512,128]{1,0:T(8,128)} %copy-done.2), custom_call_target="tpu_custom_call" | custom-call | tf_op jit(solution)/shard_map/finish/pallas_call | solution.py:329
  116.8 0.7 copy-done.1
  117.5 2.1 %update.1 = (f32[288,128]{1,0:T(8,128)}, f32[288,128]{1,0:T(8,128)}, f32[288,128]{1,0:T(8,128)}) custom-call(f32[16,24,128]{2,1,0:T(8,128)} %copy-done.1, f32[288,128]{1,0:T(8,128)} %master_ref.3, f32[288,128]{1,0:T(8,128)} %moment_ref.1, f32[288,128]{1,0:T(8,128)} %second_ref.1), custom_call_target="tpu_custom_call" | custom-call | tf_op jit(solution)/shard_map/update/pallas_call | solution.py:350
  (30 shorter events, 1.4 us)
Async XLA Ops:
  2.5 7.8 %copy-start.6 = (bf16[4,16,8,128]{3,2,1,0:T(8,128)(2,1)S(1)}, bf16[4,16,8,128]{3,2,1,0:T(8,128)(2,1)}, u32[]{:S(2)}) copy-start(bf16[4,16,8,128]{3,2,1,0:T(8,128)(2,1)} %get-tuple-element.21) | copy-start | bytes 393220
  2.5 10.7 %copy-start.9 = (bf16[16,8,128]{2,1,0:T(8,128)(2,1)S(1)}, bf16[16,8,128]{2,1,0:T(8,128)(2,1)}, u32[]{:S(2)}) copy-start(bf16[16,8,128]{2,1,0:T(8,128)(2,1)} %get-tuple-element.22) | copy-start | bytes 98308
  2.5 26.7 %all-to-all-start = ((bf16[12,144,128]{2,1,0:T(8,128)(2,1)}), bf16[12,144,128]{2,1,0:T(8,128)(2,1)S(1)}, u32[]{:S(2)}, u32[]{:S(2)}) async-start(bf16[12,144,128]{2,1,0:T(8,128)(2,1)} %get-tuple-element.20), calls=%async_computation | async-start | bytes 884736 | tf_op jit(solution)/shard_map/all_to_all | solution.py:293
  10.3 18.9 %collective-permute-start = (bf16[4,16,8,128]{3,2,1,0:T(8,128)(2,1)S(1)}, bf16[4,16,8,128]{3,2,1,0:T(8,128)(2,1)S(1)}, u32[]{:S(2)}, u32[]{:S(2)}) collective-permute-start(bf16[4,16,8,128]{3,2,1,0:T(8,128)(2,1)S(1)} %copy-done.6), channel_id=1, source_target_pairs={{0,1},{1,0},{2,3},{3,2},{4,5},{5,4},{6,7},{7,6},{8,9},{9,8},{10,11... | collective-permute-start | bytes 393224 | tf_op jit(solution)/shard_map/ppermute | solution.py:263
  13.2 14.6 %collective-permute-start.1 = (bf16[16,8,128]{2,1,0:T(8,128)(2,1)S(1)}, bf16[16,8,128]{2,1,0:T(8,128)(2,1)S(1)}, u32[]{:S(2)}, u32[]{:S(2)}) collective-permute-start(bf16[16,8,128]{2,1,0:T(8,128)(2,1)S(1)} %copy-done.9), channel_id=1, source_target_pairs={{1,3},{2,0},{3,5},{4,2},{5,7},{6,4},{7,9},{8,6},{9,11},{10,8},{11,... | collective-permute-start | bytes 98312 | tf_op jit(solution)/shard_map/ppermute | solution.py:263
  22.0 7.1 %collective-permute-start.2 = (bf16[16,8,128]{2,1,0:T(8,128)(2,1)S(1)}, bf16[16,8,128]{2,1,0:T(8,128)(2,1)S(1)}, u32[]{:S(2)}, u32[]{:S(2)}) collective-permute-start(bf16[16,8,128]{2,1,0:T(8,128)(2,1)S(1)} %copy-done.9), channel_id=1, source_target_pairs={{1,2},{2,1},{3,4},{4,3},{5,6},{6,5},{7,8},{8,7},{9,10},{10,9},{11,... | collective-permute-start | bytes 98312 | tf_op jit(solution)/shard_map/ppermute | solution.py:263
  27.8 1.4 %copy-start.4 = (bf16[16,8,128]{2,1,0:T(8,128)(2,1)}, bf16[16,8,128]{2,1,0:T(8,128)(2,1)S(1)}, u32[]{:S(2)}) copy-start(bf16[16,8,128]{2,1,0:T(8,128)(2,1)S(1)} %collective-permute-done.1.far_ref) | copy-start | bytes 98308
  29.1 0.6 copy-start.5
  29.1 0.7 copy-start.3
  29.8 0.8 copy-start
  82.9 11.5 %copy-start.8 = (bf16[128,128]{1,0:T(8,128)(2,1)S(1)}, bf16[128,128]{1,0:T(8,128)(2,1)}, u32[]{:S(2)}) copy-start(bf16[128,128]{1,0:T(8,128)(2,1)} %get-tuple-element.24) | copy-start | bytes 98308
  82.9 13.7 %copy-start.7 = (bf16[128,128]{1,0:T(8,128)(2,1)S(1)}, bf16[128,128]{1,0:T(8,128)(2,1)}, u32[]{:S(2)}) copy-start(bf16[128,128]{1,0:T(8,128)(2,1)} %get-tuple-element.25) | copy-start | bytes 98308
  82.9 33.9 %all-to-all-start.4 = ((f32[16,24,128]{2,1,0:T(8,128)}), f32[16,24,128]{2,1,0:T(8,128)S(1)}, u32[]{:S(2)}, u32[]{:S(2)}) async-start(f32[16,24,128]{2,1,0:T(8,128)} %broadcast_in_dim.5), calls=%async_computation.4 | async-start | bytes 393216 | tf_op jit(solution)/shard_map/all_to_all | solution.py:259
  94.4 10.4 %collective-permute-start.3 = (bf16[128,128]{1,0:T(8,128)(2,1)S(1)}, bf16[128,128]{1,0:T(8,128)(2,1)S(1)}, u32[]{:S(2)}, u32[]{:S(2)}) collective-permute-start(bf16[128,128]{1,0:T(8,128)(2,1)S(1)} %copy-done.8), channel_id=1, source_target_pairs={{0,2},{1,3},{2,4},{3,5},{4,6},{5,7},{6,8},{7,9},{8,10},{9,11},{10,... | collective-permute-start | bytes 98312 | tf_op jit(solution)/shard_map/ppermute | solution.py:263
  96.6 9.2 %collective-permute-start.4 = (bf16[128,128]{1,0:T(8,128)(2,1)S(1)}, bf16[128,128]{1,0:T(8,128)(2,1)S(1)}, u32[]{:S(2)}, u32[]{:S(2)}) collective-permute-start(bf16[128,128]{1,0:T(8,128)(2,1)S(1)} %copy-done.7), channel_id=1, source_target_pairs={{2,0},{3,1},{4,2},{5,3},{6,4},{7,5},{8,6},{9,7},{10,8},{11,9},{12,... | collective-permute-start | bytes 98312 | tf_op jit(solution)/shard_map/ppermute | solution.py:263
  104.8 1.0 copy-start.10
  105.8 0.6 copy-start.11
  109.4 5.0 %collective-permute-start.5 = (f32[512,128]{1,0:T(8,128)}, f32[512,128]{1,0:T(8,128)S(1)}, u32[]{:S(2)}, u32[]{:S(2)}) collective-permute-start(f32[512,128]{1,0:T(8,128)} %get-tuple-element.28), channel_id=1, source_target_pairs={{0,1},{1,0},{2,3},{3,2},{4,5},{5,4},{6,7},{7,6},{8,9},{9,8},{10,11... | collective-permute-start | bytes 786440 | tf_op jit(solution)/shard_map/ppermute | solution.py:263
  114.3 0.7 copy-start.2
  116.8 0.7 copy-start.1

commit v4 on v3

v4 whole, which is shorter than its diff:
```python
import functools
import math

import jax
import jax.numpy as jnp
from jax import lax
from jax.experimental import pallas as pl
from jax.experimental.pallas import tpu as pltpu
from jax.sharding import PartitionSpec as P

F32 = jnp.float32
BF16 = jnp.bfloat16
OUTER = 8
MIDDLE = 4
PAIR = 2
HALF = 64
PIECE = 24


def core_is_low():
    return lax.rem(lax.axis_index("spatial"), PAIR) == 0


def lane_of(shape):
    return lax.broadcasted_iota(jnp.int32, shape, len(shape) - 1)


def pick(low, when_low, when_high):
    return jnp.where(low, when_low, when_high)


def pack_body(master_ref, volume_ref, cot_ref, send_ref, near_ref, slab_ref):
    low = core_is_low()
    rows = master_ref.shape[0] // 2
    top = master_ref[:rows]
    bottom = master_ref[rows:]
    first = pick(low, top, pltpu.roll(top, HALF, 1))
    second = pick(low, pltpu.roll(bottom, HALF, 1), bottom)
    packed = jnp.where(lane_of(top.shape) < HALF, first, second).astype(BF16)
    for owner in range(send_ref.shape[0]):
        send_ref[owner] = packed
    near_ref[:2] = volume_ref[0]
    near_ref[2] = pick(low, cot_ref[0, 0].astype(F32), cot_ref[0, 1].astype(F32)).astype(BF16)
    slab_ref[:2] = volume_ref[0]
    slab_ref[2:] = cot_ref[0]


def shifted(plane, dy, dx):
    _, cols, width = plane.shape
    if dx:
        at = lax.broadcasted_iota(jnp.int32, plane.shape, 1)
        keep = at < cols - 1 if dx > 0 else at > 0
        plane = jnp.where(keep, pltpu.roll(plane, (-dx) % cols, 1), 0.0)
    if dy:
        gap = jnp.zeros((1, cols, width), plane.dtype)
        plane = jnp.concatenate([plane[1:], gap] if dy > 0 else [gap, plane[:-1]], axis=0)
    return plane


def tap_pieces(plane, sign):
    columns = [shifted(plane, 0, sign * (f - 1)) for f in range(3)]
    return [shifted(columns[f], sign * (e - 1), 0) for e in range(3) for f in range(3)]


def kernel_rows(low, mine, other):
    mine = mine.astype(F32)
    other = other.astype(F32)
    left = pick(low, mine, other)
    right = pick(low, other, mine)
    keep = lane_of(left.shape) < HALF
    first = jnp.where(keep, left, pltpu.roll(right, HALF, 1))
    second = jnp.where(keep, pltpu.roll(left, HALF, 1), right)
    return first.astype(BF16), second.astype(BF16)


def windows_body(volume_ref, cot_ref, beside_ref, near_ref, far_ref, window_ref, all_cot_ref):
    low = core_is_low()
    own = [volume_ref[0, i].astype(F32) for i in range(2)]
    beside = [beside_ref[i].astype(F32) for i in range(2)]
    near = [near_ref[i].astype(F32) for i in range(3)]
    far = [far_ref[i].astype(F32) for i in range(3)]
    planes = [pick(low, near[i], far[i]) for i in range(2)]
    planes += [pick(low, own[i], beside[i]) for i in range(2)]
    planes += [pick(low, beside[i], own[i]) for i in range(2)]
    planes += [pick(low, far[i], near[i]) for i in range(2)]
    cells = planes[0].shape[0] * planes[0].shape[1]
    width = planes[0].shape[2]
    for index, plane in enumerate(planes):
        for tap, piece in enumerate(tap_pieces(plane, 1)):
            window_ref[index * cells : (index + 1) * cells, tap * width : (tap + 1) * width] = (
                piece.reshape(cells, width).astype(BF16)
            )
    cot_own = cot_ref[0].astype(F32).reshape(2 * cells, width)
    cot_beside = beside_ref[2:].astype(F32).reshape(2 * cells, width)
    near_cot = near[2].reshape(cells, width)
    far_cot = far[2].reshape(cells, width)
    parts = [
        pick(low, near_cot, far_cot),
        pick(low, cot_own, cot_beside),
        pick(low, cot_beside, cot_own),
        pick(low, far_cot, near_cot),
    ]
    all_cot_ref[...] = jnp.concatenate(parts, axis=0).astype(BF16)


def forward_body(
    kernel_ref,
    other_ref,
    window_ref,
    cot_ref,
    out_act_ref,
    grad_ref,
    weight_ref,
    wide_ref,
    deep_ref,
    turned_ref,
    stack_ref,
    total_ref,
):
    low = core_is_low()
    owners, rows, width = kernel_ref.shape
    cells = cot_ref.shape[0] // 6
    group = owners // 3
    for owner in range(owners):
        offset, j = divmod(owner, group)
        blocks = kernel_rows(low, kernel_ref[owner], other_ref[owner])
        for k in range(2):
            at = slice((2 * j + k) * rows, (2 * j + k + 1) * rows)
            if offset < 2:
                wide_ref[at, offset * width : (offset + 1) * width] = blocks[k]
            else:
                deep_ref[at] = blocks[k]
    count = 6 * cells
    inner = 4 * cells
    span = 9 * width
    product = jnp.dot(window_ref[: count + cells], wide_ref[...], preferred_element_type=F32)
    preact = jnp.dot(window_ref[2 * cells :], deep_ref[...], preferred_element_type=F32)
    preact = preact + product[:count, :width] + product[cells:, width:]
    sigma = jax.nn.sigmoid(preact)
    slope = sigma * (1.0 + preact * (1.0 - sigma))
    act = preact[cells : cells + inner] * sigma[cells : cells + inner]
    act = pick(low, act[: inner // 2], act[inner // 2 :])
    out_act_ref[0] = act.reshape(out_act_ref.shape[1:]).astype(BF16)
    grad = cot_ref[...].astype(F32) * slope
    grad_ref[...] = pick(low, grad[:inner], grad[2 * cells :]).astype(BF16)
    turned_ref[...] = grad[cells : cells + inner].T
    mine = pick(low, turned_ref[:HALF], turned_ref[HALF:]).astype(BF16)
    stack_ref[...] = jnp.zeros_like(stack_ref)
    for offset in range(3):
        stack_ref[offset * HALF : (offset + 1) * HALF, offset * cells : offset * cells + inner] = mine
    stacked = jnp.dot(stack_ref[...], window_ref[cells : cells + count], preferred_element_type=F32)
    for offset in range(3):
        total_ref[:, offset * span : (offset + 1) * span] = stacked[offset * HALF : (offset + 1) * HALF]
    lane = lane_of((HALF, width))

    def columns(start):
        tile, offset = divmod(start, width)
        here = total_ref[:, tile * width : (tile + 1) * width]
        if not offset:
            return here
        here = pltpu.roll(here, width - offset, 1)
        if (tile + 1) * width >= total_ref.shape[1]:
            return here
        after = pltpu.roll(total_ref[:, (tile + 1) * width : (tile + 2) * width], width - offset, 1)
        return jnp.where(lane < width - offset, here, after)

    shard = 2 * rows
    rest = shard - 2 * width
    folds = width // rest
    lines = HALF // folds
    for owner in range(owners):
        start = owner * shard
        weight_ref[owner, :HALF] = columns(start).astype(BF16)
        weight_ref[owner, HALF : 2 * HALF] = columns(start + width).astype(BF16)
        tail = columns(start + 2 * width)
        folded = tail[:lines]
        for fold in range(1, folds):
            part = pltpu.roll(tail[fold * lines : (fold + 1) * lines], fold * rest, 1)
            folded = jnp.where(lane[:lines] >= fold * rest, part, folded)
        weight_ref[owner, 2 * HALF :] = folded.astype(BF16)


def backward_body(kernel_ref, other_ref, grad_ref, out_ref, window_ref, turn_ref):
    low = core_is_low()
    owners, rows, width = kernel_ref.shape
    shape = out_ref.shape[2:]
    cells = grad_ref.shape[0] // 4
    for owner in range(owners):
        blocks = kernel_rows(low, kernel_ref[owner], other_ref[owner])
        for k in range(2):
            turn_ref[(2 * owner + k) * rows : (2 * owner + k + 1) * rows] = blocks[k]
    for index in range(4):
        plane = grad_ref[index * cells : (index + 1) * cells].astype(F32).reshape(shape)
        for tap, piece in enumerate(tap_pieces(plane, -1)):
            window_ref[index * cells : (index + 1) * cells, tap * width : (tap + 1) * width] = (
                piece.reshape(cells, width).astype(BF16)
            )
    total = jnp.zeros((2 * cells, width), F32)
    for offset in range(3):
        for tap in range(9):
            at = (offset * 9 + tap) * width
            total = total + lax.dot_general(
                window_ref[(2 - offset) * cells : (4 - offset) * cells, tap * width : (tap + 1) * width],
                turn_ref[at : at + width],
                (((1,), (1,)), ((), ())),
                preferred_element_type=F32,
            )
    out_ref[0] = total.reshape(2, *shape).astype(BF16)


def update_body(cells_all, grads_ref, master_ref, moment_ref, second_ref, out_ref, out_m_ref, out_s_ref, grad_ref):
    rows, width = master_ref.shape
    pieces = rows // 2 // PIECE
    halves = []
    for half in range(PAIR):
        halves.append(
            jnp.concatenate([grads_ref[PAIR * i + half] for i in range(pieces)], axis=0)
        )
    rest = rows - 2 * width
    folds = width // rest
    group = HALF // folds
    for part in range(2):
        both = jnp.concatenate([h[part * HALF : (part + 1) * HALF] for h in halves], axis=0)
        grad_ref[part * width : (part + 1) * width] = both.T
    tails = []
    for h in halves:
        tail = h[2 * HALF :]
        for fold in range(folds):
            tails.append(pltpu.roll(tail, width - fold * rest, 1) if fold else tail)
    assert len(tails) * group == width
    grad_ref[2 * width :] = jnp.concatenate(tails, axis=0).T[:rest]
    weight_grad = grad_ref[...] / math.sqrt(cells_all)
    moment_next = 0.9 * moment_ref[...] + 0.1 * weight_grad
    second_next = 0.999 * second_ref[...] + 0.001 * weight_grad * weight_grad
    master = master_ref[...]
    out_ref[...] = master - 0.001 * (moment_next / (jnp.sqrt(second_next) + 1e-08) + 0.01 * master)
    out_m_ref[...] = moment_next
    out_s_ref[...] = second_next


def exchanged(tiles, groups):
    return lax.all_to_all(tiles, "spatial", 0, 0, tiled=True, axis_index_groups=groups)


def moved(value, perm):
    return lax.ppermute(value, "spatial", perm)


def layer(volume, cotangent, master, moment, second):
    _, planes, rows, cols, width = volume.shape
    cells = rows * cols
    owners = lax.axis_size("dp")
    count = lax.axis_size("spatial")
    shard = master.shape[0]
    taps_all = owners * shard
    like = jax.ShapeDtypeStruct

    def inside(pairs):
        return [(i, j) for i, j in pairs if 0 <= j < count]

    swap = [(i, i ^ 1) for i in range(count)]
    outward = inside((i, i - 1 if i % 2 == 0 else i + 1) for i in range(count))

    packed = like((owners, shard // 2, width), BF16)
    send, edge, slab = pl.pallas_call(
        pack_body,
        out_shape=(packed, like((3, rows, cols, width), BF16), like((4, rows, cols, width), BF16)),
        name="pack",
    )(master, volume, cotangent)
    halves = lax.all_to_all(send, "dp", 0, 0, tiled=True)
    near = moved(edge, outward)
    beside = moved(slab, swap)
    far = moved(near, swap)
    window, all_cot = pl.pallas_call(
        windows_body,
        out_shape=(like((8 * cells, 9 * width), BF16), like((6 * cells, width), BF16)),
        name="windows",
    )(volume, cotangent, beside, near, far)
    others = moved(halves, swap)
    activation, grad, weight = pl.pallas_call(
        forward_body,
        out_shape=(like(volume.shape, BF16), like((4 * cells, width), BF16), packed),
        scratch_shapes=[
            pltpu.VMEM((9 * width, 2 * width), BF16),
            pltpu.VMEM((9 * width, width), BF16),
            pltpu.VMEM((width, 4 * cells), F32),
            pltpu.VMEM((3 * HALF, 6 * cells), BF16),
            pltpu.VMEM((HALF, taps_all), F32),
        ],
        name="forward",
    )(halves, others, window, all_cot)
    arrived = lax.all_to_all(weight, "dp", 0, 0, tiled=True)
    input_grad = pl.pallas_call(
        backward_body,
        out_shape=like(volume.shape, BF16),
        scratch_shapes=[
            pltpu.VMEM((4 * cells, 9 * width), BF16),
            pltpu.VMEM((taps_all, width), BF16),
        ],
        cost_estimate=pl.CostEstimate(
            flops=2 * 2 * cells * taps_all * width, bytes_accessed=taps_all * width, transcendentals=0
        ),
        name="backward",
    )(halves, others, grad)

    same_y = [
        [(y * MIDDLE + h) * PAIR + c for h in range(MIDDLE)] for y in range(OUTER) for c in range(PAIR)
    ]
    same_rest = [[y * MIDDLE * PAIR + r for y in range(OUTER)] for r in range(MIDDLE * PAIR)]
    same_z = [
        [(y * MIDDLE + h) * PAIR + c for y in range(OUTER) for c in range(PAIR)] for h in range(MIDDLE)
    ]
    pieces = shard // 2 // PIECE
    summed = arrived.astype(F32).sum(axis=0).reshape(pieces, PIECE, width)
    summed = jnp.pad(summed, ((0, OUTER - pieces), (0, 0), (0, 0)))
    piece = exchanged(summed, same_rest)
    piece = piece.sum(0)
    piece = exchanged(jnp.broadcast_to(piece[None], (MIDDLE, PIECE, width)), same_y)
    piece = piece.sum(0)
    joined = exchanged(jnp.broadcast_to(piece[None], (OUTER * PAIR, PIECE, width)), same_z)
    cells_all = owners * count * planes * cells
    state = like(master.shape, F32)
    master_next, moment_next, second_next = pl.pallas_call(
        functools.partial(update_body, cells_all),
        out_shape=(state, state, state),
        scratch_shapes=[pltpu.VMEM(master.shape, F32)],
        name="update",
    )(joined, master, moment, second)
    return (activation, input_grad, master_next, moment_next, second_next)


def solution(mesh):
    return jax.shard_map(
        layer,
        mesh=mesh,
        in_specs=(
            P("dp", "spatial", None, None, None),
            P("dp", "spatial", None, None, None),
            P("dp", None),
            P("dp", None),
            P("dp", None),
        ),
        out_specs=(
            P("dp", "spatial", None, None, None),
            P("dp", "spatial", None, None, None),
            P("dp", None),
            P("dp", None),
            P("dp", None),
        ),
        check_vma=False,
    )
```

time: 120 us -> 124 us (1.033)
  the two profiles are of different devices: /device:TPU:33 before, /device:TPU:1 now
where the time goes in v4:
time: 124 us
  blocking collectives  66.4 us (54%)
  starting transfers between devices  27.1 us (22%)
  Pallas kernels  15 us (12%)
  waiting for transfers between devices  11.6 us (9%)
  local copies, waits for them, and re-layouts  2.8 us (2%)
    all_to_all x2, blocking collectives, exchanged(): lax.all_to_all(tiles, 'spatial', 0, 0, tiled=True, axis_index_groups=groups)  34.3 us
    ppermute x4, starting transfers between devices, moved(): return lax.ppermute(value, 'spatial', perm)  19.5 us
    all_to_all x1, blocking collectives, layer(): halves = lax.all_to_all(send, 'dp', 0, 0, tiled=True)  17.4 us
    all_to_all x1, blocking collectives, layer(): arrived = lax.all_to_all(weight, 'dp', 0, 0, tiled=True)  14.8 us
    all_to_all x1, waiting for transfers between devices, exchanged(): lax.all_to_all(tiles, 'spatial', 0, 0, tiled=True, axis_index_groups=groups)  7.67 us
    all_to_all x1, starting transfers between devices, exchanged(): lax.all_to_all(tiles, 'spatial', 0, 0, tiled=True, axis_index_groups=groups)  7.62 us
    pallas_call x1, Pallas kernels, layer(): pl.pallas_call(forward_body, out_shape=(like(volume.shape, BF16), like((4...  5.6 us
    ppermute x4, waiting for transfers between devices, moved(): return lax.ppermute(value, 'spatial', perm)  3.92 us
  transfers between devices with their start and end apart: 5, of which 3 were waited for; matrix products, arithmetic and copies ran while one was open for 0% of the time, Pallas kernels for 4%

profile of v4, /device:TPU:1, one launch (start us, length us, event | category | flops | bytes accessed | tf_op | source)
XLA Modules:
  0.0 123.7 jit_solution(7260377611905332996)
XLA Ops:
  0.6 1.8 %pack.1 = (bf16[12,144,128]{2,1,0:T(8,128)(2,1)}, bf16[3,16,8,128]{3,2,1,0:T(8,128)(2,1)}, bf16[4,16,8,128]{3,2,1,0:T(8,128)(2,1)}) custom-call(f32[288,128]{1,0:T(8,128)} %master_ref.3, bf16[1,2,16,8,128]{4,3,2,1,0:T(8,128)(2,1)} %volume_ref.3, bf16[1,2,16,8,128]{4,3,2,1,0:T(8,128)(2,1)} %cot_ref.3), custom_call_target="tpu_custom_call" | custom-call | tf_op jit(solution)/shard_map/pack/pallas_call | solution.py:265
  2.5 17.4 %all_to_all.25.kernel_ref = bf16[12,144,128]{2,1,0:T(8,128)(2,1)S(1)} all-to-all(bf16[12,144,128]{2,1,0:T(8,128)(2,1)} %get-tuple-element.16), channel_id=1, replica_groups=mesh['dp'=12,'spatial'=64] {'dp'}, dimensions={0} | all-to-all | bytes 884736 | tf_op jit(solution)/shard_map/all_to_all | solution.py:270
  19.8 8.5 %collective-permute-start = (bf16[12,144,128]{2,1,0:T(8,128)(2,1)S(1)}, bf16[12,144,128]{2,1,0:T(8,128)(2,1)S(1)}, u32[]{:S(2)}, u32[]{:S(2)}) collective-permute-start(bf16[12,144,128]{2,1,0:T(8,128)(2,1)S(1)} %all_to_all.25.kernel_ref), channel_id=1, source_target_pairs={{0,1},{1,0},{2,3},{3,2},{4,5},{5,4},{6,7},{7,6},{8,9},{9,8},{10,11... | collective-permute-start | bytes 1327112 | tf_op jit(solution)/shard_map/ppermute | solution.py:246
  28.3 7.2 %collective-permute-start.2 = (bf16[3,16,8,128]{3,2,1,0:T(8,128)(2,1)}, bf16[3,16,8,128]{3,2,1,0:T(8,128)(2,1)S(1)}, u32[]{:S(2)}, u32[]{:S(2)}) collective-permute-start(bf16[3,16,8,128]{3,2,1,0:T(8,128)(2,1)} %get-tuple-element.18), channel_id=1, source_target_pairs={{1,2},{2,1},{3,4},{4,3},{5,6},{6,5},{7,8},{8,7},{9,10},{10,9},{11,... | collective-permute-start | bytes 294920 | tf_op jit(solution)/shard_map/ppermute | solution.py:246
  35.5 1.9 %collective-permute-start.1 = (bf16[4,16,8,128]{3,2,1,0:T(8,128)(2,1)}, bf16[4,16,8,128]{3,2,1,0:T(8,128)(2,1)S(1)}, u32[]{:S(2)}, u32[]{:S(2)}) collective-permute-start(bf16[4,16,8,128]{3,2,1,0:T(8,128)(2,1)} %get-tuple-element.17), channel_id=1, source_target_pairs={{0,1},{1,0},{2,3},{3,2},{4,5},{5,4},{6,7},{7,6},{8,9},{9,8},{10,11... | collective-permute-start | bytes 393224 | tf_op jit(solution)/shard_map/ppermute | solution.py:246
  37.4 2.7 %collective-permute-done.2.near_ref = bf16[3,16,8,128]{3,2,1,0:T(8,128)(2,1)S(1)} collective-permute-done((bf16[3,16,8,128]{3,2,1,0:T(8,128)(2,1)}, bf16[3,16,8,128]{3,2,1,0:T(8,128)(2,1)S(1)}, u32[]{:S(2)}, u32[]{:S(2)}) %collective-permute-start.2) | collective-permute-done | bytes 98336 | tf_op jit(solution)/shard_map/ppermute | solution.py:246
  40.1 1.9 %collective-permute-start.3 = (bf16[3,16,8,128]{3,2,1,0:T(8,128)(2,1)S(1)}, bf16[3,16,8,128]{3,2,1,0:T(8,128)(2,1)S(1)}, u32[]{:S(2)}, u32[]{:S(2)}) collective-permute-start(bf16[3,16,8,128]{3,2,1,0:T(8,128)(2,1)S(1)} %collective-permute-done.2.near_ref), channel_id=1, source_target_pairs={{0,1},{1,0},{2,3},{3,2},{4,5},{5,4},{6,7},{7,6},{8,9},{9,8},{10,11... | collective-permute-start | bytes 294920 | tf_op jit(solution)/shard_map/ppermute | solution.py:246
  42.0 0.0 collective-permute-done.1.beside_ref
  42.1 0.0 copy-start.3
  42.1 1.2 %collective-permute-done.3.far_ref = bf16[3,16,8,128]{3,2,1,0:T(8,128)(2,1)S(1)} collective-permute-done((bf16[3,16,8,128]{3,2,1,0:T(8,128)(2,1)S(1)}, bf16[3,16,8,128]{3,2,1,0:T(8,128)(2,1)S(1)}, u32[]{:S(2)}, u32[]{:S(2)}) %collective-permute-start.3) | collective-permute-done | bytes 98336 | tf_op jit(solution)/shard_map/ppermute | solution.py:246
  43.3 0.6 copy-done.5
  44.0 2.8 %windows.1 = (bf16[1024,1152]{1,0:T(8,128)(2,1)}, bf16[768,128]{1,0:T(8,128)(2,1)}) custom-call(bf16[1,2,16,8,128]{4,3,2,1,0:T(8,128)(2,1)} %volume_ref.3, bf16[1,2,16,8,128]{4,3,2,1,0:T(8,128)(2,1)} %cot_ref.3, bf16[4,16,8,128]{3,2,1,0:T(8,128)(2,1)} %copy-done.3, bf16[3,16,8,128]{3,2,1,0:T(8,128)(2,1)} %copy-done.4, bf16[3,16,8,128]{3,2,1,0:T(8,128)(2,1)} %copy-done.5), custom_call_target="tpu_custom_call" | custom-call | tf_op jit(solution)/shard_map/windows/pallas_call | solution.py:274
  46.8 0.8 copy-done.1
  47.6 5.6 %forward.1 = (bf16[1,2,16,8,128]{4,3,2,1,0:T(8,128)(2,1)}, bf16[512,128]{1,0:T(8,128)(2,1)}, bf16[12,144,128]{2,1,0:T(8,128)(2,1)}) custom-call(bf16[12,144,128]{2,1,0:T(8,128)(2,1)} %copy-done, bf16[12,144,128]{2,1,0:T(8,128)(2,1)} %copy-done.1, bf16[1024,1152]{1,0:T(8,128)(2,1)} %get-tuple-element.19.window_ref, bf16[768,128]{1,0:T(8,128)(2,1)} %get-tuple-element.20.cot_ref), custom_call_target="tpu_custom_call" | custom-call | tf_op jit(solution)/shard_map/forward/pallas_call | solution.py:280
  53.2 14.8 %all_to_all.26 = bf16[12,144,128]{2,1,0:T(8,128)(2,1)S(1)} all-to-all(bf16[12,144,128]{2,1,0:T(8,128)(2,1)} %get-tuple-element.23), channel_id=1, replica_groups=mesh['dp'=12,'spatial'=64] {'dp'}, dimensions={0} | all-to-all | bytes 884736 | tf_op jit(solution)/shard_map/all_to_all | solution.py:292
  67.9 0.1 convert_reduce_fusion
  68.0 16.7 %all_to_all.27 = f32[8,24,128]{2,1,0:T(8,128)S(1)} all-to-all(f32[8,24,128]{2,1,0:T(8,128)S(1)} %pad.4), channel_id=1, replica_groups={{0,8,16,24,32,40,48,56},{1,9,17,25,33,41,49,57},{2,10,18,26,34,42,50,58..., dimensions={0} | all-to-all | bytes 196608 | tf_op jit(solution)/shard_map/all_to_all | solution.py:242
  84.7 17.6 %all_to_all.28 = f32[4,24,128]{2,1,0:T(8,128)S(1)} all-to-all(f32[4,24,128]{2,1,0:T(8,128)S(1)} %broadcast_in_dim.4), channel_id=1, replica_groups={{0,2,4,6},{1,3,5,7},{8,10,12,14},{9,11,13,15},{16,18,20,22},{17,19,21,2..., dimensions={0} | all-to-all | bytes 98304 | tf_op jit(solution)/shard_map/all_to_all | solution.py:242
  102.4 0.7 broadcast_in_dim.5
  103.0 7.6 %all-to-all-start.4 = ((f32[16,24,128]{2,1,0:T(8,128)}), f32[16,24,128]{2,1,0:T(8,128)S(1)}, u32[]{:S(2)}, u32[]{:S(2)}) async-start(f32[16,24,128]{2,1,0:T(8,128)} %broadcast_in_dim.5), calls=%async_computation.4 | async-start | bytes 393216 | tf_op jit(solution)/shard_map/all_to_all | solution.py:242
  110.7 2.6 %backward.1 = bf16[1,2,16,8,128]{4,3,2,1,0:T(8,128)(2,1)} custom-call(bf16[12,144,128]{2,1,0:T(8,128)(2,1)} %copy-done, bf16[12,144,128]{2,1,0:T(8,128)(2,1)} %copy-done.1, bf16[512,128]{1,0:T(8,128)(2,1)} %get-tuple-element.22.grad_ref), custom_call_target="tpu_custom_call" | custom-call | flops 226492416 | bytes 442368 | tf_op jit(solution)/shard_map/backward/pallas_call | solution.py:293
  113.3 7.7 %all-to-all-done.4.grads_ref = f32[16,24,128]{2,1,0:T(8,128)S(1)} async-done(((f32[16,24,128]{2,1,0:T(8,128)}), f32[16,24,128]{2,1,0:T(8,128)S(1)}, u32[]{:S(2)}, u32[]{:S(2)}) %all-to-all-start.4) | async-done | bytes 196640 | tf_op jit(solution)/shard_map/all_to_all | solution.py:242
  120.9 0.7 copy-done.2
  121.6 2.1 %update.1 = (f32[288,128]{1,0:T(8,128)}, f32[288,128]{1,0:T(8,128)}, f32[288,128]{1,0:T(8,128)}) custom-call(f32[16,24,128]{2,1,0:T(8,128)} %copy-done.2, f32[288,128]{1,0:T(8,128)} %master_ref.3, f32[288,128]{1,0:T(8,128)} %moment_ref.1, f32[288,128]{1,0:T(8,128)} %second_ref.1), custom_call_target="tpu_custom_call" | custom-call | tf_op jit(solution)/shard_map/update/pallas_call | solution.py:323
  (13 shorter events, 0.0 us)
Async XLA Ops:
  19.8 27.0 %copy-start = (bf16[12,144,128]{2,1,0:T(8,128)(2,1)}, bf16[12,144,128]{2,1,0:T(8,128)(2,1)S(1)}, u32[]{:S(2)}) copy-start(bf16[12,144,128]{2,1,0:T(8,128)(2,1)S(1)} %all_to_all.25.kernel_ref) | copy-start | bytes 1327108
  19.8 27.0 %collective-permute-start = (bf16[12,144,128]{2,1,0:T(8,128)(2,1)S(1)}, bf16[12,144,128]{2,1,0:T(8,128)(2,1)S(1)}, u32[]{:S(2)}, u32[]{:S(2)}) collective-permute-start(bf16[12,144,128]{2,1,0:T(8,128)(2,1)S(1)} %all_to_all.25.kernel_ref), channel_id=1, source_target_pairs={{0,1},{1,0},{2,3},{3,2},{4,5},{5,4},{6,7},{7,6},{8,9},{9,8},{10,11... | collective-permute-start | bytes 1327112 | tf_op jit(solution)/shard_map/ppermute | solution.py:246
  28.3 11.8 %collective-permute-start.2 = (bf16[3,16,8,128]{3,2,1,0:T(8,128)(2,1)}, bf16[3,16,8,128]{3,2,1,0:T(8,128)(2,1)S(1)}, u32[]{:S(2)}, u32[]{:S(2)}) collective-permute-start(bf16[3,16,8,128]{3,2,1,0:T(8,128)(2,1)} %get-tuple-element.18), channel_id=1, source_target_pairs={{1,2},{2,1},{3,4},{4,3},{5,6},{6,5},{7,8},{8,7},{9,10},{10,9},{11,... | collective-permute-start | bytes 294920 | tf_op jit(solution)/shard_map/ppermute | solution.py:246
  35.5 6.5 %collective-permute-start.1 = (bf16[4,16,8,128]{3,2,1,0:T(8,128)(2,1)}, bf16[4,16,8,128]{3,2,1,0:T(8,128)(2,1)S(1)}, u32[]{:S(2)}, u32[]{:S(2)}) collective-permute-start(bf16[4,16,8,128]{3,2,1,0:T(8,128)(2,1)} %get-tuple-element.17), channel_id=1, source_target_pairs={{0,1},{1,0},{2,3},{3,2},{4,5},{5,4},{6,7},{7,6},{8,9},{9,8},{10,11... | collective-permute-start | bytes 393224 | tf_op jit(solution)/shard_map/ppermute | solution.py:246
  40.1 3.2 %copy-start.4 = (bf16[3,16,8,128]{3,2,1,0:T(8,128)(2,1)}, bf16[3,16,8,128]{3,2,1,0:T(8,128)(2,1)S(1)}, u32[]{:S(2)}) copy-start(bf16[3,16,8,128]{3,2,1,0:T(8,128)(2,1)S(1)} %collective-permute-done.2.near_ref) | copy-start | bytes 294916
  40.1 3.2 %collective-permute-start.3 = (bf16[3,16,8,128]{3,2,1,0:T(8,128)(2,1)S(1)}, bf16[3,16,8,128]{3,2,1,0:T(8,128)(2,1)S(1)}, u32[]{:S(2)}, u32[]{:S(2)}) collective-permute-start(bf16[3,16,8,128]{3,2,1,0:T(8,128)(2,1)S(1)} %collective-permute-done.2.near_ref), channel_id=1, source_target_pairs={{0,1},{1,0},{2,3},{3,2},{4,5},{5,4},{6,7},{7,6},{8,9},{9,8},{10,11... | collective-permute-start | bytes 294920 | tf_op jit(solution)/shard_map/ppermute | solution.py:246
  42.1 1.3 %copy-start.3 = (bf16[4,16,8,128]{3,2,1,0:T(8,128)(2,1)}, bf16[4,16,8,128]{3,2,1,0:T(8,128)(2,1)S(1)}, u32[]{:S(2)}) copy-start(bf16[4,16,8,128]{3,2,1,0:T(8,128)(2,1)S(1)} %collective-permute-done.1.beside_ref) | copy-start | bytes 393220
  43.3 0.6 copy-start.5
  46.8 0.8 copy-start.1
  103.0 17.9 %all-to-all-start.4 = ((f32[16,24,128]{2,1,0:T(8,128)}), f32[16,24,128]{2,1,0:T(8,128)S(1)}, u32[]{:S(2)}, u32[]{:S(2)}) async-start(f32[16,24,128]{2,1,0:T(8,128)} %broadcast_in_dim.5), calls=%async_computation.4 | async-start | bytes 393216 | tf_op jit(solution)/shard_map/all_to_all | solution.py:242
  120.9 0.7 copy-start.2

commit v5 on v4

--- a/solution.py
+++ b/solution.py
@@ -73,44 +73,16 @@
     return first.astype(BF16), second.astype(BF16)
 
 
-def windows_body(volume_ref, cot_ref, beside_ref, near_ref, far_ref, window_ref, all_cot_ref):
-    low = core_is_low()
-    own = [volume_ref[0, i].astype(F32) for i in range(2)]
-    beside = [beside_ref[i].astype(F32) for i in range(2)]
-    near = [near_ref[i].astype(F32) for i in range(3)]
-    far = [far_ref[i].astype(F32) for i in range(3)]
-    planes = [pick(low, near[i], far[i]) for i in range(2)]
-    planes += [pick(low, own[i], beside[i]) for i in range(2)]
-    planes += [pick(low, beside[i], own[i]) for i in range(2)]
-    planes += [pick(low, far[i], near[i]) for i in range(2)]
-    cells = planes[0].shape[0] * planes[0].shape[1]
-    width = planes[0].shape[2]
-    for index, plane in enumerate(planes):
-        for tap, piece in enumerate(tap_pieces(plane, 1)):
-            window_ref[index * cells : (index + 1) * cells, tap * width : (tap + 1) * width] = (
-                piece.reshape(cells, width).astype(BF16)
-            )
-    cot_own = cot_ref[0].astype(F32).reshape(2 * cells, width)
-    cot_beside = beside_ref[2:].astype(F32).reshape(2 * cells, width)
-    near_cot = near[2].reshape(cells, width)
-    far_cot = far[2].reshape(cells, width)
-    parts = [
-        pick(low, near_cot, far_cot),
-        pick(low, cot_own, cot_beside),
-        pick(low, cot_beside, cot_own),
-        pick(low, far_cot, near_cot),
-    ]
-    all_cot_ref[...] = jnp.concatenate(parts, axis=0).astype(BF16)
-
-
 def forward_body(
     kernel_ref,
-    other_ref,
-    window_ref,
+    got_ref,
+    volume_ref,
     cot_ref,
+    near_ref,
     out_act_ref,
     grad_ref,
     weight_ref,
+    window_ref,
     wide_ref,
     deep_ref,
     turned_ref,
@@ -119,11 +91,36 @@
 ):
     low = core_is_low()
     owners, rows, width = kernel_ref.shape
-    cells = cot_ref.shape[0] // 6
+    shape = volume_ref.shape[2:]
+    cells = shape[0] * shape[1]
+    halves = owners * rows
+
+    def handed(index):
+        return got_ref[halves + index * cells : halves + (index + 1) * cells].astype(F32).reshape(shape)
+
+    own = [volume_ref[0, i].astype(F32) for i in range(2)]
+    near = [near_ref[i].astype(F32) for i in range(3)]
+    far = [handed(i) for i in range(3)]
+    beside = [handed(3 + i) for i in range(4)]
+    planes = [pick(low, near[i], far[i]) for i in range(2)]
+    planes += [pick(low, own[i], beside[i]) for i in range(2)]
+    planes += [pick(low, beside[i], own[i]) for i in range(2)]
+    planes += [pick(low, far[i], near[i]) for i in range(2)]
+    for index, plane in enumerate(planes):
+        for tap, piece in enumerate(tap_pieces(plane, 1)):
+            window_ref[index * cells : (index + 1) * cells, tap * width : (tap + 1) * width] = (
+                piece.reshape(cells, width).astype(BF16)
+            )
+    cot_own = [cot_ref[0, i].astype(F32) for i in range(2)]
+    cots = [pick(low, near[2], far[2])]
+    cots += [pick(low, cot_own[i], beside[2 + i]) for i in range(2)]
+    cots += [pick(low, beside[2 + i], cot_own[i]) for i in range(2)]
+    cots += [pick(low, far[2], near[2])]
+    cotangent = jnp.concatenate([c.reshape(cells, width) for c in cots], axis=0)
     group = owners // 3
     for owner in range(owners):
         offset, j = divmod(owner, group)
-        blocks = kernel_rows(low, kernel_ref[owner], other_ref[owner])
+        blocks = kernel_rows(low, kernel_ref[owner], got_ref[owner * rows : (owner + 1) * rows])
         for k in range(2):
             at = slice((2 * j + k) * rows, (2 * j + k + 1) * rows)
             if offset < 2:
@@ -141,7 +138,7 @@
     act = preact[cells : cells + inner] * sigma[cells : cells + inner]
     act = pick(low, act[: inner // 2], act[inner // 2 :])
     out_act_ref[0] = act.reshape(out_act_ref.shape[1:]).astype(BF16)
-    grad = cot_ref[...].astype(F32) * slope
+    grad = cotangent * slope
     grad_ref[...] = pick(low, grad[:inner], grad[2 * cells :]).astype(BF16)
     turned_ref[...] = grad[cells : cells + inner].T
     mine = pick(low, turned_ref[:HALF], turned_ref[HALF:]).astype(BF16)
@@ -180,13 +177,13 @@
         weight_ref[owner, 2 * HALF :] = folded.astype(BF16)
 
 
-def backward_body(kernel_ref, other_ref, grad_ref, out_ref, window_ref, turn_ref):
+def backward_body(kernel_ref, got_ref, grad_ref, out_ref, window_ref, turn_ref):
     low = core_is_low()
     owners, rows, width = kernel_ref.shape
     shape = out_ref.shape[2:]
     cells = grad_ref.shape[0] // 4
     for owner in range(owners):
-        blocks = kernel_rows(low, kernel_ref[owner], other_ref[owner])
+        blocks = kernel_rows(low, kernel_ref[owner], got_ref[owner * rows : (owner + 1) * rows])
         for k in range(2):
             turn_ref[(2 * owner + k) * rows : (2 * owner + k + 1) * rows] = blocks[k]
     for index in range(4):
@@ -266,21 +263,17 @@
         pack_body,
         out_shape=(packed, like((3, rows, cols, width), BF16), like((4, rows, cols, width), BF16)),
         name="pack",
+        compiler_params=pltpu.CompilerParams(vmem_limit_bytes=8 << 20),
     )(master, volume, cotangent)
     halves = lax.all_to_all(send, "dp", 0, 0, tiled=True)
     near = moved(edge, outward)
-    beside = moved(slab, swap)
-    far = moved(near, swap)
-    window, all_cot = pl.pallas_call(
-        windows_body,
-        out_shape=(like((8 * cells, 9 * width), BF16), like((6 * cells, width), BF16)),
-        name="windows",
-    )(volume, cotangent, beside, near, far)
-    others = moved(halves, swap)
+    whole = jnp.concatenate([v.reshape(-1, width) for v in (halves, near, slab)], axis=0)
+    got = moved(whole, swap)
     activation, grad, weight = pl.pallas_call(
         forward_body,
         out_shape=(like(volume.shape, BF16), like((4 * cells, width), BF16), packed),
         scratch_shapes=[
+            pltpu.VMEM((8 * cells, 9 * width), BF16),
             pltpu.VMEM((9 * width, 2 * width), BF16),
             pltpu.VMEM((9 * width, width), BF16),
             pltpu.VMEM((width, 4 * cells), F32),
@@ -288,7 +281,8 @@
             pltpu.VMEM((HALF, taps_all), F32),
         ],
         name="forward",
-    )(halves, others, window, all_cot)
+        compiler_params=pltpu.CompilerParams(vmem_limit_bytes=28 << 20),
+    )(halves, got, volume, cotangent, near)
     arrived = lax.all_to_all(weight, "dp", 0, 0, tiled=True)
     input_grad = pl.pallas_call(
         backward_body,
@@ -301,7 +295,8 @@
             flops=2 * 2 * cells * taps_all * width, bytes_accessed=taps_all * width, transcendentals=0
         ),
         name="backward",
-    )(halves, others, grad)
+    compiler_params=pltpu.CompilerParams(vmem_limit_bytes=20 << 20),
+    )(halves, got, grad)
 
     same_y = [
         [(y * MIDDLE + h) * PAIR + c for h in range(MIDDLE)] for y in range(OUTER) for c in range(PAIR)
@@ -325,6 +320,7 @@
         out_shape=(state, state, state),
         scratch_shapes=[pltpu.VMEM(master.shape, F32)],
         name="update",
+        compiler_params=pltpu.CompilerParams(vmem_limit_bytes=8 << 20),
     )(joined, master, moment, second)
     return (activation, input_grad, master_next, moment_next, second_next)
 

time: 124 us -> 109 us (0.88)
  blocking collectives: 66.4 us -> 54.2 us
  Pallas kernels: 15 us -> 6.85 us
  starting transfers between devices: 27.1 us -> 29.7 us
  waiting for transfers between devices: 11.6 us -> 13.1 us
    all_to_all x1 -> x0, blocking collectives: 17.4 us -> none  [layer(): halves = lax.all_to_all(send, 'dp', 0, 0, tiled=True)]
    all_to_all x0 -> x1, starting transfers between devices: none -> 8.49 us  [layer(): halves = lax.all_to_all(send, 'dp', 0, 0, tiled=True)]
    all_to_all x1, blocking collectives: 14.8 us -> 21.9 us  [layer(): arrived = lax.all_to_all(weight, 'dp', 0, 0, tiled=True)]
    ppermute x4 -> x2, starting transfers between devices: 19.5 us -> 13.4 us  [moved(): return lax.ppermute(value, 'spatial', perm)]
    pallas_call x1 -> x0, Pallas kernels: 2.84 us -> none  [layer(): pl.pallas_call(windows_body, out_shape=(like((8 * cells, 9 * width), BF16...]
    pallas_call x1, Pallas kernels: 5.6 us -> 3.59 us  [layer(): pl.pallas_call(forward_body, out_shape=(like(volume.shape, BF16), like((4...]
    all_to_all x2, blocking collectives: 34.3 us -> 32.4 us  [exchanged(): lax.all_to_all(tiles, 'spatial', 0, 0, tiled=True, axis_index_groups=groups)]
    unnamed x12 -> x16, local copies, waits for them, and re-layouts: 2.1 us -> 2.61 us
  transfers between devices with their start and end apart: 5 -> 4, of which waited for: 3 -> 3; matrix products, arithmetic and copies ran while one was open for 0% -> 0% of each run, Pallas kernels for 4% -> 1%
where the time goes in v5:
time: 109 us; the launch traced here: 108 us
  blocking collectives  54.2 us (50%)
  starting transfers between devices  29.7 us (27%)
  waiting for transfers between devices  13.1 us (12%)
  Pallas kernels  6.85 us (6%)
  local copies, waits for them, and re-layouts  3.31 us (3%)
    all_to_all x2, blocking collectives, exchanged(): lax.all_to_all(tiles, 'spatial', 0, 0, tiled=True, axis_index_groups=groups)  32.4 us
    all_to_all x1, blocking collectives, layer(): arrived = lax.all_to_all(weight, 'dp', 0, 0, tiled=True)  21.9 us
    ppermute x2, starting transfers between devices, moved(): return lax.ppermute(value, 'spatial', perm)  13.4 us
    all_to_all x1, waiting for transfers between devices, exchanged(): lax.all_to_all(tiles, 'spatial', 0, 0, tiled=True, axis_index_groups=groups)  8.79 us
    all_to_all x1, starting transfers between devices, layer(): halves = lax.all_to_all(send, 'dp', 0, 0, tiled=True)  8.49 us
    all_to_all x1, starting transfers between devices, exchanged(): lax.all_to_all(tiles, 'spatial', 0, 0, tiled=True, axis_index_groups=groups)  7.81 us
    ppermute x2, waiting for transfers between devices, moved(): return lax.ppermute(value, 'spatial', perm)  4.35 us
    pallas_call x1, Pallas kernels, layer(): pl.pallas_call(forward_body, out_shape=(like(volume.shape, BF16), like((4...  3.59 us
  transfers between devices with their start and end apart: 4, of which 3 were waited for; matrix products, arithmetic and copies ran while one was open for 0% of the time, Pallas kernels for 1%

profile of v5, /device:TPU:1, one launch (start us, length us, event | category | flops | bytes accessed | tf_op | source)
XLA Modules:
  0.0 108.1 jit_solution(1371517895001525563)
XLA Ops:
  0.6 0.0 copy-start
  0.6 0.9 copy-done
  1.5 0.8 copy-done.2
  2.4 0.8 copy-done.4
  3.2 0.9 pack.1
  4.1 8.5 %all-to-all-start = ((bf16[12,144,128]{2,1,0:T(8,128)(2,1)}), bf16[12,144,128]{2,1,0:T(8,128)(2,1)S(1)}, u32[]{:S(2)}, u32[]{:S(2)}) async-start(bf16[12,144,128]{2,1,0:T(8,128)(2,1)} %get-tuple-element.14), calls=%async_computation | async-start | bytes 884736 | tf_op jit(solution)/shard_map/all_to_all | solution.py:268
  12.6 9.7 %collective-permute-start = (bf16[3,16,8,128]{3,2,1,0:T(8,128)(2,1)S(1)}, bf16[3,16,8,128]{3,2,1,0:T(8,128)(2,1)S(1)}, u32[]{:S(2)}, u32[]{:S(2)}) collective-permute-start(bf16[3,16,8,128]{3,2,1,0:T(8,128)(2,1)S(1)} %get-tuple-element.15), channel_id=1, source_target_pairs={{1,2},{2,1},{3,4},{4,3},{5,6},{6,5},{7,8},{8,7},{9,10},{10,9},{11,... | collective-permute-start | bytes 294920 | tf_op jit(solution)/shard_map/ppermute | solution.py:243
  22.3 2.6 %collective-permute-done.near_ref = bf16[3,16,8,128]{3,2,1,0:T(8,128)(2,1)S(1)} collective-permute-done((bf16[3,16,8,128]{3,2,1,0:T(8,128)(2,1)S(1)}, bf16[3,16,8,128]{3,2,1,0:T(8,128)(2,1)S(1)}, u32[]{:S(2)}, u32[]{:S(2)}) %collective-permute-start) | collective-permute-done | bytes 98336 | tf_op jit(solution)/shard_map/ppermute | solution.py:243
  24.9 0.0 all-to-all-done.kernel_ref
  24.9 3.7 %collective-permute-start.1 = (bf16[2624,128]{1,0:T(8,128)(2,1)S(1)}, bf16[2624,128]{1,0:T(8,128)(2,1)S(1)}, u32[]{:S(2)}, u32[]{:S(2)}) collective-permute-start(bf16[2624,128]{1,0:T(8,128)(2,1)S(1)} %pad_maximum_fusion), channel_id=1, source_target_pairs={{0,1},{1,0},{2,3},{3,2},{4,5},{5,4},{6,7},{7,6},{8,9},{9,8},{10,11... | collective-permute-start | bytes 2015240 | tf_op jit(solution)/shard_map/ppermute | solution.py:243
  28.7 1.7 %collective-permute-done.1.got_ref = bf16[2624,128]{1,0:T(8,128)(2,1)S(1)} collective-permute-done((bf16[2624,128]{1,0:T(8,128)(2,1)S(1)}, bf16[2624,128]{1,0:T(8,128)(2,1)S(1)}, u32[]{:S(2)}, u32[]{:S(2)}) %collective-permute-start.1) | collective-permute-done | bytes 671776 | tf_op jit(solution)/shard_map/ppermute | solution.py:243
  30.4 3.6 %forward.1 = (bf16[1,2,16,8,128]{4,3,2,1,0:T(8,128)(2,1)}, bf16[512,128]{1,0:T(8,128)(2,1)S(1)}, bf16[12,144,128]{2,1,0:T(8,128)(2,1)S(1)}) custom-call(bf16[12,144,128]{2,1,0:T(8,128)(2,1)S(1)} %all-to-all-done.kernel_ref, bf16[2624,128]{1,0:T(8,128)(2,1)S(1)} %collective-permute-done.1.got_ref, bf16[1,2,16,8,128]{4,3,2,1,0:T(8,128)(2,1)S(1)} %copy-done.3, ...), custom_call_target="tpu_custom_call" | custom-call | tf_op jit(solution)/shard_map/forward/pallas_call | solution.py:272
  34.0 21.9 %all_to_all.25 = bf16[12,144,128]{2,1,0:T(8,128)(2,1)S(1)} all-to-all(bf16[12,144,128]{2,1,0:T(8,128)(2,1)S(1)} %get-tuple-element.19), channel_id=1, replica_groups=mesh['dp'=12,'spatial'=64] {'dp'}, dimensions={0} | all-to-all | bytes 884736 | tf_op jit(solution)/shard_map/all_to_all | solution.py:286
  55.9 0.1 convert_reduce_fusion
  56.0 15.3 %all_to_all.26 = f32[8,24,128]{2,1,0:T(8,128)S(1)} all-to-all(f32[8,24,128]{2,1,0:T(8,128)S(1)} %pad.4), channel_id=1, replica_groups={{0,8,16,24,32,40,48,56},{1,9,17,25,33,41,49,57},{2,10,18,26,34,42,50,58..., dimensions={0} | all-to-all | bytes 196608 | tf_op jit(solution)/shard_map/all_to_all | solution.py:239
  71.3 17.0 %all_to_all.27 = f32[4,24,128]{2,1,0:T(8,128)S(1)} all-to-all(f32[4,24,128]{2,1,0:T(8,128)S(1)} %broadcast_in_dim.4), channel_id=1, replica_groups={{0,2,4,6},{1,3,5,7},{8,10,12,14},{9,11,13,15},{16,18,20,22},{17,19,21,2..., dimensions={0} | all-to-all | bytes 98304 | tf_op jit(solution)/shard_map/all_to_all | solution.py:239
  88.4 0.7 broadcast_in_dim.5
  89.0 7.8 %all-to-all-start.4 = ((f32[16,24,128]{2,1,0:T(8,128)}), f32[16,24,128]{2,1,0:T(8,128)S(1)}, u32[]{:S(2)}, u32[]{:S(2)}) async-start(f32[16,24,128]{2,1,0:T(8,128)} %broadcast_in_dim.5), calls=%async_computation.4 | async-start | bytes 393216 | tf_op jit(solution)/shard_map/all_to_all | solution.py:239
  96.9 0.0 copy-start.6
  96.9 0.0 copy-start.7
  96.9 1.4 %backward.1 = bf16[1,2,16,8,128]{4,3,2,1,0:T(8,128)(2,1)} custom-call(bf16[12,144,128]{2,1,0:T(8,128)(2,1)S(1)} %all-to-all-done.kernel_ref, bf16[2624,128]{1,0:T(8,128)(2,1)S(1)} %collective-permute-done.1.got_ref, bf16[512,128]{1,0:T(8,128)(2,1)S(1)} %get-tuple-element.18.grad_ref), custom_call_target="tpu_custom_call" | custom-call | flops 226492416 | bytes 442368 | tf_op jit(solution)/shard_map/backward/pallas_call | solution.py:287
  98.3 8.8 %all-to-all-done.4.grads_ref = f32[16,24,128]{2,1,0:T(8,128)S(1)} async-done(((f32[16,24,128]{2,1,0:T(8,128)}), f32[16,24,128]{2,1,0:T(8,128)S(1)}, u32[]{:S(2)}, u32[]{:S(2)}) %all-to-all-start.4) | async-done | bytes 196640 | tf_op jit(solution)/shard_map/all_to_all | solution.py:239
  107.1 0.0 copy-done.1
  107.1 1.0 update.1
  (14 shorter events, 0.1 us)
Async XLA Ops:
  0.6 0.9 copy-start
  1.5 0.8 copy-start.2
  2.4 0.8 copy-start.4
  4.1 20.8 %all-to-all-start = ((bf16[12,144,128]{2,1,0:T(8,128)(2,1)}), bf16[12,144,128]{2,1,0:T(8,128)(2,1)S(1)}, u32[]{:S(2)}, u32[]{:S(2)}) async-start(bf16[12,144,128]{2,1,0:T(8,128)(2,1)} %get-tuple-element.14), calls=%async_computation | async-start | bytes 884736 | tf_op jit(solution)/shard_map/all_to_all | solution.py:268
  12.6 12.3 %collective-permute-start = (bf16[3,16,8,128]{3,2,1,0:T(8,128)(2,1)S(1)}, bf16[3,16,8,128]{3,2,1,0:T(8,128)(2,1)S(1)}, u32[]{:S(2)}, u32[]{:S(2)}) collective-permute-start(bf16[3,16,8,128]{3,2,1,0:T(8,128)(2,1)S(1)} %get-tuple-element.15), channel_id=1, source_target_pairs={{1,2},{2,1},{3,4},{4,3},{5,6},{6,5},{7,8},{8,7},{9,10},{10,9},{11,... | collective-permute-start | bytes 294920 | tf_op jit(solution)/shard_map/ppermute | solution.py:243
  24.9 5.5 %copy-start.3 = (bf16[1,2,16,8,128]{4,3,2,1,0:T(8,128)(2,1)S(1)}, bf16[1,2,16,8,128]{4,3,2,1,0:T(8,128)(2,1)}, u32[]{:S(2)}) copy-start(bf16[1,2,16,8,128]{4,3,2,1,0:T(8,128)(2,1)} %volume_ref.3) | copy-start | bytes 196612
  24.9 5.5 %copy-start.5 = (bf16[1,2,16,8,128]{4,3,2,1,0:T(8,128)(2,1)S(1)}, bf16[1,2,16,8,128]{4,3,2,1,0:T(8,128)(2,1)}, u32[]{:S(2)}) copy-start(bf16[1,2,16,8,128]{4,3,2,1,0:T(8,128)(2,1)} %cot_ref.3) | copy-start | bytes 196612
  24.9 5.5 %collective-permute-start.1 = (bf16[2624,128]{1,0:T(8,128)(2,1)S(1)}, bf16[2624,128]{1,0:T(8,128)(2,1)S(1)}, u32[]{:S(2)}, u32[]{:S(2)}) collective-permute-start(bf16[2624,128]{1,0:T(8,128)(2,1)S(1)} %pad_maximum_fusion), channel_id=1, source_target_pairs={{0,1},{1,0},{2,3},{3,2},{4,5},{5,4},{6,7},{7,6},{8,9},{9,8},{10,11... | collective-permute-start | bytes 2015240 | tf_op jit(solution)/shard_map/ppermute | solution.py:243
  89.0 18.1 %all-to-all-start.4 = ((f32[16,24,128]{2,1,0:T(8,128)}), f32[16,24,128]{2,1,0:T(8,128)S(1)}, u32[]{:S(2)}, u32[]{:S(2)}) async-start(f32[16,24,128]{2,1,0:T(8,128)} %broadcast_in_dim.5), calls=%async_computation.4 | async-start | bytes 393216 | tf_op jit(solution)/shard_map/all_to_all | solution.py:239
  96.9 10.3 %copy-start.1 = (f32[288,128]{1,0:T(8,128)S(1)}, f32[288,128]{1,0:T(8,128)}, u32[]{:S(2)}) copy-start(f32[288,128]{1,0:T(8,128)} %master_ref.3) | copy-start | bytes 442372
  96.9 10.3 %copy-start.6 = (f32[288,128]{1,0:T(8,128)S(1)}, f32[288,128]{1,0:T(8,128)}, u32[]{:S(2)}) copy-start(f32[288,128]{1,0:T(8,128)} %moment_ref.1) | copy-start | bytes 442372
  96.9 10.3 %copy-start.7 = (f32[288,128]{1,0:T(8,128)S(1)}, f32[288,128]{1,0:T(8,128)}, u32[]{:S(2)}) copy-start(f32[288,128]{1,0:T(8,128)} %second_ref.1) | copy-start | bytes 442372

commit v6 on v5

--- a/solution.py
+++ b/solution.py
@@ -29,7 +29,7 @@
     return jnp.where(low, when_low, when_high)
 
 
-def pack_body(master_ref, volume_ref, cot_ref, send_ref, near_ref, slab_ref):
+def pack_body(master_ref, send_ref):
     low = core_is_low()
     rows = master_ref.shape[0] // 2
     top = master_ref[:rows]
@@ -39,6 +39,10 @@
     packed = jnp.where(lane_of(top.shape) < HALF, first, second).astype(BF16)
     for owner in range(send_ref.shape[0]):
         send_ref[owner] = packed
+
+
+def edges_body(volume_ref, cot_ref, near_ref, slab_ref):
+    low = core_is_low()
     near_ref[:2] = volume_ref[0]
     near_ref[2] = pick(low, cot_ref[0, 0].astype(F32), cot_ref[0, 1].astype(F32)).astype(BF16)
     slab_ref[:2] = volume_ref[0]
@@ -102,20 +106,16 @@
     near = [near_ref[i].astype(F32) for i in range(3)]
     far = [handed(i) for i in range(3)]
     beside = [handed(3 + i) for i in range(4)]
-    planes = [pick(low, near[i], far[i]) for i in range(2)]
-    planes += [pick(low, own[i], beside[i]) for i in range(2)]
-    planes += [pick(low, beside[i], own[i]) for i in range(2)]
-    planes += [pick(low, far[i], near[i]) for i in range(2)]
+    low_planes = [*near[:2], *own, *beside[:2], far[0]]
+    high_planes = [far[1], *beside[:2], *own, *near[:2]]
+    planes = [pick(low, x, y) for x, y in zip(low_planes, high_planes)]
     for index, plane in enumerate(planes):
         for tap, piece in enumerate(tap_pieces(plane, 1)):
             window_ref[index * cells : (index + 1) * cells, tap * width : (tap + 1) * width] = (
                 piece.reshape(cells, width).astype(BF16)
             )
     cot_own = [cot_ref[0, i].astype(F32) for i in range(2)]
-    cots = [pick(low, near[2], far[2])]
-    cots += [pick(low, cot_own[i], beside[2 + i]) for i in range(2)]
-    cots += [pick(low, beside[2 + i], cot_own[i]) for i in range(2)]
-    cots += [pick(low, far[2], near[2])]
+    cots = [pick(low, x, y) for x, y in zip([near[2], *cot_own, *beside[2:]], [*beside[2:], *cot_own, near[2]])]
     cotangent = jnp.concatenate([c.reshape(cells, width) for c in cots], axis=0)
     group = owners // 3
     for owner in range(owners):
@@ -127,7 +127,7 @@
                 wide_ref[at, offset * width : (offset + 1) * width] = blocks[k]
             else:
                 deep_ref[at] = blocks[k]
-    count = 6 * cells
+    count = 5 * cells
     inner = 4 * cells
     span = 9 * width
     product = jnp.dot(window_ref[: count + cells], wide_ref[...], preferred_element_type=F32)
@@ -135,17 +135,18 @@
     preact = preact + product[:count, :width] + product[cells:, width:]
     sigma = jax.nn.sigmoid(preact)
     slope = sigma * (1.0 + preact * (1.0 - sigma))
-    act = preact[cells : cells + inner] * sigma[cells : cells + inner]
-    act = pick(low, act[: inner // 2], act[inner // 2 :])
+    act = (preact * sigma)[cells : 4 * cells]
+    act = pick(low, act[: inner // 2], act[cells:])
     out_act_ref[0] = act.reshape(out_act_ref.shape[1:]).astype(BF16)
     grad = cotangent * slope
-    grad_ref[...] = pick(low, grad[:inner], grad[2 * cells :]).astype(BF16)
-    turned_ref[...] = grad[cells : cells + inner].T
+    grad_ref[...] = pick(low, grad[:inner], grad[cells:]).astype(BF16)
+    turned_ref[...] = pick(low, grad[cells:], grad[:inner]).T
     mine = pick(low, turned_ref[:HALF], turned_ref[HALF:]).astype(BF16)
     stack_ref[...] = jnp.zeros_like(stack_ref)
     for offset in range(3):
         stack_ref[offset * HALF : (offset + 1) * HALF, offset * cells : offset * cells + inner] = mine
-    stacked = jnp.dot(stack_ref[...], window_ref[cells : cells + count], preferred_element_type=F32)
+    at = pl.multiple_of(jnp.where(low, cells, 0), cells)
+    stacked = jnp.dot(stack_ref[...], window_ref[pl.ds(at, 6 * cells)], preferred_element_type=F32)
     for offset in range(3):
         total_ref[:, offset * span : (offset + 1) * span] = stacked[offset * HALF : (offset + 1) * HALF]
     lane = lane_of((HALF, width))
@@ -259,13 +260,19 @@
     outward = inside((i, i - 1 if i % 2 == 0 else i + 1) for i in range(count))
 
     packed = like((owners, shard // 2, width), BF16)
-    send, edge, slab = pl.pallas_call(
+    send = pl.pallas_call(
         pack_body,
-        out_shape=(packed, like((3, rows, cols, width), BF16), like((4, rows, cols, width), BF16)),
+        out_shape=packed,
         name="pack",
         compiler_params=pltpu.CompilerParams(vmem_limit_bytes=8 << 20),
-    )(master, volume, cotangent)
+    )(master)
     halves = lax.all_to_all(send, "dp", 0, 0, tiled=True)
+    edge, slab = pl.pallas_call(
+        edges_body,
+        out_shape=(like((3, rows, cols, width), BF16), like((4, rows, cols, width), BF16)),
+        name="edges",
+        compiler_params=pltpu.CompilerParams(vmem_limit_bytes=4 << 20),
+    )(volume, cotangent)
     near = moved(edge, outward)
     whole = jnp.concatenate([v.reshape(-1, width) for v in (halves, near, slab)], axis=0)
     got = moved(whole, swap)
@@ -273,7 +280,7 @@
         forward_body,
         out_shape=(like(volume.shape, BF16), like((4 * cells, width), BF16), packed),
         scratch_shapes=[
-            pltpu.VMEM((8 * cells, 9 * width), BF16),
+            pltpu.VMEM((7 * cells, 9 * width), BF16),
             pltpu.VMEM((9 * width, 2 * width), BF16),
             pltpu.VMEM((9 * width, width), BF16),
             pltpu.VMEM((width, 4 * cells), F32),

time: 109 us -> 107 us (0.982)
  local copies, waits for them, and re-layouts: 3.31 us -> 1.63 us
    unnamed x16 -> x12, local copies, waits for them, and re-layouts: 2.61 us -> 0.93 us
where the time goes in v6:
time: 107 us; the launch traced here: 106 us
  blocking collectives  54.2 us (51%)
  starting transfers between devices  29.6 us (28%)
  waiting for transfers between devices  13.2 us (12%)
  Pallas kernels  6.76 us (6%)
  local copies, waits for them, and re-layouts  1.63 us (2%)
    all_to_all x2, blocking collectives, exchanged(): lax.all_to_all(tiles, 'spatial', 0, 0, tiled=True, axis_index_groups=groups)  32.4 us
    all_to_all x1, blocking collectives, layer(): arrived = lax.all_to_all(weight, 'dp', 0, 0, tiled=True)  21.9 us
    ppermute x2, starting transfers between devices, moved(): return lax.ppermute(value, 'spatial', perm)  13.3 us
    all_to_all x1, waiting for transfers between devices, exchanged(): lax.all_to_all(tiles, 'spatial', 0, 0, tiled=True, axis_index_groups=groups)  8.8 us
    all_to_all x1, starting transfers between devices, layer(): halves = lax.all_to_all(send, 'dp', 0, 0, tiled=True)  8.49 us
    all_to_all x1, starting transfers between devices, exchanged(): lax.all_to_all(tiles, 'spatial', 0, 0, tiled=True, axis_index_groups=groups)  7.81 us
    ppermute x2, waiting for transfers between devices, moved(): return lax.ppermute(value, 'spatial', perm)  4.35 us
    pallas_call x1, Pallas kernels, layer(): pl.pallas_call(forward_body, out_shape=(like(volume.shape, BF16), like((4...  3.47 us
  transfers between devices with their start and end apart: 4, of which 3 were waited for; matrix products, arithmetic and copies ran while one was open for 0% of the time, Pallas kernels for 1%

profile of v6, /device:TPU:1, one launch (start us, length us, event | category | flops | bytes accessed | tf_op | source)
XLA Modules:
  0.0 106.3 jit_solution(1439888434421942574)
XLA Ops:
  0.6 0.0 copy-start
  0.6 0.9 copy-done
  1.5 0.9 pack.1
  2.4 8.5 %all-to-all-start = ((bf16[12,144,128]{2,1,0:T(8,128)(2,1)}), bf16[12,144,128]{2,1,0:T(8,128)(2,1)S(1)}, u32[]{:S(2)}, u32[]{:S(2)}) async-start(bf16[12,144,128]{2,1,0:T(8,128)(2,1)} %pack.1), calls=%async_computation | async-start | bytes 884736 | tf_op jit(solution)/shard_map/all_to_all | solution.py:269
  10.9 0.0 copy-done.2
  10.9 0.0 copy-done.3
  11.0 9.7 %collective-permute-start = (bf16[3,16,8,128]{3,2,1,0:T(8,128)(2,1)S(1)}, bf16[3,16,8,128]{3,2,1,0:T(8,128)(2,1)S(1)}, u32[]{:S(2)}, u32[]{:S(2)}) collective-permute-start(bf16[3,16,8,128]{3,2,1,0:T(8,128)(2,1)S(1)} %get-tuple-element.13), channel_id=1, source_target_pairs={{1,2},{2,1},{3,4},{4,3},{5,6},{6,5},{7,8},{8,7},{9,10},{10,9},{11,... | collective-permute-start | bytes 294920 | tf_op jit(solution)/shard_map/ppermute | solution.py:244
  20.6 2.6 %collective-permute-done.near_ref = bf16[3,16,8,128]{3,2,1,0:T(8,128)(2,1)S(1)} collective-permute-done((bf16[3,16,8,128]{3,2,1,0:T(8,128)(2,1)S(1)}, bf16[3,16,8,128]{3,2,1,0:T(8,128)(2,1)S(1)}, u32[]{:S(2)}, u32[]{:S(2)}) %collective-permute-start) | collective-permute-done | bytes 98336 | tf_op jit(solution)/shard_map/ppermute | solution.py:244
  23.3 0.0 all-to-all-done.kernel_ref
  23.3 3.7 %collective-permute-start.1 = (bf16[2624,128]{1,0:T(8,128)(2,1)S(1)}, bf16[2624,128]{1,0:T(8,128)(2,1)S(1)}, u32[]{:S(2)}, u32[]{:S(2)}) collective-permute-start(bf16[2624,128]{1,0:T(8,128)(2,1)S(1)} %pad_maximum_fusion), channel_id=1, source_target_pairs={{0,1},{1,0},{2,3},{3,2},{4,5},{5,4},{6,7},{7,6},{8,9},{9,8},{10,11... | collective-permute-start | bytes 2015240 | tf_op jit(solution)/shard_map/ppermute | solution.py:244
  27.0 1.7 %collective-permute-done.1.got_ref = bf16[2624,128]{1,0:T(8,128)(2,1)S(1)} collective-permute-done((bf16[2624,128]{1,0:T(8,128)(2,1)S(1)}, bf16[2624,128]{1,0:T(8,128)(2,1)S(1)}, u32[]{:S(2)}, u32[]{:S(2)}) %collective-permute-start.1) | collective-permute-done | bytes 671776 | tf_op jit(solution)/shard_map/ppermute | solution.py:244
  28.7 3.5 %forward.1 = (bf16[1,2,16,8,128]{4,3,2,1,0:T(8,128)(2,1)}, bf16[512,128]{1,0:T(8,128)(2,1)S(1)}, bf16[12,144,128]{2,1,0:T(8,128)(2,1)S(1)}) custom-call(bf16[12,144,128]{2,1,0:T(8,128)(2,1)S(1)} %all-to-all-done.kernel_ref, bf16[2624,128]{1,0:T(8,128)(2,1)S(1)} %collective-permute-done.1.got_ref, bf16[1,2,16,8,128]{4,3,2,1,0:T(8,128)(2,1)S(1)} %copy-done.2, ...), custom_call_target="tpu_custom_call" | custom-call | tf_op jit(solution)/shard_map/forward/pallas_call | solution.py:279
  32.2 21.9 %all_to_all.25 = bf16[12,144,128]{2,1,0:T(8,128)(2,1)S(1)} all-to-all(bf16[12,144,128]{2,1,0:T(8,128)(2,1)S(1)} %get-tuple-element.17), channel_id=1, replica_groups=mesh['dp'=12,'spatial'=64] {'dp'}, dimensions={0} | all-to-all | bytes 884736 | tf_op jit(solution)/shard_map/all_to_all | solution.py:293
  54.1 0.1 convert_reduce_fusion
  54.1 15.4 %all_to_all.26 = f32[8,24,128]{2,1,0:T(8,128)S(1)} all-to-all(f32[8,24,128]{2,1,0:T(8,128)S(1)} %pad.4), channel_id=1, replica_groups={{0,8,16,24,32,40,48,56},{1,9,17,25,33,41,49,57},{2,10,18,26,34,42,50,58..., dimensions={0} | all-to-all | bytes 196608 | tf_op jit(solution)/shard_map/all_to_all | solution.py:240
  69.5 17.0 %all_to_all.27 = f32[4,24,128]{2,1,0:T(8,128)S(1)} all-to-all(f32[4,24,128]{2,1,0:T(8,128)S(1)} %broadcast_in_dim.4), channel_id=1, replica_groups={{0,2,4,6},{1,3,5,7},{8,10,12,14},{9,11,13,15},{16,18,20,22},{17,19,21,2..., dimensions={0} | all-to-all | bytes 98304 | tf_op jit(solution)/shard_map/all_to_all | solution.py:240
  86.5 0.7 broadcast_in_dim.5
  87.2 7.8 %all-to-all-start.4 = ((f32[16,24,128]{2,1,0:T(8,128)}), f32[16,24,128]{2,1,0:T(8,128)S(1)}, u32[]{:S(2)}, u32[]{:S(2)}) async-start(f32[16,24,128]{2,1,0:T(8,128)} %broadcast_in_dim.5), calls=%async_computation.4 | async-start | bytes 393216 | tf_op jit(solution)/shard_map/all_to_all | solution.py:240
  95.1 0.0 copy-start.4
  95.1 0.0 copy-start.5
  95.1 1.4 %backward.1 = bf16[1,2,16,8,128]{4,3,2,1,0:T(8,128)(2,1)} custom-call(bf16[12,144,128]{2,1,0:T(8,128)(2,1)S(1)} %all-to-all-done.kernel_ref, bf16[2624,128]{1,0:T(8,128)(2,1)S(1)} %collective-permute-done.1.got_ref, bf16[512,128]{1,0:T(8,128)(2,1)S(1)} %get-tuple-element.16.grad_ref), custom_call_target="tpu_custom_call" | custom-call | flops 226492416 | bytes 442368 | tf_op jit(solution)/shard_map/backward/pallas_call | solution.py:294
  96.5 8.8 %all-to-all-done.4.grads_ref = f32[16,24,128]{2,1,0:T(8,128)S(1)} async-done(((f32[16,24,128]{2,1,0:T(8,128)}), f32[16,24,128]{2,1,0:T(8,128)S(1)}, u32[]{:S(2)}, u32[]{:S(2)}) %all-to-all-start.4) | async-done | bytes 196640 | tf_op jit(solution)/shard_map/all_to_all | solution.py:240
  105.3 0.0 copy-done.1
  105.3 1.0 update.1
  (11 shorter events, 0.1 us)
Async XLA Ops:
  0.6 0.9 copy-start
  1.5 9.4 %copy-start.2 = (bf16[1,2,16,8,128]{4,3,2,1,0:T(8,128)(2,1)S(1)}, bf16[1,2,16,8,128]{4,3,2,1,0:T(8,128)(2,1)}, u32[]{:S(2)}) copy-start(bf16[1,2,16,8,128]{4,3,2,1,0:T(8,128)(2,1)} %volume_ref.3) | copy-start | bytes 196612
  1.5 9.4 %copy-start.3 = (bf16[1,2,16,8,128]{4,3,2,1,0:T(8,128)(2,1)S(1)}, bf16[1,2,16,8,128]{4,3,2,1,0:T(8,128)(2,1)}, u32[]{:S(2)}) copy-start(bf16[1,2,16,8,128]{4,3,2,1,0:T(8,128)(2,1)} %cot_ref.3) | copy-start | bytes 196612
  2.4 20.9 %all-to-all-start = ((bf16[12,144,128]{2,1,0:T(8,128)(2,1)}), bf16[12,144,128]{2,1,0:T(8,128)(2,1)S(1)}, u32[]{:S(2)}, u32[]{:S(2)}) async-start(bf16[12,144,128]{2,1,0:T(8,128)(2,1)} %pack.1), calls=%async_computation | async-start | bytes 884736 | tf_op jit(solution)/shard_map/all_to_all | solution.py:269
  11.0 12.3 %collective-permute-start = (bf16[3,16,8,128]{3,2,1,0:T(8,128)(2,1)S(1)}, bf16[3,16,8,128]{3,2,1,0:T(8,128)(2,1)S(1)}, u32[]{:S(2)}, u32[]{:S(2)}) collective-permute-start(bf16[3,16,8,128]{3,2,1,0:T(8,128)(2,1)S(1)} %get-tuple-element.13), channel_id=1, source_target_pairs={{1,2},{2,1},{3,4},{4,3},{5,6},{6,5},{7,8},{8,7},{9,10},{10,9},{11,... | collective-permute-start | bytes 294920 | tf_op jit(solution)/shard_map/ppermute | solution.py:244
  23.3 5.4 %collective-permute-start.1 = (bf16[2624,128]{1,0:T(8,128)(2,1)S(1)}, bf16[2624,128]{1,0:T(8,128)(2,1)S(1)}, u32[]{:S(2)}, u32[]{:S(2)}) collective-permute-start(bf16[2624,128]{1,0:T(8,128)(2,1)S(1)} %pad_maximum_fusion), channel_id=1, source_target_pairs={{0,1},{1,0},{2,3},{3,2},{4,5},{5,4},{6,7},{7,6},{8,9},{9,8},{10,11... | collective-permute-start | bytes 2015240 | tf_op jit(solution)/shard_map/ppermute | solution.py:244
  87.2 18.1 %all-to-all-start.4 = ((f32[16,24,128]{2,1,0:T(8,128)}), f32[16,24,128]{2,1,0:T(8,128)S(1)}, u32[]{:S(2)}, u32[]{:S(2)}) async-start(f32[16,24,128]{2,1,0:T(8,128)} %broadcast_in_dim.5), calls=%async_computation.4 | async-start | bytes 393216 | tf_op jit(solution)/shard_map/all_to_all | solution.py:240
  95.0 10.3 %copy-start.1 = (f32[288,128]{1,0:T(8,128)S(1)}, f32[288,128]{1,0:T(8,128)}, u32[]{:S(2)}) copy-start(f32[288,128]{1,0:T(8,128)} %master_ref.3) | copy-start | bytes 442372
  95.1 10.3 %copy-start.4 = (f32[288,128]{1,0:T(8,128)S(1)}, f32[288,128]{1,0:T(8,128)}, u32[]{:S(2)}) copy-start(f32[288,128]{1,0:T(8,128)} %moment_ref.1) | copy-start | bytes 442372
  95.1 10.3 %copy-start.5 = (f32[288,128]{1,0:T(8,128)S(1)}, f32[288,128]{1,0:T(8,128)}, u32[]{:S(2)}) copy-start(f32[288,128]{1,0:T(8,128)} %second_ref.1) | copy-start | bytes 442372

commit v7 on v6

--- a/solution.py
+++ b/solution.py
@@ -131,7 +131,18 @@
     inner = 4 * cells
     span = 9 * width
     product = jnp.dot(window_ref[: count + cells], wide_ref[...], preferred_element_type=F32)
-    preact = jnp.dot(window_ref[2 * cells :], deep_ref[...], preferred_element_type=F32)
+    part = count // 2
+    preact = jnp.concatenate(
+        [
+            jnp.dot(
+                window_ref[2 * cells + i * part : 2 * cells + (i + 1) * part],
+                deep_ref[...],
+                preferred_element_type=F32,
+            )
+            for i in range(2)
+        ],
+        axis=0,
+    )
     preact = preact + product[:count, :width] + product[cells:, width:]
     sigma = jax.nn.sigmoid(preact)
     slope = sigma * (1.0 + preact * (1.0 - sigma))
@@ -146,9 +157,14 @@
     for offset in range(3):
         stack_ref[offset * HALF : (offset + 1) * HALF, offset * cells : offset * cells + inner] = mine
     at = pl.multiple_of(jnp.where(low, cells, 0), cells)
-    stacked = jnp.dot(stack_ref[...], window_ref[pl.ds(at, 6 * cells)], preferred_element_type=F32)
-    for offset in range(3):
-        total_ref[:, offset * span : (offset + 1) * span] = stacked[offset * HALF : (offset + 1) * HALF]
+    for left, right in ((0, 5 * width), (5 * width, span)):
+        stacked = jnp.dot(
+            stack_ref[...], window_ref[pl.ds(at, 6 * cells), left:right], preferred_element_type=F32
+        )
+        for offset in range(3):
+            total_ref[:, offset * span + left : offset * span + right] = stacked[
+                offset * HALF : (offset + 1) * HALF
+            ]
     lane = lane_of((HALF, width))
 
     def columns(start):
@@ -204,6 +220,27 @@
                 preferred_element_type=F32,
             )
     out_ref[0] = total.reshape(2, *shape).astype(BF16)
+
+
+def finish_body(
+    cells_all,
+    grads_ref,
+    master_ref,
+    moment_ref,
+    second_ref,
+    kernel_ref,
+    got_ref,
+    hidden_ref,
+    out_ref,
+    out_m_ref,
+    out_s_ref,
+    out_input_ref,
+    grad_ref,
+    window_ref,
+    turn_ref,
+):
+    update_body(cells_all, grads_ref, master_ref, moment_ref, second_ref, out_ref, out_m_ref, out_s_ref, grad_ref)
+    backward_body(kernel_ref, got_ref, hidden_ref, out_input_ref, window_ref, turn_ref)
 
 
 def update_body(cells_all, grads_ref, master_ref, moment_ref, second_ref, out_ref, out_m_ref, out_s_ref, grad_ref):
@@ -291,20 +328,6 @@
         compiler_params=pltpu.CompilerParams(vmem_limit_bytes=28 << 20),
     )(halves, got, volume, cotangent, near)
     arrived = lax.all_to_all(weight, "dp", 0, 0, tiled=True)
-    input_grad = pl.pallas_call(
-        backward_body,
-        out_shape=like(volume.shape, BF16),
-        scratch_shapes=[
-            pltpu.VMEM((4 * cells, 9 * width), BF16),
-            pltpu.VMEM((taps_all, width), BF16),
-        ],
-        cost_estimate=pl.CostEstimate(
-            flops=2 * 2 * cells * taps_all * width, bytes_accessed=taps_all * width, transcendentals=0
-        ),
-        name="backward",
-    compiler_params=pltpu.CompilerParams(vmem_limit_bytes=20 << 20),
-    )(halves, got, grad)
-
     same_y = [
         [(y * MIDDLE + h) * PAIR + c for h in range(MIDDLE)] for y in range(OUTER) for c in range(PAIR)
     ]
@@ -322,13 +345,17 @@
     joined = exchanged(jnp.broadcast_to(piece[None], (OUTER * PAIR, PIECE, width)), same_z)
     cells_all = owners * count * planes * cells
     state = like(master.shape, F32)
-    master_next, moment_next, second_next = pl.pallas_call(
-        functools.partial(update_body, cells_all),
-        out_shape=(state, state, state),
-        scratch_shapes=[pltpu.VMEM(master.shape, F32)],
-        name="update",
-        compiler_params=pltpu.CompilerParams(vmem_limit_bytes=8 << 20),
-    )(joined, master, moment, second)
+    master_next, moment_next, second_next, input_grad = pl.pallas_call(
+        functools.partial(finish_body, cells_all),
+        out_shape=(state, state, state, like(volume.shape, BF16)),
+        scratch_shapes=[
+            pltpu.VMEM(master.shape, F32),
+            pltpu.VMEM((4 * cells, 9 * width), BF16),
+            pltpu.VMEM((taps_all, width), BF16),
+        ],
+        name="finish",
+        compiler_params=pltpu.CompilerParams(vmem_limit_bytes=20 << 20),
+    )(joined, master, moment, second, halves, got, grad)
     return (activation, input_grad, master_next, moment_next, second_next)
 
 

time: 107 us -> 105 us (0.981)
  blocking collectives: 54.2 us -> 71.6 us
  waiting for transfers between devices: 13.2 us -> 4.35 us
  starting transfers between devices: 29.6 us -> 21.8 us
  Pallas kernels: 6.76 us -> 5.33 us
    all_to_all x2 -> x3, blocking collectives: 32.4 us -> 49.7 us  [exchanged(): lax.all_to_all(tiles, 'spatial', 0, 0, tiled=True, axis_index_groups=groups)]
    all_to_all x1 -> x0, waiting for transfers between devices: 8.8 us -> none  [exchanged(): lax.all_to_all(tiles, 'spatial', 0, 0, tiled=True, axis_index_groups=groups)]
    all_to_all x1 -> x0, starting transfers between devices: 7.81 us -> none  [exchanged(): lax.all_to_all(tiles, 'spatial', 0, 0, tiled=True, axis_index_groups=groups)]
    pallas_call x2 -> x1, Pallas kernels: 2.4 us -> 1.54 us  [layer(): pl.pallas_call(functools.partial(finish_body, cells_all), out_shape=(stat...]
  transfers between devices with their start and end apart: 4 -> 3, of which waited for: 3 -> 2; matrix products, arithmetic and copies ran while one was open for 0% -> 0% of each run, Pallas kernels for 1% -> 0%
where the time goes in v7:
time: 105 us
  blocking collectives  71.6 us (68%)
  starting transfers between devices  21.8 us (21%)
  Pallas kernels  5.33 us (5%)
  waiting for transfers between devices  4.35 us (4%)
    all_to_all x3, blocking collectives, exchanged(): lax.all_to_all(tiles, 'spatial', 0, 0, tiled=True, axis_index_groups=groups)  49.7 us
    all_to_all x1, blocking collectives, layer(): arrived = lax.all_to_all(weight, 'dp', 0, 0, tiled=True)  21.9 us
    ppermute x2, starting transfers between devices, moved(): return lax.ppermute(value, 'spatial', perm)  13.3 us
    all_to_all x1, starting transfers between devices, layer(): halves = lax.all_to_all(send, 'dp', 0, 0, tiled=True)  8.49 us
    ppermute x2, waiting for transfers between devices, moved(): return lax.ppermute(value, 'spatial', perm)  4.35 us
    pallas_call x1, Pallas kernels, layer(): pl.pallas_call(forward_body, out_shape=(like(volume.shape, BF16), like((4...  2.89 us
  transfers between devices with their start and end apart: 3, of which 2 were waited for; matrix products, arithmetic and copies ran while one was open for 0% of the time, Pallas kernels for 0%

profile of v7, /device:TPU:1, one launch (start us, length us, event | category | flops | bytes accessed | tf_op | source)
XLA Modules:
  0.0 104.9 jit_solution(10154349209892161245)
XLA Ops:
  0.6 0.0 copy-start
  0.6 0.9 copy-done
  1.5 0.9 pack.1
  2.4 8.5 %all-to-all-start = ((bf16[12,144,128]{2,1,0:T(8,128)(2,1)}), bf16[12,144,128]{2,1,0:T(8,128)(2,1)S(1)}, u32[]{:S(2)}, u32[]{:S(2)}) async-start(bf16[12,144,128]{2,1,0:T(8,128)(2,1)} %pack.1), calls=%async_computation | async-start | bytes 884736 | tf_op jit(solution)/shard_map/all_to_all | solution.py:306
  10.9 0.0 copy-done.2
  10.9 0.0 copy-done.3
  11.0 9.7 %collective-permute-start = (bf16[3,16,8,128]{3,2,1,0:T(8,128)(2,1)S(1)}, bf16[3,16,8,128]{3,2,1,0:T(8,128)(2,1)S(1)}, u32[]{:S(2)}, u32[]{:S(2)}) collective-permute-start(bf16[3,16,8,128]{3,2,1,0:T(8,128)(2,1)S(1)} %get-tuple-element.14), channel_id=1, source_target_pairs={{1,2},{2,1},{3,4},{4,3},{5,6},{6,5},{7,8},{8,7},{9,10},{10,9},{11,... | collective-permute-start | bytes 294920 | tf_op jit(solution)/shard_map/ppermute | solution.py:281
  20.7 2.6 %collective-permute-done.near_ref = bf16[3,16,8,128]{3,2,1,0:T(8,128)(2,1)S(1)} collective-permute-done((bf16[3,16,8,128]{3,2,1,0:T(8,128)(2,1)S(1)}, bf16[3,16,8,128]{3,2,1,0:T(8,128)(2,1)S(1)}, u32[]{:S(2)}, u32[]{:S(2)}) %collective-permute-start) | collective-permute-done | bytes 98336 | tf_op jit(solution)/shard_map/ppermute | solution.py:281
  23.3 0.0 all-to-all-done.kernel_ref
  23.3 3.7 %collective-permute-start.1 = (bf16[2624,128]{1,0:T(8,128)(2,1)S(1)}, bf16[2624,128]{1,0:T(8,128)(2,1)S(1)}, u32[]{:S(2)}, u32[]{:S(2)}) collective-permute-start(bf16[2624,128]{1,0:T(8,128)(2,1)S(1)} %pad_maximum_fusion), channel_id=1, source_target_pairs={{0,1},{1,0},{2,3},{3,2},{4,5},{5,4},{6,7},{7,6},{8,9},{9,8},{10,11... | collective-permute-start | bytes 2015240 | tf_op jit(solution)/shard_map/ppermute | solution.py:281
  27.0 1.7 %collective-permute-done.1.got_ref = bf16[2624,128]{1,0:T(8,128)(2,1)S(1)} collective-permute-done((bf16[2624,128]{1,0:T(8,128)(2,1)S(1)}, bf16[2624,128]{1,0:T(8,128)(2,1)S(1)}, u32[]{:S(2)}, u32[]{:S(2)}) %collective-permute-start.1) | collective-permute-done | bytes 671776 | tf_op jit(solution)/shard_map/ppermute | solution.py:281
  28.7 2.9 %forward.1 = (bf16[1,2,16,8,128]{4,3,2,1,0:T(8,128)(2,1)}, bf16[512,128]{1,0:T(8,128)(2,1)S(1)}, bf16[12,144,128]{2,1,0:T(8,128)(2,1)S(1)}) custom-call(bf16[12,144,128]{2,1,0:T(8,128)(2,1)S(1)} %all-to-all-done.kernel_ref, bf16[2624,128]{1,0:T(8,128)(2,1)S(1)} %collective-permute-done.1.got_ref, bf16[1,2,16,8,128]{4,3,2,1,0:T(8,128)(2,1)S(1)} %copy-done.2, ...), custom_call_target="tpu_custom_call" | custom-call | tf_op jit(solution)/shard_map/forward/pallas_call | solution.py:316
  31.6 21.9 %all_to_all.25 = bf16[12,144,128]{2,1,0:T(8,128)(2,1)S(1)} all-to-all(bf16[12,144,128]{2,1,0:T(8,128)(2,1)S(1)} %get-tuple-element.17), channel_id=1, replica_groups=mesh['dp'=12,'spatial'=64] {'dp'}, dimensions={0} | all-to-all | bytes 884736 | tf_op jit(solution)/shard_map/all_to_all | solution.py:330
  53.5 0.1 convert_reduce_fusion
  53.6 0.0 copy-start.1
  53.6 0.0 copy-start.4
  53.6 0.0 copy-start.5
  53.6 15.5 %all_to_all.26 = f32[8,24,128]{2,1,0:T(8,128)S(1)} all-to-all(f32[8,24,128]{2,1,0:T(8,128)S(1)} %pad.4), channel_id=1, replica_groups={{0,8,16,24,32,40,48,56},{1,9,17,25,33,41,49,57},{2,10,18,26,34,42,50,58..., dimensions={0} | all-to-all | bytes 196608 | tf_op jit(solution)/shard_map/all_to_all | solution.py:277
  69.1 17.0 %all_to_all.27 = f32[4,24,128]{2,1,0:T(8,128)S(1)} all-to-all(f32[4,24,128]{2,1,0:T(8,128)S(1)} %broadcast_in_dim.4), channel_id=1, replica_groups={{0,2,4,6},{1,3,5,7},{8,10,12,14},{9,11,13,15},{16,18,20,22},{17,19,21,2..., dimensions={0} | all-to-all | bytes 98304 | tf_op jit(solution)/shard_map/all_to_all | solution.py:277
  86.2 17.2 %all_to_all.28.grads_ref = f32[16,24,128]{2,1,0:T(8,128)S(1)} all-to-all(f32[16,24,128]{2,1,0:T(8,128)S(1)} %broadcast_in_dim.5), channel_id=1, replica_groups={{0,1,8,9,16,17,24,25,32,33,40,41,48,49,56,57},{2,3,10,11,18,19,26,27,34..., dimensions={0} | all-to-all | bytes 393216 | tf_op jit(solution)/shard_map/all_to_all | solution.py:277
  103.4 0.0 copy-done.1
  103.4 0.0 copy-done.4
  103.4 0.0 copy-done.5
  103.4 1.5 %finish.1 = (f32[288,128]{1,0:T(8,128)}, f32[288,128]{1,0:T(8,128)}, f32[288,128]{1,0:T(8,128)}, bf16[1,2,16,8,128]{4,3,2,1,0:T(8,128)(2,1)}) custom-call(f32[16,24,128]{2,1,0:T(8,128)S(1)} %all_to_all.28.grads_ref, f32[288,128]{1,0:T(8,128)S(1)} %copy-done.1, f32[288,128]{1,0:T(8,128)S(1)} %copy-done.4, f32[288,128]{1,0:T(8,128)S(1)} %copy-done.5, ...), custom_call_target="tpu_custom_call" | custom-call | tf_op jit(solution)/shard_map/finish/pallas_call | solution.py:348
  (9 shorter events, 0.1 us)
Async XLA Ops:
  0.6 0.9 copy-start
  1.5 9.4 %copy-start.2 = (bf16[1,2,16,8,128]{4,3,2,1,0:T(8,128)(2,1)S(1)}, bf16[1,2,16,8,128]{4,3,2,1,0:T(8,128)(2,1)}, u32[]{:S(2)}) copy-start(bf16[1,2,16,8,128]{4,3,2,1,0:T(8,128)(2,1)} %volume_ref.3) | copy-start | bytes 196612
  1.5 9.4 %copy-start.3 = (bf16[1,2,16,8,128]{4,3,2,1,0:T(8,128)(2,1)S(1)}, bf16[1,2,16,8,128]{4,3,2,1,0:T(8,128)(2,1)}, u32[]{:S(2)}) copy-start(bf16[1,2,16,8,128]{4,3,2,1,0:T(8,128)(2,1)} %cot_ref.3) | copy-start | bytes 196612
  2.4 20.9 %all-to-all-start = ((bf16[12,144,128]{2,1,0:T(8,128)(2,1)}), bf16[12,144,128]{2,1,0:T(8,128)(2,1)S(1)}, u32[]{:S(2)}, u32[]{:S(2)}) async-start(bf16[12,144,128]{2,1,0:T(8,128)(2,1)} %pack.1), calls=%async_computation | async-start | bytes 884736 | tf_op jit(solution)/shard_map/all_to_all | solution.py:306
  11.0 12.3 %collective-permute-start = (bf16[3,16,8,128]{3,2,1,0:T(8,128)(2,1)S(1)}, bf16[3,16,8,128]{3,2,1,0:T(8,128)(2,1)S(1)}, u32[]{:S(2)}, u32[]{:S(2)}) collective-permute-start(bf16[3,16,8,128]{3,2,1,0:T(8,128)(2,1)S(1)} %get-tuple-element.14), channel_id=1, source_target_pairs={{1,2},{2,1},{3,4},{4,3},{5,6},{6,5},{7,8},{8,7},{9,10},{10,9},{11,... | collective-permute-start | bytes 294920 | tf_op jit(solution)/shard_map/ppermute | solution.py:281
  23.3 5.4 %collective-permute-start.1 = (bf16[2624,128]{1,0:T(8,128)(2,1)S(1)}, bf16[2624,128]{1,0:T(8,128)(2,1)S(1)}, u32[]{:S(2)}, u32[]{:S(2)}) collective-permute-start(bf16[2624,128]{1,0:T(8,128)(2,1)S(1)} %pad_maximum_fusion), channel_id=1, source_target_pairs={{0,1},{1,0},{2,3},{3,2},{4,5},{5,4},{6,7},{7,6},{8,9},{9,8},{10,11... | collective-permute-start | bytes 2015240 | tf_op jit(solution)/shard_map/ppermute | solution.py:281
  53.6 49.8 %copy-start.1 = (f32[288,128]{1,0:T(8,128)S(1)}, f32[288,128]{1,0:T(8,128)}, u32[]{:S(2)}) copy-start(f32[288,128]{1,0:T(8,128)} %master_ref.3) | copy-start | bytes 442372
  53.6 49.8 %copy-start.4 = (f32[288,128]{1,0:T(8,128)S(1)}, f32[288,128]{1,0:T(8,128)}, u32[]{:S(2)}) copy-start(f32[288,128]{1,0:T(8,128)} %moment_ref.1) | copy-start | bytes 442372
  53.6 49.8 %copy-start.5 = (f32[288,128]{1,0:T(8,128)S(1)}, f32[288,128]{1,0:T(8,128)}, u32[]{:S(2)}) copy-start(f32[288,128]{1,0:T(8,128)} %second_ref.1) | copy-start | bytes 442372

commit v8 on v6

--- a/solution.py
+++ b/solution.py
@@ -131,7 +131,18 @@
     inner = 4 * cells
     span = 9 * width
     product = jnp.dot(window_ref[: count + cells], wide_ref[...], preferred_element_type=F32)
-    preact = jnp.dot(window_ref[2 * cells :], deep_ref[...], preferred_element_type=F32)
+    part = count // 2
+    preact = jnp.concatenate(
+        [
+            jnp.dot(
+                window_ref[2 * cells + i * part : 2 * cells + (i + 1) * part],
+                deep_ref[...],
+                preferred_element_type=F32,
+            )
+            for i in range(2)
+        ],
+        axis=0,
+    )
     preact = preact + product[:count, :width] + product[cells:, width:]
     sigma = jax.nn.sigmoid(preact)
     slope = sigma * (1.0 + preact * (1.0 - sigma))
@@ -146,9 +157,14 @@
     for offset in range(3):
         stack_ref[offset * HALF : (offset + 1) * HALF, offset * cells : offset * cells + inner] = mine
     at = pl.multiple_of(jnp.where(low, cells, 0), cells)
-    stacked = jnp.dot(stack_ref[...], window_ref[pl.ds(at, 6 * cells)], preferred_element_type=F32)
-    for offset in range(3):
-        total_ref[:, offset * span : (offset + 1) * span] = stacked[offset * HALF : (offset + 1) * HALF]
+    for left, right in ((0, 5 * width), (5 * width, span)):
+        stacked = jnp.dot(
+            stack_ref[...], window_ref[pl.ds(at, 6 * cells), left:right], preferred_element_type=F32
+        )
+        for offset in range(3):
+            total_ref[:, offset * span + left : offset * span + right] = stacked[
+                offset * HALF : (offset + 1) * HALF
+            ]
     lane = lane_of((HALF, width))
 
     def columns(start):

time: 107 us -> 106 us (level)
  no operation moved by 1% of the time
where the time goes in v8:
time: 106 us
  blocking collectives  54.2 us (51%)
  starting transfers between devices  29.6 us (28%)
  waiting for transfers between devices  13.2 us (12%)
  Pallas kernels  6.18 us (6%)
  local copies, waits for them, and re-layouts  1.63 us (2%)
    all_to_all x2, blocking collectives, exchanged(): lax.all_to_all(tiles, 'spatial', 0, 0, tiled=True, axis_index_groups=groups)  32.3 us
    all_to_all x1, blocking collectives, layer(): arrived = lax.all_to_all(weight, 'dp', 0, 0, tiled=True)  21.9 us
    ppermute x2, starting transfers between devices, moved(): return lax.ppermute(value, 'spatial', perm)  13.3 us
    all_to_all x1, waiting for transfers between devices, exchanged(): lax.all_to_all(tiles, 'spatial', 0, 0, tiled=True, axis_index_groups=groups)  8.8 us
    all_to_all x1, starting transfers between devices, layer(): halves = lax.all_to_all(send, 'dp', 0, 0, tiled=True)  8.49 us
    all_to_all x1, starting transfers between devices, exchanged(): lax.all_to_all(tiles, 'spatial', 0, 0, tiled=True, axis_index_groups=groups)  7.82 us
    ppermute x2, waiting for transfers between devices, moved(): return lax.ppermute(value, 'spatial', perm)  4.35 us
    pallas_call x1, Pallas kernels, layer(): pl.pallas_call(forward_body, out_shape=(like(volume.shape, BF16), like((4...  2.89 us
  transfers between devices with their start and end apart: 4, of which 3 were waited for; matrix products, arithmetic and copies ran while one was open for 0% of the time, Pallas kernels for 1%

profile of v8, /device:TPU:1, one launch (start us, length us, event | category | flops | bytes accessed | tf_op | source)
XLA Modules:
  0.0 105.7 jit_solution(14621204671879127557)
XLA Ops:
  0.6 0.0 copy-start
  0.6 0.9 copy-done
  1.5 0.9 pack.1
  2.4 8.5 %all-to-all-start = ((bf16[12,144,128]{2,1,0:T(8,128)(2,1)}), bf16[12,144,128]{2,1,0:T(8,128)(2,1)S(1)}, u32[]{:S(2)}, u32[]{:S(2)}) async-start(bf16[12,144,128]{2,1,0:T(8,128)(2,1)} %pack.1), calls=%async_computation | async-start | bytes 884736 | tf_op jit(solution)/shard_map/all_to_all | solution.py:285
  10.9 0.0 copy-done.2
  10.9 0.0 copy-done.3
  11.0 9.7 %collective-permute-start = (bf16[3,16,8,128]{3,2,1,0:T(8,128)(2,1)S(1)}, bf16[3,16,8,128]{3,2,1,0:T(8,128)(2,1)S(1)}, u32[]{:S(2)}, u32[]{:S(2)}) collective-permute-start(bf16[3,16,8,128]{3,2,1,0:T(8,128)(2,1)S(1)} %get-tuple-element.13), channel_id=1, source_target_pairs={{1,2},{2,1},{3,4},{4,3},{5,6},{6,5},{7,8},{8,7},{9,10},{10,9},{11,... | collective-permute-start | bytes 294920 | tf_op jit(solution)/shard_map/ppermute | solution.py:260
  20.6 2.6 %collective-permute-done.near_ref = bf16[3,16,8,128]{3,2,1,0:T(8,128)(2,1)S(1)} collective-permute-done((bf16[3,16,8,128]{3,2,1,0:T(8,128)(2,1)S(1)}, bf16[3,16,8,128]{3,2,1,0:T(8,128)(2,1)S(1)}, u32[]{:S(2)}, u32[]{:S(2)}) %collective-permute-start) | collective-permute-done | bytes 98336 | tf_op jit(solution)/shard_map/ppermute | solution.py:260
  23.3 0.0 all-to-all-done.kernel_ref
  23.3 3.7 %collective-permute-start.1 = (bf16[2624,128]{1,0:T(8,128)(2,1)S(1)}, bf16[2624,128]{1,0:T(8,128)(2,1)S(1)}, u32[]{:S(2)}, u32[]{:S(2)}) collective-permute-start(bf16[2624,128]{1,0:T(8,128)(2,1)S(1)} %pad_maximum_fusion), channel_id=1, source_target_pairs={{0,1},{1,0},{2,3},{3,2},{4,5},{5,4},{6,7},{7,6},{8,9},{9,8},{10,11... | collective-permute-start | bytes 2015240 | tf_op jit(solution)/shard_map/ppermute | solution.py:260
  27.0 1.7 %collective-permute-done.1.got_ref = bf16[2624,128]{1,0:T(8,128)(2,1)S(1)} collective-permute-done((bf16[2624,128]{1,0:T(8,128)(2,1)S(1)}, bf16[2624,128]{1,0:T(8,128)(2,1)S(1)}, u32[]{:S(2)}, u32[]{:S(2)}) %collective-permute-start.1) | collective-permute-done | bytes 671776 | tf_op jit(solution)/shard_map/ppermute | solution.py:260
  28.7 2.9 %forward.1 = (bf16[1,2,16,8,128]{4,3,2,1,0:T(8,128)(2,1)}, bf16[512,128]{1,0:T(8,128)(2,1)S(1)}, bf16[12,144,128]{2,1,0:T(8,128)(2,1)S(1)}) custom-call(bf16[12,144,128]{2,1,0:T(8,128)(2,1)S(1)} %all-to-all-done.kernel_ref, bf16[2624,128]{1,0:T(8,128)(2,1)S(1)} %collective-permute-done.1.got_ref, bf16[1,2,16,8,128]{4,3,2,1,0:T(8,128)(2,1)S(1)} %copy-done.2, ...), custom_call_target="tpu_custom_call" | custom-call | tf_op jit(solution)/shard_map/forward/pallas_call | solution.py:295
  31.6 21.9 %all_to_all.25 = bf16[12,144,128]{2,1,0:T(8,128)(2,1)S(1)} all-to-all(bf16[12,144,128]{2,1,0:T(8,128)(2,1)S(1)} %get-tuple-element.17), channel_id=1, replica_groups=mesh['dp'=12,'spatial'=64] {'dp'}, dimensions={0} | all-to-all | bytes 884736 | tf_op jit(solution)/shard_map/all_to_all | solution.py:309
  53.5 0.1 convert_reduce_fusion
  53.6 15.3 %all_to_all.26 = f32[8,24,128]{2,1,0:T(8,128)S(1)} all-to-all(f32[8,24,128]{2,1,0:T(8,128)S(1)} %pad.4), channel_id=1, replica_groups={{0,8,16,24,32,40,48,56},{1,9,17,25,33,41,49,57},{2,10,18,26,34,42,50,58..., dimensions={0} | all-to-all | bytes 196608 | tf_op jit(solution)/shard_map/all_to_all | solution.py:256
  68.9 17.0 %all_to_all.27 = f32[4,24,128]{2,1,0:T(8,128)S(1)} all-to-all(f32[4,24,128]{2,1,0:T(8,128)S(1)} %broadcast_in_dim.4), channel_id=1, replica_groups={{0,2,4,6},{1,3,5,7},{8,10,12,14},{9,11,13,15},{16,18,20,22},{17,19,21,2..., dimensions={0} | all-to-all | bytes 98304 | tf_op jit(solution)/shard_map/all_to_all | solution.py:256
  86.0 0.7 broadcast_in_dim.5
  86.6 7.8 %all-to-all-start.4 = ((f32[16,24,128]{2,1,0:T(8,128)}), f32[16,24,128]{2,1,0:T(8,128)S(1)}, u32[]{:S(2)}, u32[]{:S(2)}) async-start(f32[16,24,128]{2,1,0:T(8,128)} %broadcast_in_dim.5), calls=%async_computation.4 | async-start | bytes 393216 | tf_op jit(solution)/shard_map/all_to_all | solution.py:256
  94.5 0.0 copy-start.4
  94.5 0.0 copy-start.5
  94.5 1.4 %backward.1 = bf16[1,2,16,8,128]{4,3,2,1,0:T(8,128)(2,1)} custom-call(bf16[12,144,128]{2,1,0:T(8,128)(2,1)S(1)} %all-to-all-done.kernel_ref, bf16[2624,128]{1,0:T(8,128)(2,1)S(1)} %collective-permute-done.1.got_ref, bf16[512,128]{1,0:T(8,128)(2,1)S(1)} %get-tuple-element.16.grad_ref), custom_call_target="tpu_custom_call" | custom-call | flops 226492416 | bytes 442368 | tf_op jit(solution)/shard_map/backward/pallas_call | solution.py:310
  95.9 8.8 %all-to-all-done.4.grads_ref = f32[16,24,128]{2,1,0:T(8,128)S(1)} async-done(((f32[16,24,128]{2,1,0:T(8,128)}), f32[16,24,128]{2,1,0:T(8,128)S(1)}, u32[]{:S(2)}, u32[]{:S(2)}) %all-to-all-start.4) | async-done | bytes 196640 | tf_op jit(solution)/shard_map/all_to_all | solution.py:256
  104.7 0.0 copy-done.1
  104.7 1.0 update.1
  (11 shorter events, 0.1 us)
Async XLA Ops:
  0.6 0.9 copy-start
  1.5 9.4 %copy-start.2 = (bf16[1,2,16,8,128]{4,3,2,1,0:T(8,128)(2,1)S(1)}, bf16[1,2,16,8,128]{4,3,2,1,0:T(8,128)(2,1)}, u32[]{:S(2)}) copy-start(bf16[1,2,16,8,128]{4,3,2,1,0:T(8,128)(2,1)} %volume_ref.3) | copy-start | bytes 196612
  1.5 9.4 %copy-start.3 = (bf16[1,2,16,8,128]{4,3,2,1,0:T(8,128)(2,1)S(1)}, bf16[1,2,16,8,128]{4,3,2,1,0:T(8,128)(2,1)}, u32[]{:S(2)}) copy-start(bf16[1,2,16,8,128]{4,3,2,1,0:T(8,128)(2,1)} %cot_ref.3) | copy-start | bytes 196612
  2.4 20.9 %all-to-all-start = ((bf16[12,144,128]{2,1,0:T(8,128)(2,1)}), bf16[12,144,128]{2,1,0:T(8,128)(2,1)S(1)}, u32[]{:S(2)}, u32[]{:S(2)}) async-start(bf16[12,144,128]{2,1,0:T(8,128)(2,1)} %pack.1), calls=%async_computation | async-start | bytes 884736 | tf_op jit(solution)/shard_map/all_to_all | solution.py:285
  11.0 12.3 %collective-permute-start = (bf16[3,16,8,128]{3,2,1,0:T(8,128)(2,1)S(1)}, bf16[3,16,8,128]{3,2,1,0:T(8,128)(2,1)S(1)}, u32[]{:S(2)}, u32[]{:S(2)}) collective-permute-start(bf16[3,16,8,128]{3,2,1,0:T(8,128)(2,1)S(1)} %get-tuple-element.13), channel_id=1, source_target_pairs={{1,2},{2,1},{3,4},{4,3},{5,6},{6,5},{7,8},{8,7},{9,10},{10,9},{11,... | collective-permute-start | bytes 294920 | tf_op jit(solution)/shard_map/ppermute | solution.py:260
  23.3 5.4 %collective-permute-start.1 = (bf16[2624,128]{1,0:T(8,128)(2,1)S(1)}, bf16[2624,128]{1,0:T(8,128)(2,1)S(1)}, u32[]{:S(2)}, u32[]{:S(2)}) collective-permute-start(bf16[2624,128]{1,0:T(8,128)(2,1)S(1)} %pad_maximum_fusion), channel_id=1, source_target_pairs={{0,1},{1,0},{2,3},{3,2},{4,5},{5,4},{6,7},{7,6},{8,9},{9,8},{10,11... | collective-permute-start | bytes 2015240 | tf_op jit(solution)/shard_map/ppermute | solution.py:260
  86.6 18.1 %all-to-all-start.4 = ((f32[16,24,128]{2,1,0:T(8,128)}), f32[16,24,128]{2,1,0:T(8,128)S(1)}, u32[]{:S(2)}, u32[]{:S(2)}) async-start(f32[16,24,128]{2,1,0:T(8,128)} %broadcast_in_dim.5), calls=%async_computation.4 | async-start | bytes 393216 | tf_op jit(solution)/shard_map/all_to_all | solution.py:256
  94.5 10.3 %copy-start.1 = (f32[288,128]{1,0:T(8,128)S(1)}, f32[288,128]{1,0:T(8,128)}, u32[]{:S(2)}) copy-start(f32[288,128]{1,0:T(8,128)} %master_ref.3) | copy-start | bytes 442372
  94.5 10.3 %copy-start.4 = (f32[288,128]{1,0:T(8,128)S(1)}, f32[288,128]{1,0:T(8,128)}, u32[]{:S(2)}) copy-start(f32[288,128]{1,0:T(8,128)} %moment_ref.1) | copy-start | bytes 442372
  94.5 10.3 %copy-start.5 = (f32[288,128]{1,0:T(8,128)S(1)}, f32[288,128]{1,0:T(8,128)}, u32[]{:S(2)}) copy-start(f32[288,128]{1,0:T(8,128)} %second_ref.1) | copy-start | bytes 442372

commit v9 on v8

--- a/solution.py
+++ b/solution.py
@@ -29,16 +29,25 @@
     return jnp.where(low, when_low, when_high)
 
 
-def pack_body(master_ref, send_ref):
+def pack_body(master_ref, send_ref, rows_ref, packed_ref, in_sem, out_sems):
     low = core_is_low()
-    rows = master_ref.shape[0] // 2
-    top = master_ref[:rows]
-    bottom = master_ref[rows:]
+    fetch = pltpu.make_async_copy(master_ref, rows_ref, in_sem)
+    fetch.start()
+    fetch.wait()
+    rows = rows_ref.shape[0] // 2
+    top = rows_ref[:rows]
+    bottom = rows_ref[rows:]
     first = pick(low, top, pltpu.roll(top, HALF, 1))
     second = pick(low, pltpu.roll(bottom, HALF, 1), bottom)
-    packed = jnp.where(lane_of(top.shape) < HALF, first, second).astype(BF16)
-    for owner in range(send_ref.shape[0]):
-        send_ref[owner] = packed
+    packed_ref[...] = jnp.where(lane_of(top.shape) < HALF, first, second).astype(BF16)
+    copies = [
+        pltpu.make_async_copy(packed_ref, send_ref.at[owner], out_sems.at[owner])
+        for owner in range(send_ref.shape[0])
+    ]
+    for copy in copies:
+        copy.start()
+    for copy in copies:
+        copy.wait()
 
 
 def edges_body(volume_ref, cot_ref, near_ref, slab_ref):
@@ -279,6 +288,14 @@
     send = pl.pallas_call(
         pack_body,
         out_shape=packed,
+        in_specs=[pl.BlockSpec(memory_space=pltpu.HBM)],
+        out_specs=pl.BlockSpec(memory_space=pltpu.HBM),
+        scratch_shapes=[
+            pltpu.VMEM(master.shape, F32),
+            pltpu.VMEM(packed.shape[1:], BF16),
+            pltpu.SemaphoreType.DMA,
+            pltpu.SemaphoreType.DMA((owners,)),
+        ],
         name="pack",
         compiler_params=pltpu.CompilerParams(vmem_limit_bytes=8 << 20),
     )(master)

time: 106 us -> 106 us (level)
  no operation moved by 1% of the time
where the time goes in v9:
time: 106 us
  blocking collectives  54.2 us (51%)
  starting transfers between devices  29.6 us (28%)
  waiting for transfers between devices  13.2 us (12%)
  Pallas kernels  6.46 us (6%)
  local copies, waits for them, and re-layouts  1.63 us (2%)
    all_to_all x2, blocking collectives, exchanged(): lax.all_to_all(tiles, 'spatial', 0, 0, tiled=True, axis_index_groups=groups)  32.4 us
    all_to_all x1, blocking collectives, layer(): arrived = lax.all_to_all(weight, 'dp', 0, 0, tiled=True)  21.9 us
    ppermute x2, starting transfers between devices, moved(): return lax.ppermute(value, 'spatial', perm)  13.3 us
    all_to_all x1, waiting for transfers between devices, exchanged(): lax.all_to_all(tiles, 'spatial', 0, 0, tiled=True, axis_index_groups=groups)  8.8 us
    all_to_all x1, starting transfers between devices, layer(): halves = lax.all_to_all(send, 'dp', 0, 0, tiled=True)  8.5 us
    all_to_all x1, starting transfers between devices, exchanged(): lax.all_to_all(tiles, 'spatial', 0, 0, tiled=True, axis_index_groups=groups)  7.81 us
    ppermute x2, waiting for transfers between devices, moved(): return lax.ppermute(value, 'spatial', perm)  4.35 us
    pallas_call x1, Pallas kernels, layer(): pl.pallas_call(forward_body, out_shape=(like(volume.shape, BF16), like((4...  2.89 us
  transfers between devices with their start and end apart: 4, of which 3 were waited for; matrix products, arithmetic and copies ran while one was open for 0% of the time, Pallas kernels for 1%

profile of v9, /device:TPU:1, one launch (start us, length us, event | category | flops | bytes accessed | tf_op | source)
XLA Modules:
  0.0 106.0 jit_solution(5368726659035063703)
XLA Ops:
  0.6 0.0 copy-start
  0.6 0.9 copy-done
  1.5 1.1 %pack.1 = bf16[12,144,128]{2,1,0:T(8,128)(2,1)} custom-call(f32[288,128]{1,0:T(8,128)S(1)} %copy-done), custom_call_target="tpu_custom_call" | custom-call | tf_op jit(solution)/shard_map/pack/pallas_call | solution.py:288
  2.7 8.5 %all-to-all-start = ((bf16[12,144,128]{2,1,0:T(8,128)(2,1)}), bf16[12,144,128]{2,1,0:T(8,128)(2,1)S(1)}, u32[]{:S(2)}, u32[]{:S(2)}) async-start(bf16[12,144,128]{2,1,0:T(8,128)(2,1)} %pack.1), calls=%async_computation | async-start | bytes 884736 | tf_op jit(solution)/shard_map/all_to_all | solution.py:302
  11.2 0.0 copy-done.2
  11.2 0.0 copy-done.3
  11.3 9.7 %collective-permute-start = (bf16[3,16,8,128]{3,2,1,0:T(8,128)(2,1)S(1)}, bf16[3,16,8,128]{3,2,1,0:T(8,128)(2,1)S(1)}, u32[]{:S(2)}, u32[]{:S(2)}) collective-permute-start(bf16[3,16,8,128]{3,2,1,0:T(8,128)(2,1)S(1)} %get-tuple-element.13), channel_id=1, source_target_pairs={{1,2},{2,1},{3,4},{4,3},{5,6},{6,5},{7,8},{8,7},{9,10},{10,9},{11,... | collective-permute-start | bytes 294920 | tf_op jit(solution)/shard_map/ppermute | solution.py:269
  20.9 2.6 %collective-permute-done.near_ref = bf16[3,16,8,128]{3,2,1,0:T(8,128)(2,1)S(1)} collective-permute-done((bf16[3,16,8,128]{3,2,1,0:T(8,128)(2,1)S(1)}, bf16[3,16,8,128]{3,2,1,0:T(8,128)(2,1)S(1)}, u32[]{:S(2)}, u32[]{:S(2)}) %collective-permute-start) | collective-permute-done | bytes 98336 | tf_op jit(solution)/shard_map/ppermute | solution.py:269
  23.6 0.0 all-to-all-done.kernel_ref
  23.6 3.7 %collective-permute-start.1 = (bf16[2624,128]{1,0:T(8,128)(2,1)S(1)}, bf16[2624,128]{1,0:T(8,128)(2,1)S(1)}, u32[]{:S(2)}, u32[]{:S(2)}) collective-permute-start(bf16[2624,128]{1,0:T(8,128)(2,1)S(1)} %pad_maximum_fusion), channel_id=1, source_target_pairs={{0,1},{1,0},{2,3},{3,2},{4,5},{5,4},{6,7},{7,6},{8,9},{9,8},{10,11... | collective-permute-start | bytes 2015240 | tf_op jit(solution)/shard_map/ppermute | solution.py:269
  27.3 1.7 %collective-permute-done.1.got_ref = bf16[2624,128]{1,0:T(8,128)(2,1)S(1)} collective-permute-done((bf16[2624,128]{1,0:T(8,128)(2,1)S(1)}, bf16[2624,128]{1,0:T(8,128)(2,1)S(1)}, u32[]{:S(2)}, u32[]{:S(2)}) %collective-permute-start.1) | collective-permute-done | bytes 671776 | tf_op jit(solution)/shard_map/ppermute | solution.py:269
  29.0 2.9 %forward.1 = (bf16[1,2,16,8,128]{4,3,2,1,0:T(8,128)(2,1)}, bf16[512,128]{1,0:T(8,128)(2,1)S(1)}, bf16[12,144,128]{2,1,0:T(8,128)(2,1)S(1)}) custom-call(bf16[12,144,128]{2,1,0:T(8,128)(2,1)S(1)} %all-to-all-done.kernel_ref, bf16[2624,128]{1,0:T(8,128)(2,1)S(1)} %collective-permute-done.1.got_ref, bf16[1,2,16,8,128]{4,3,2,1,0:T(8,128)(2,1)S(1)} %copy-done.2, ...), custom_call_target="tpu_custom_call" | custom-call | tf_op jit(solution)/shard_map/forward/pallas_call | solution.py:312
  31.9 21.9 %all_to_all.25 = bf16[12,144,128]{2,1,0:T(8,128)(2,1)S(1)} all-to-all(bf16[12,144,128]{2,1,0:T(8,128)(2,1)S(1)} %get-tuple-element.17), channel_id=1, replica_groups=mesh['dp'=12,'spatial'=64] {'dp'}, dimensions={0} | all-to-all | bytes 884736 | tf_op jit(solution)/shard_map/all_to_all | solution.py:326
  53.8 0.1 convert_reduce_fusion
  53.9 15.3 %all_to_all.26 = f32[8,24,128]{2,1,0:T(8,128)S(1)} all-to-all(f32[8,24,128]{2,1,0:T(8,128)S(1)} %pad.4), channel_id=1, replica_groups={{0,8,16,24,32,40,48,56},{1,9,17,25,33,41,49,57},{2,10,18,26,34,42,50,58..., dimensions={0} | all-to-all | bytes 196608 | tf_op jit(solution)/shard_map/all_to_all | solution.py:265
  69.2 17.0 %all_to_all.27 = f32[4,24,128]{2,1,0:T(8,128)S(1)} all-to-all(f32[4,24,128]{2,1,0:T(8,128)S(1)} %broadcast_in_dim.4), channel_id=1, replica_groups={{0,2,4,6},{1,3,5,7},{8,10,12,14},{9,11,13,15},{16,18,20,22},{17,19,21,2..., dimensions={0} | all-to-all | bytes 98304 | tf_op jit(solution)/shard_map/all_to_all | solution.py:265
  86.3 0.7 broadcast_in_dim.5
  86.9 7.8 %all-to-all-start.4 = ((f32[16,24,128]{2,1,0:T(8,128)}), f32[16,24,128]{2,1,0:T(8,128)S(1)}, u32[]{:S(2)}, u32[]{:S(2)}) async-start(f32[16,24,128]{2,1,0:T(8,128)} %broadcast_in_dim.5), calls=%async_computation.4 | async-start | bytes 393216 | tf_op jit(solution)/shard_map/all_to_all | solution.py:265
  94.8 0.0 copy-start.4
  94.8 0.0 copy-start.5
  94.8 1.4 %backward.1 = bf16[1,2,16,8,128]{4,3,2,1,0:T(8,128)(2,1)} custom-call(bf16[12,144,128]{2,1,0:T(8,128)(2,1)S(1)} %all-to-all-done.kernel_ref, bf16[2624,128]{1,0:T(8,128)(2,1)S(1)} %collective-permute-done.1.got_ref, bf16[512,128]{1,0:T(8,128)(2,1)S(1)} %get-tuple-element.16.grad_ref), custom_call_target="tpu_custom_call" | custom-call | flops 226492416 | bytes 442368 | tf_op jit(solution)/shard_map/backward/pallas_call | solution.py:327
  96.2 8.8 %all-to-all-done.4.grads_ref = f32[16,24,128]{2,1,0:T(8,128)S(1)} async-done(((f32[16,24,128]{2,1,0:T(8,128)}), f32[16,24,128]{2,1,0:T(8,128)S(1)}, u32[]{:S(2)}, u32[]{:S(2)}) %all-to-all-start.4) | async-done | bytes 196640 | tf_op jit(solution)/shard_map/all_to_all | solution.py:265
  105.0 0.0 copy-done.4
  105.0 1.0 update.1
  (11 shorter events, 0.1 us)
Async XLA Ops:
  0.6 0.9 copy-start
  1.5 9.7 %copy-start.2 = (bf16[1,2,16,8,128]{4,3,2,1,0:T(8,128)(2,1)S(1)}, bf16[1,2,16,8,128]{4,3,2,1,0:T(8,128)(2,1)}, u32[]{:S(2)}) copy-start(bf16[1,2,16,8,128]{4,3,2,1,0:T(8,128)(2,1)} %volume_ref.3) | copy-start | bytes 196612
  1.5 9.7 %copy-start.3 = (bf16[1,2,16,8,128]{4,3,2,1,0:T(8,128)(2,1)S(1)}, bf16[1,2,16,8,128]{4,3,2,1,0:T(8,128)(2,1)}, u32[]{:S(2)}) copy-start(bf16[1,2,16,8,128]{4,3,2,1,0:T(8,128)(2,1)} %cot_ref.3) | copy-start | bytes 196612
  2.7 20.9 %all-to-all-start = ((bf16[12,144,128]{2,1,0:T(8,128)(2,1)}), bf16[12,144,128]{2,1,0:T(8,128)(2,1)S(1)}, u32[]{:S(2)}, u32[]{:S(2)}) async-start(bf16[12,144,128]{2,1,0:T(8,128)(2,1)} %pack.1), calls=%async_computation | async-start | bytes 884736 | tf_op jit(solution)/shard_map/all_to_all | solution.py:302
  11.3 12.3 %collective-permute-start = (bf16[3,16,8,128]{3,2,1,0:T(8,128)(2,1)S(1)}, bf16[3,16,8,128]{3,2,1,0:T(8,128)(2,1)S(1)}, u32[]{:S(2)}, u32[]{:S(2)}) collective-permute-start(bf16[3,16,8,128]{3,2,1,0:T(8,128)(2,1)S(1)} %get-tuple-element.13), channel_id=1, source_target_pairs={{1,2},{2,1},{3,4},{4,3},{5,6},{6,5},{7,8},{8,7},{9,10},{10,9},{11,... | collective-permute-start | bytes 294920 | tf_op jit(solution)/shard_map/ppermute | solution.py:269
  23.6 5.4 %collective-permute-start.1 = (bf16[2624,128]{1,0:T(8,128)(2,1)S(1)}, bf16[2624,128]{1,0:T(8,128)(2,1)S(1)}, u32[]{:S(2)}, u32[]{:S(2)}) collective-permute-start(bf16[2624,128]{1,0:T(8,128)(2,1)S(1)} %pad_maximum_fusion), channel_id=1, source_target_pairs={{0,1},{1,0},{2,3},{3,2},{4,5},{5,4},{6,7},{7,6},{8,9},{9,8},{10,11... | collective-permute-start | bytes 2015240 | tf_op jit(solution)/shard_map/ppermute | solution.py:269
  86.9 18.1 %all-to-all-start.4 = ((f32[16,24,128]{2,1,0:T(8,128)}), f32[16,24,128]{2,1,0:T(8,128)S(1)}, u32[]{:S(2)}, u32[]{:S(2)}) async-start(f32[16,24,128]{2,1,0:T(8,128)} %broadcast_in_dim.5), calls=%async_computation.4 | async-start | bytes 393216 | tf_op jit(solution)/shard_map/all_to_all | solution.py:265
  94.8 10.3 %copy-start.1 = (f32[288,128]{1,0:T(8,128)S(1)}, f32[288,128]{1,0:T(8,128)}, u32[]{:S(2)}) copy-start(f32[288,128]{1,0:T(8,128)} %master_ref.3) | copy-start | bytes 442372
  94.8 10.3 %copy-start.4 = (f32[288,128]{1,0:T(8,128)S(1)}, f32[288,128]{1,0:T(8,128)}, u32[]{:S(2)}) copy-start(f32[288,128]{1,0:T(8,128)} %moment_ref.1) | copy-start | bytes 442372
  94.8 10.3 %copy-start.5 = (f32[288,128]{1,0:T(8,128)S(1)}, f32[288,128]{1,0:T(8,128)}, u32[]{:S(2)}) copy-start(f32[288,128]{1,0:T(8,128)} %second_ref.1) | copy-start | bytes 442372
